TPU v7x, 32 devices: a 4x4x1 block of a 4x4x8 slice. The times are simulated.
32 devices in a mesh: dp: 1 (over z), tp: 4 (over y), sp: 8 (over x, core).
Axes of the slice: x: 4, y: 4, z: 1, core: 2. Of those that a mesh axis runs over, the one named last changes fastest.
The devices are a block of a 4x4x8 slice.
Arguments:
- encoded: bfloat16 [64, 256, 1536], P('dp', 'sp')
- enc_gain: float32 [1536], replicated
- enc_bias: float32 [1536], replicated
- probe: float32 [1536], replicated
- w_query: bfloat16 [1536, 16, 96], P(None, 'tp')
- b_query: float32 [16, 96], P('tp')
- w_key: bfloat16 [1536, 16, 96], P(None, 'tp')
- w_value: bfloat16 [1536, 16, 96], P(None, 'tp')
- b_value: float32 [16, 96], P('tp')
- w_out: bfloat16 [16, 96, 1536], P('tp')
- b_out: float32 [1536], replicated
- head_gain: float32 [1536], replicated
- head_bias: float32 [1536], replicated
- w_up: bfloat16 [1536, 6144], P(None, 'tp')
- b_up: float32 [6144], P('tp')
- w_down: bfloat16 [6144, 1536], P('tp')
- b_down: float32 [1536], replicated
- out_grad: bfloat16 [64, 1536], P('dp')
Outputs:
- output 1: bfloat16 [64, 1536], P('dp')
- output 2: bfloat16 [64, 256, 1536], P('dp', 'sp')
- output 3: float32 [1536], P('dp')
- output 4: float32 [1536, 16, 96], P('dp', 'tp')
- output 5: float32 [1536, 16, 96], P('dp', 'tp')
- output 6: float32 [1536, 16, 96], P('dp', 'tp')
- output 7: float32 [16, 96, 1536], P(('dp', 'tp'))
- output 8: float32 [1536, 6144], P('dp', 'tp')
- output 9: float32 [6144, 1536], P(('dp', 'tp'))
All inputs are finite; a program needn't handle non-finite values.
Results may differ from a plain program's by a relative error of at most 0.0186865.
Values sent between devices are 32-bit elements.
A program may use at most 768 MiB of HBM per device.

v0:
```python
import functools
import jax
import jax.numpy as jnp
from jax import lax
from jax.sharding import PartitionSpec as P

NORM_EPS = 1e-6
IN_SPECS = (P('dp', 'sp', None), P(), P(), P(), P(None, 'tp', None), P('tp', None), P(None, 'tp', None), P(None, 'tp', None), P('tp', None), P('tp', None, None), P(), P(), P(), P(None, 'tp'), P('tp'), P('tp', None), P(), P('dp', None))
OUT_SPECS = (P('dp', None), P('dp', 'sp', None), P('dp'), P('dp', 'tp', None), P('dp', 'tp', None), P('dp', 'tp', None), P(('dp', 'tp'), None, None), P('dp', 'tp'), P(('dp', 'tp'), None))


def layer_norm(rows_in, norm_gain, norm_bias):
    row_mean = jnp.mean(rows_in, axis=-1, keepdims=True)
    centred = rows_in - row_mean
    inv_std = lax.rsqrt(jnp.mean(centred * centred, axis=-1, keepdims=True) + NORM_EPS)
    return centred * inv_std * norm_gain + norm_bias


def norm_vjp(rows_in, norm_gain, norm_bias, cotangent):
    pull_back = jax.vjp(functools.partial(layer_norm, norm_gain=norm_gain, norm_bias=norm_bias), rows_in)[1]
    return pull_back(cotangent)[0]


def gelu_vjp(pre_act, cotangent):
    pull_back = jax.vjp(functools.partial(jax.nn.gelu, approximate=True), pre_act)[1]
    return pull_back(cotangent)[0]


def local_head(encoded, enc_gain, enc_bias, probe, w_query, b_query, w_key, w_value, b_value, w_out, b_out, head_gain, head_bias, w_up, b_up, w_down, b_down, out_grad):
    head_dim = b_query.shape[1]
    score_scale = head_dim ** -0.5
    enc_f32 = encoded.astype(jnp.float32)
    normed = layer_norm(enc_f32, enc_gain, enc_bias).astype(jnp.bfloat16)
    query_heads = (jnp.einsum('w,whd->hd', probe.astype(jnp.bfloat16), w_query, preferred_element_type=jnp.float32) + b_query).astype(jnp.bfloat16)
    key_heads = jnp.einsum('bnw,whd->bnhd', normed, w_key, preferred_element_type=jnp.float32).astype(jnp.bfloat16)
    value_heads = (jnp.einsum('bnw,whd->bnhd', normed, w_value, preferred_element_type=jnp.float32) + b_value).astype(jnp.bfloat16)
    scores = jnp.einsum('bnhd,hd->bhn', key_heads, query_heads, preferred_element_type=jnp.float32) * score_scale
    score_max = lax.pmax(jnp.max(scores, axis=-1, keepdims=True), 'sp')
    exp_scores = jnp.exp(scores - score_max)
    exp_total = lax.psum(jnp.sum(exp_scores, axis=-1, keepdims=True), 'sp')
    value_sum = lax.psum(jnp.einsum('bhn,bnhd->bhd', exp_scores.astype(jnp.bfloat16), value_heads, preferred_element_type=jnp.float32), 'sp')
    pooled_bf = (value_sum / exp_total).astype(jnp.bfloat16)
    attn_out = lax.psum(jnp.einsum('bhd,hdw->bw', pooled_bf, w_out, preferred_element_type=jnp.float32), 'tp') + b_out
    normed_out = layer_norm(attn_out, head_gain, head_bias).astype(jnp.bfloat16)
    pre_act = jnp.dot(normed_out, w_up, preferred_element_type=jnp.float32) + b_up
    hidden = jax.nn.gelu(pre_act, approximate=True).astype(jnp.bfloat16)
    pooled = (attn_out + lax.psum(jnp.dot(hidden, w_down, preferred_element_type=jnp.float32), 'tp') + b_down).astype(jnp.bfloat16)

    grad_w_down = jnp.einsum('bf,bw->fw', hidden, out_grad, preferred_element_type=jnp.float32)
    grad_hidden = jnp.einsum('bw,fw->bf', out_grad, w_down, preferred_element_type=jnp.float32)
    grad_pre = gelu_vjp(pre_act, grad_hidden).astype(jnp.bfloat16)
    grad_w_up = jnp.einsum('bw,bf->wf', normed_out, grad_pre, preferred_element_type=jnp.float32)
    grad_normed_out = lax.psum(jnp.einsum('bf,wf->bw', grad_pre, w_up, preferred_element_type=jnp.float32), 'tp')
    grad_attn = (out_grad.astype(jnp.float32) + norm_vjp(attn_out, head_gain, head_bias, grad_normed_out)).astype(jnp.bfloat16)
    grad_w_out = jnp.einsum('bhd,bw->hdw', pooled_bf, grad_attn, preferred_element_type=jnp.float32)
    grad_pooled = jnp.einsum('bw,hdw->bhd', grad_attn, w_out, preferred_element_type=jnp.float32).astype(jnp.bfloat16)
    weights = exp_scores / exp_total
    grad_weights = jnp.einsum('bhd,bnhd->bhn', grad_pooled, value_heads, preferred_element_type=jnp.float32)
    mean_term = lax.psum(jnp.sum(weights * grad_weights, axis=-1, keepdims=True), 'sp')
    grad_scores = (weights * (grad_weights - mean_term) * score_scale).astype(jnp.bfloat16)
    grad_query = lax.psum(jnp.einsum('bhn,bnhd->hd', grad_scores, key_heads, preferred_element_type=jnp.float32), 'sp')
    grad_keys = jnp.einsum('bhn,hd->bnhd', grad_scores, query_heads, preferred_element_type=jnp.float32).astype(jnp.bfloat16)
    grad_values = jnp.einsum('bhn,bhd->bnhd', weights.astype(jnp.bfloat16), grad_pooled, preferred_element_type=jnp.float32).astype(jnp.bfloat16)
    grad_w_key = lax.psum(jnp.einsum('bnw,bnhd->whd', normed, grad_keys, preferred_element_type=jnp.float32), 'sp')
    grad_w_value = lax.psum(jnp.einsum('bnw,bnhd->whd', normed, grad_values, preferred_element_type=jnp.float32), 'sp')
    grad_normed = lax.psum(jnp.einsum('bnhd,whd->bnw', grad_keys, w_key, preferred_element_type=jnp.float32) + jnp.einsum('bnhd,whd->bnw', grad_values, w_value, preferred_element_type=jnp.float32), 'tp')
    grad_encoded = norm_vjp(enc_f32, enc_gain, enc_bias, grad_normed).astype(jnp.bfloat16)
    grad_w_query = probe[:, None, None] * grad_query[None, :, :]
    grad_probe = lax.psum(jnp.einsum('whd,hd->w', w_query, grad_query.astype(jnp.bfloat16), preferred_element_type=jnp.float32), 'tp')
    return (pooled, grad_encoded, grad_probe, grad_w_query, grad_w_key, grad_w_value, grad_w_out, grad_w_up, grad_w_down)


def solution(mesh):
    return jax.shard_map(local_head, mesh=mesh, in_specs=IN_SPECS, out_specs=OUT_SPECS, check_vma=False)
```

profile of v0, /device:TPU:97, one launch (start us, length us, event | category | flops | bytes accessed | tf_op | source)
XLA Modules:
  0.0 538.9 jit_solution(1896983281859256634)
XLA Ops:
  7.3 3.9 convert_reduce_fusion
  11.3 0.8 copy-done.2
  12.0 1.8 fusion.4
  13.9 0.5 fusion.79
  14.4 0.6 fusion.75
  15.0 3.9 fusion.33
  18.9 1.3 copy-done.10
  20.2 2.8 fusion.38
  23.0 0.1 copy.35
  23.1 13.8 %pmax.7 = f32[64,4]{0,1:T(4,128)S(1)} all-reduce(f32[64,4]{0,1:T(4,128)S(1)} %bitcast_reduce_fusion), channel_id=1, replica_groups=mesh['dp'=1,'tp'=4,'sp'=8] {'sp'}, use_global_device_ids=true, to_apply=%region_3.0 | all-reduce | flops 256 | bytes 2048 | tf_op jit(solution)/shard_map/pmax | solution.py:38
  37.0 0.1 copy.36
  37.1 0.4 copy-done.35
  37.5 6.1 %add_convert_fusion.1 = bf16[64,32,4,96]{3,1,2,0:T(8,128)(2,1)S(1)} fusion(f32[4,96]{1,0:T(4,128)S(1)} %copy-done.47, bf16[1536,4,96]{0,2,1:T(8,128)(2,1)} %param.25, bf16[64,32,1536]{2,1,0:T(8,128)(2,1)} %param.18, f32[1536]{0:T(1024)S(1)} %copy-done.45, f32[1536]{0:T(1024)S(1)} %copy-done.31, f32[64,32]{1,0:T(8,128)S(1)} %fusion.63, ...), kind=kOutput, calls=%fused_computation.25 | convolution fusion | flops 2436366336 | bytes 9074176 | tf_op jit(solution)/shard_map/bnw,whd->bnhd/dot_general | solution.py:36
  43.7 0.7 fusion.80
  44.3 0.7 copy.72
  45.1 0.1 all-reduce.10.cloned.1.call-start
  45.2 14.6 %psum.78 = f32[64,4]{0,1:T(4,128)S(1)} all-reduce(f32[64,4]{0,1:T(4,128)S(1)} %get-tuple-element.20), channel_id=1, replica_groups=mesh['dp'=1,'tp'=4,'sp'=8] {'sp'}, use_global_device_ids=true, to_apply=%region_6.0 | all-reduce | flops 256 | bytes 2048 | tf_op jit(solution)/shard_map/psum | solution.py:40
  59.7 40.5 %all-reduce.8.cloned.1.call-done = f32[64,4,96]{2,0,1:T(8,128)} async-done(((f32[64,4,96]{2,0,1:T(8,128)}), f32[64,4,96]{2,0,1:T(8,128)}) %all-reduce.8.cloned.1.call-update) | async-done | bytes 98320 | tf_op jit(solution)/shard_map/psum | solution.py:41
  100.2 2.1 convolution_bitcast_fusion
  102.4 0.2 all-reduce.12.cloned.1.call-start
  102.6 3.9 fusion.81
  106.5 32.9 %all-reduce.10.cloned.1.call-done = f32[64,1536]{1,0:T(8,128)} async-done(((f32[64,1536]{1,0:T(8,128)}), f32[64,1536]{1,0:T(8,128)}) %all-reduce.10.cloned.1.call-update) | async-done | bytes 393232 | tf_op jit(solution)/shard_map/psum | solution.py:43
  139.4 1.1 add_reduce_fusion
  140.6 1.2 multiply_reduce_fusion.1
  141.8 0.5 copy-done.44
  142.3 3.6 fusion.50
  146.0 4.7 fusion.82
  150.8 4.0 fusion.69
  154.8 33.7 %all-reduce.12.cloned.1.call-done = f32[64,1536]{1,0:T(8,128)} async-done(((f32[64,1536]{1,0:T(8,128)}), f32[64,1536]{1,0:T(8,128)}) %all-reduce.12.cloned.1.call-update) | async-done | bytes 393232 | tf_op jit(solution)/shard_map/psum | solution.py:53
  188.5 1.2 multiply_reduce_fusion
  189.7 0.7 multiply_multiply_fusion.3
  190.4 1.3 fusion.77
  191.6 0.1 fusion.51
  191.8 1.2 fusion.78
  193.0 2.8 fusion.52
  195.8 0.1 copy.39
  195.9 0.9 fusion.54
  196.8 14.6 %psum.82 = f32[64,4]{0,1:T(4,128)S(1)} all-reduce(f32[64,4]{0,1:T(4,128)S(1)} %fusion.54), channel_id=1, replica_groups=mesh['dp'=1,'tp'=4,'sp'=8] {'sp'}, use_global_device_ids=true, to_apply=%region_15.0 | all-reduce | flops 256 | bytes 2048 | tf_op jit(solution)/shard_map/psum | solution.py:59
  211.4 1.5 convert_bitcast_fusion
  212.9 2.0 fusion.24
  215.0 4.7 fusion.29
  219.6 1.3 fusion.25
  220.9 1.3 copy-done.5
  222.2 6.9 %bitcast_add_fusion = f32[64,32,1536]{2,1,0:T(8,128)} fusion(f32[64,32,1536,1]{2,1,3,0:T(8,128)S(1)} %fusion.29, bf16[64,32,4,96]{3,0,1,2:T(8,128)(2,1)S(1)} %fusion.25, bf16[1536,4,96]{0,2,1:T(8,128)(2,1)S(1)} %copy-done.17), kind=kOutput, calls=%fused_computation.12 | convolution fusion | flops 2419064832 | bytes 27918336 | tf_op jit(solution)/shard_map/bnhd,whd->bnw/dot_general | solution.py:66
  229.3 0.3 all-reduce.14.cloned.1.call-start
  229.5 5.2 fusion.68
  234.8 5.2 fusion.70
  240.0 0.1 copy.42
  240.2 2.1 fusion.36
  242.3 12.9 %psum.84 = f32[4,96]{1,0:T(4,128)S(1)} all-reduce(f32[4,96]{1,0:T(4,128)S(1)} %bitcast.149), channel_id=1, replica_groups=mesh['dp'=1,'tp'=4,'sp'=8] {'sp'}, use_global_device_ids=true, to_apply=%region_19.0 | all-reduce | flops 384 | bytes 3072 | tf_op jit(solution)/shard_map/psum | solution.py:61
  255.2 0.3 convolution_reduce_fusion
  255.5 9.4 %psum.85 = f32[1536]{0:T(1024)} all-reduce(f32[1536]{0:T(1024)S(1)} %convolution_reduce_fusion), channel_id=1, replica_groups=mesh['dp'=1,'tp'=4,'sp'=8] {'tp'}, use_global_device_ids=true, to_apply=%region_20.0 | all-reduce | flops 1536 | bytes 12288 | tf_op jit(solution)/shard_map/psum | solution.py:69
  264.9 1.6 broadcast_multiply_fusion
  266.5 9.1 %fusion.21 = f32[1536,4,96]{0,2,1:T(8,128)} fusion(bf16[64,32,4,96]{3,0,1,2:T(8,128)(2,1)} %copy-done.5, bf16[64,32,1536]{2,1,0:T(8,128)(2,1)} %param.18, f32[1536]{0:T(1024)S(1)} %copy-done.46, f32[1536]{0:T(1024)S(1)} %copy-done.32, f32[64,32]{1,0:T(8,128)S(1)} %copy-done.25, f32[64,32]{1,0:T(8,128)S(1)} %copy-done.19), kind=kOutput, calls=%fused_computation.27 | convolution fusion | flops 2434793472 | bytes 10252288 | tf_op jit(solution)/shard_map/bnw,bnhd->whd/dot_general | solution.py:65
  275.6 5.6 %fusion.18 = f32[1536,4,96]{0,2,1:T(8,128)} fusion(bf16[64,32,4,96]{3,0,1,2:T(8,128)(2,1)S(1)} %copy-done.12, bf16[64,32,1536]{2,1,0:T(8,128)(2,1)S(1)} %bitcast.141, f32[1536]{0:T(1024)S(1)} %copy-done.46, f32[1536]{0:T(1024)S(1)} %copy-done.32, f32[64,32]{1,0:T(8,128)S(1)} %copy-done.25, f32[64,32]{1,0:T(8,128)S(1)} %copy-done.19), kind=kOutput, calls=%fused_computation.26 | convolution fusion | flops 2434793472 | bytes 10252288 | tf_op jit(solution)/shard_map/bnw,bnhd->whd/dot_general | solution.py:64
  281.3 2.0 fusion.67
  283.3 173.3 %all-reduce.16.cloned.1.call-done = (f32[64,1536]{1,0:T(8,128)}, f32[64,32,1536]{2,1,0:T(8,128)}) async-done(((f32[64,1536]{1,0:T(8,128)}, f32[64,32,1536]{2,1,0:T(8,128)}), (f32[64,1536]{1,0:T(8,128)}, f32[64,32,1536]{2,1,0:T(8,128)})) %all-reduce.16.cloned.1.call-update) | async-done | bytes 12976144 | tf_op jit(solution)/shard_map/psum | solution.py:47
  456.7 8.9 %fusion.8 = f32[64,32]{1,0:T(8,128)S(1)} fusion(bf16[64,32,1536]{2,1,0:T(8,128)(2,1)} %param.18, f32[64,32,1536]{2,1,0:T(8,128)} %get-tuple-element.12, f32[1536]{0:T(1024)S(1)} %copy-done.32, f32[64,32]{1,0:T(8,128)S(1)} %copy-done.19), kind=kLoop, calls=%fused_computation.11 | loop fusion | flops 15726592 | bytes 18896896 | tf_op jit(solution)/shard_map/transpose(jvp())/reduce_sum | solution.py:16
  465.6 8.9 %fusion.17 = f32[64,32]{1,0:T(8,128)S(1)} fusion(f32[64,32]{1,0:T(8,128)S(1)} %multiply_multiply_fusion.2, f32[64,32]{1,0:T(8,128)S(1)} %copy-done.19, bf16[64,32,1536]{2,1,0:T(8,128)(2,1)} %param.18, f32[64,32]{1,0:T(8,128)S(1)} %copy-done.25, f32[64,32,1536]{2,1,0:T(8,128)} %get-tuple-element.12, f32[1536]{0:T(1024)S(1)} %copy-done.32), kind=kLoop, calls=%fused_computation.22 | loop fusion | flops 25163776 | bytes 18913280 | tf_op jit(solution)/shard_map/transpose(jvp())/reduce_sum | solution.py:14
  474.5 0.7 add_convert_fusion.3
  475.2 9.3 %add_convert_fusion = bf16[64,32,1536]{2,1,0:T(8,128)(2,1)} fusion(f32[64,32]{1,0:T(8,128)S(1)} %negate_multiply_fusion, f32[64,32]{1,0:T(8,128)S(1)} %multiply_multiply_fusion.2, f32[64,32]{1,0:T(8,128)S(1)} %copy-done.19, bf16[64,32,1536]{2,1,0:T(8,128)(2,1)S(1)} %bitcast.143, f32[64,32]{1,0:T(8,128)S(1)} %copy-done.25, ...), kind=kLoop, calls=%fused_computation.13 | loop fusion | flops 28311552 | bytes 25204736 | tf_op jit(solution)/shard_map/convert_element_type | solution.py:67
  484.5 42.6 %all-reduce.14.cloned.1.call-done = (f32[1536,4,96]{0,2,1:T(8,128)}, f32[1536,4,96]{0,2,1:T(8,128)}) async-done(((f32[1536,4,96]{0,2,1:T(8,128)}, f32[1536,4,96]{0,2,1:T(8,128)}), (f32[1536,4,96]{0,2,1:T(8,128)}, f32[1536,4,96]{0,2,1:T(8,128)})) %all-reduce.14.cloned.1.call-update) | async-done | bytes 4718608 | tf_op jit(solution)/shard_map/psum | solution.py:64
  527.1 3.4 copy.80
  530.5 1.4 copy.81
  (122 shorter events, 0.8 us)
Async XLA Ops:
  7.2 7.8 %copy-start = (bf16[1536,4,96]{0,2,1:T(8,128)(2,1)S(1)}, bf16[1536,4,96]{0,2,1:T(8,128)(2,1)}, u32[]{:S(2)}) copy-start(bf16[1536,4,96]{0,2,1:T(8,128)(2,1)} %param.24) | copy-start | bytes 3538948
  7.2 6.7 %copy-start.36 = (f32[1536]{0:T(1024)S(1)}, f32[1536]{0:T(1024)}, u32[]{:S(2)}) copy-start(f32[1536]{0:T(1024)} %param.21) | copy-start | bytes 18436
  7.2 7.2 %copy-start.43 = (f32[4,96]{1,0:T(4,128)S(1)}, f32[4,96]{1,0:T(4,128)}, u32[]{:S(2)}) copy-start(f32[4,96]{1,0:T(4,128)} %param.23) | copy-start | bytes 4612
  7.2 7.7 %copy-start.31 = (f32[1536]{0:T(1024)S(1)}, f32[1536]{0:T(1024)}, u32[]{:S(2)}) copy-start(f32[1536]{0:T(1024)} %param.19) | copy-start | bytes 18436
  7.2 7.7 %copy-start.45 = (f32[1536]{0:T(1024)S(1)}, f32[1536]{0:T(1024)}, u32[]{:S(2)}) copy-start(f32[1536]{0:T(1024)} %param.20) | copy-start | bytes 18436
  7.3 93.0 %all-reduce.8.cloned.1.call-start = ((), (), s32[]{:S(2)}) async-start(), calls=%async_computation | async-start | bytes 262144 | tf_op jit(solution)/shard_map/psum | solution.py:41
  7.3 4.7 copy-start.2
  7.3 6.6 %copy-start.7 = (bf16[1536,4,96]{0,2,1:T(8,128)(2,1)S(1)}, bf16[1536,4,96]{0,2,1:T(8,128)(2,1)}, u32[]{:S(2)}) copy-start(bf16[1536,4,96]{0,2,1:T(8,128)(2,1)} %param.22) | copy-start | bytes 3538948
  12.0 25.1 %copy-start.18 = (f32[64,32]{1,0:T(8,128)}, f32[64,32]{1,0:T(8,128)S(1)}, u32[]{:S(2)}) copy-start(f32[64,32]{1,0:T(8,128)S(1)} %broadcast_multiply_fusion.1) | copy-start | bytes 24580
  13.8 5.0 copy-start.26
  13.9 23.3 %copy-start.24 = (f32[64,32]{1,0:T(8,128)}, f32[64,32]{1,0:T(8,128)S(1)}, u32[]{:S(2)}) copy-start(f32[64,32]{1,0:T(8,128)S(1)} %fusion.63) | copy-start | bytes 24580
  15.0 22.6 %copy-start.47 = (f32[4,96]{1,0:T(4,128)S(1)}, f32[4,96]{1,0:T(4,128)}, u32[]{:S(2)}) copy-start(f32[4,96]{1,0:T(4,128)} %param.26) | copy-start | bytes 4612
  18.9 1.3 copy-start.10
  23.1 20.6 %copy-start.16 = (f32[4,1,64,32]{2,3,0,1:T(8,128)}, f32[4,1,64,32]{2,3,0,1:T(8,128)S(1)}, u32[]{:S(2)}) copy-start(f32[4,1,64,32]{2,3,0,1:T(8,128)S(1)} %copy.35) | copy-start | bytes 98308
  37.0 0.6 copy-start.35
  37.5 62.7 %copy-start.6 = (bf16[4,96,1536]{2,1,0:T(8,128)(2,1)S(1)}, bf16[4,96,1536]{2,1,0:T(8,128)(2,1)}, u32[]{:S(2)}) copy-start(bf16[4,96,1536]{2,1,0:T(8,128)(2,1)} %param.27) | copy-start | bytes 3538948
  37.5 65.1 %copy-start.13 = (bf16[64,1536]{1,0:T(8,128)(2,1)S(1)}, bf16[64,1536]{1,0:T(8,128)(2,1)}, u32[]{:S(2)}) copy-start(bf16[64,1536]{1,0:T(8,128)(2,1)} %param.35) | copy-start | bytes 589828
  43.7 1.4 copy-start.48
  43.7 95.8 %copy-start.20 = (f32[1536]{0:T(1024)S(1)}, f32[1536]{0:T(1024)}, u32[]{:S(2)}) copy-start(f32[1536]{0:T(1024)} %param.28) | copy-start | bytes 18436
  43.7 98.6 %copy-start.28 = (f32[1536]{0:T(1024)S(1)}, f32[1536]{0:T(1024)}, u32[]{:S(2)}) copy-start(f32[1536]{0:T(1024)} %param.29) | copy-start | bytes 18436
  45.1 94.3 %all-reduce.10.cloned.1.call-start = ((), (), s32[]{:S(2)}) async-start(), calls=%async_computation.1 | async-start | bytes 786432 | tf_op jit(solution)/shard_map/psum | solution.py:43
  59.7 82.1 %copy-start.33 = (f32[64,4]{0,1:T(4,128)}, f32[64,4]{0,1:T(4,128)S(1)}, u32[]{:S(2)}) copy-start(f32[64,4]{0,1:T(4,128)S(1)} %psum.78) | copy-start | bytes 3076
  102.4 86.1 %all-reduce.12.cloned.1.call-start = ((), (), s32[]{:S(2)}) async-start(), calls=%async_computation.2 | async-start | bytes 786432 | tf_op jit(solution)/shard_map/psum | solution.py:53
  140.6 5.4 copy-start.38
  141.8 0.5 copy-start.44
  142.3 3.6 copy-start.41
  146.0 42.5 %copy-start.3 = (f32[64,1536]{1,0:T(8,128)S(1)}, f32[64,1536]{1,0:T(8,128)}, u32[]{:S(2)}) copy-start(f32[64,1536]{1,0:T(8,128)} %all-reduce.10.cloned.1.call-done) | copy-start | bytes 1179652
  150.7 306.0 %all-reduce.16.cloned.1.call-start = ((), (), s32[]{:S(2)}) async-start(), calls=%async_computation.4 | async-start | bytes 25952256 | tf_op jit(solution)/shard_map/psum | solution.py:47
  191.8 1.2 copy-start.14
  214.9 4.7 copy-start.11
  214.9 4.7 copy-start.21
  214.9 7.3 %copy-start.17 = (bf16[1536,4,96]{0,2,1:T(8,128)(2,1)S(1)}, bf16[1536,4,96]{0,2,1:T(8,128)(2,1)}, u32[]{:S(2)}) copy-start(bf16[1536,4,96]{0,2,1:T(8,128)(2,1)} %param.25) | copy-start | bytes 3538948
  220.9 1.3 copy-start.5
  229.2 5.5 %copy-start.30 = (f32[1536]{0:T(1024)S(1)}, f32[1536]{0:T(1024)}, u32[]{:S(2)}) copy-start(f32[1536]{0:T(1024)} %param.30) | copy-start | bytes 18436
  229.2 5.5 %copy-start.39 = (f32[64]{0:T(128)S(1)}, f32[64]{0:T(128)}, u32[]{:S(2)}) copy-start(f32[64]{0:T(128)} %copy-done.38) | copy-start | bytes 772
  229.3 5.5 %copy-start.42 = (f32[64]{0:T(128)S(1)}, f32[64]{0:T(128)}, u32[]{:S(2)}) copy-start(f32[64]{0:T(128)} %copy-done.41) | copy-start | bytes 772
  229.3 297.8 %all-reduce.14.cloned.1.call-start = ((), (), s32[]{:S(2)}) async-start(), calls=%async_computation.3 | async-start | bytes 9437184 | tf_op jit(solution)/shard_map/psum | solution.py:64
  234.7 5.3 copy-start.29
  234.7 20.5 %copy-start.8 = (bf16[1536,4,96]{0,2,1:T(8,128)(2,1)S(1)}, bf16[1536,4,96]{0,2,1:T(8,128)(2,1)}, u32[]{:S(2)}) copy-start(bf16[1536,4,96]{0,2,1:T(8,128)(2,1)} %param.22) | copy-start | bytes 3538948
  234.7 30.1 %copy-start.37 = (f32[1536]{0:T(1024)S(1)}, f32[1536]{0:T(1024)}, u32[]{:S(2)}) copy-start(f32[1536]{0:T(1024)} %param.21) | copy-start | bytes 18436
  240.0 26.5 %copy-start.19 = (f32[64,32]{1,0:T(8,128)S(1)}, f32[64,32]{1,0:T(8,128)}, u32[]{:S(2)}) copy-start(f32[64,32]{1,0:T(8,128)} %copy-done.18) | copy-start | bytes 24580
  240.0 26.5 %copy-start.25 = (f32[64,32]{1,0:T(8,128)S(1)}, f32[64,32]{1,0:T(8,128)}, u32[]{:S(2)}) copy-start(f32[64,32]{1,0:T(8,128)} %copy-done.24) | copy-start | bytes 24580
  240.0 26.5 %copy-start.32 = (f32[1536]{0:T(1024)S(1)}, f32[1536]{0:T(1024)}, u32[]{:S(2)}) copy-start(f32[1536]{0:T(1024)} %param.19) | copy-start | bytes 18436
  240.0 26.5 %copy-start.46 = (f32[1536]{0:T(1024)S(1)}, f32[1536]{0:T(1024)}, u32[]{:S(2)}) copy-start(f32[1536]{0:T(1024)} %param.20) | copy-start | bytes 18436
  255.2 20.4 %slice-start = ((s8[6291456]{0:T(1024)(128)(4,1)}), s8[2097152]{0:T(1024)(128)(4,1)S(1)}, s32[]{:S(2)}) async-start(s8[6291456]{0:T(1024)(128)(4,1)} %bitcast.140), calls=%async_computation.5 | async-start | bytes 4194304
  266.5 9.1 %slice-start.1 = ((s8[6291456]{0:T(1024)(128)(4,1)}), s8[4194304]{0:T(1024)(128)(4,1)S(1)}, s32[]{:S(2)}) async-start(s8[6291456]{0:T(1024)(128)(4,1)} %bitcast.140), calls=%async_computation.6 | async-start | bytes 8388608
  266.5 9.1 %copy-start.12 = (bf16[64,32,4,96]{3,0,1,2:T(8,128)(2,1)S(1)}, bf16[64,32,4,96]{3,0,1,2:T(8,128)(2,1)}, u32[]{:S(2)}) copy-start(bf16[64,32,4,96]{3,0,1,2:T(8,128)(2,1)} %copy-done.11) | copy-start | bytes 4718596
  275.6 5.7 %copy-start.15 = (bf16[64,1536,1]{1,0,2:T(8,128)(2,1)S(1)}, bf16[64,1536,1]{1,0,2:T(8,128)(2,1)}, u32[]{:S(2)}) copy-start(bf16[64,1536,1]{1,0,2:T(8,128)(2,1)} %copy-done.14) | copy-start | bytes 589828
  275.6 5.7 %copy-start.22 = (f32[64,4,96]{2,0,1:T(8,128)S(1)}, f32[64,4,96]{2,0,1:T(8,128)}, u32[]{:S(2)}) copy-start(f32[64,4,96]{2,0,1:T(8,128)} %all-reduce.8.cloned.1.call-done) | copy-start | bytes 294916
  275.6 5.7 %copy-start.34 = (f32[64,4]{0,1:T(4,128)S(1)}, f32[64,4]{0,1:T(4,128)}, u32[]{:S(2)}) copy-start(f32[64,4]{0,1:T(4,128)} %copy-done.33) | copy-start | bytes 3076
  456.7 8.9 %copy-start.27 = (f32[64,32]{1,0:T(8,128)S(1)}, f32[64,32]{1,0:T(8,128)}, u32[]{:S(2)}) copy-start(f32[64,32]{1,0:T(8,128)} %copy-done.26) | copy-start | bytes 24580
  456.7 18.6 %slice-start.2 = ((s8[6291456]{0:T(1024)(128)(4,1)}), s8[2097152]{0:T(1024)(128)(4,1)S(1)}, s32[]{:S(2)}) async-start(s8[6291456]{0:T(1024)(128)(4,1)} %bitcast.142), calls=%async_computation.7 | async-start | bytes 4194304
  465.6 8.9 %copy-start.4 = (f32[64,1536]{1,0:T(8,128)S(1)}, f32[64,1536]{1,0:T(8,128)}, u32[]{:S(2)}) copy-start(f32[64,1536]{1,0:T(8,128)} %all-reduce.10.cloned.1.call-done) | copy-start | bytes 1179652
  465.6 8.9 %copy-start.23 = (f32[64,1536]{1,0:T(8,128)S(1)}, f32[64,1536]{1,0:T(8,128)}, u32[]{:S(2)}) copy-start(f32[64,1536]{1,0:T(8,128)} %get-tuple-element.11) | copy-start | bytes 1179652
  465.6 8.9 %copy-start.40 = (f32[1536]{0:T(1024)S(1)}, f32[1536]{0:T(1024)}, u32[]{:S(2)}) copy-start(f32[1536]{0:T(1024)} %param.34) | copy-start | bytes 18436
  465.6 9.6 %slice-start.3 = ((s8[6291456]{0:T(1024)(128)(4,1)}), s8[4194304]{0:T(1024)(128)(4,1)S(1)}, s32[]{:S(2)}) async-start(s8[6291456]{0:T(1024)(128)(4,1)} %bitcast.142), calls=%async_computation.8 | async-start | bytes 8388608
  475.2 56.7 %copy-start.1 = (bf16[1536,4,96]{0,2,1:T(8,128)(2,1)S(1)}, bf16[1536,4,96]{0,2,1:T(8,128)(2,1)}, u32[]{:S(2)}) copy-start(bf16[1536,4,96]{0,2,1:T(8,128)(2,1)} %param.24) | copy-start | bytes 3538948
  527.1 3.4 copy-start.9
Sparse Core Ops, SparseCore 0:
  45.2 54.9 all-reduce.7
  103.2 36.2 all-reduce.9
  150.8 37.6 all-reduce.11
  229.3 227.2 all-reduce.15
  459.6 67.5 all-reduce.13
where the time goes:
time: 547 us; the launch traced here: 539 us
  waiting for transfers between devices  323 us (59%)
  matrix products  77.2 us (14%)
  blocking collectives  65.3 us (12%)
  other arithmetic  47.1 us (9%)
  between operations  14.9 us (3%)
  local copies, waits for them, and re-layouts  10.5 us (2%)
    psum x1, waiting for transfers between devices, local_head(): lax.psum(jnp.dot(hidden, w_down, preferred_element_type=jnp.float32), 'tp')  173 us
    psum x1, waiting for transfers between devices, local_head(): lax.psum(jnp.einsum('bnw,bnhd->whd', normed, grad_keys, preferred_element...  42.6 us
    psum x1, waiting for transfers between devices, local_head(): lax.psum(jnp.einsum('bhn,bnhd->bhd', exp_scores.astype(jnp.bfloat16), val...  40.5 us
    psum x1, waiting for transfers between devices, local_head(): lax.psum(jnp.einsum('bf,wf->bw', grad_pre, w_up, preferred_element_type=j...  33.7 us
    psum x1, waiting for transfers between devices, local_head(): lax.psum(jnp.einsum('bhd,hdw->bw', pooled_bf, w_out, preferred_element_ty...  32.9 us
    psum x1, blocking collectives, local_head(): lax.psum(jnp.sum(weights * grad_weights, axis=-1, keepdims=True), 'sp')  14.6 us
    psum x1, blocking collectives, local_head(): exp_total = lax.psum(jnp.sum(exp_scores, axis=-1, keepdims=True), 'sp')  14.6 us
    pmax x1, blocking collectives, local_head(): score_max = lax.pmax(jnp.max(scores, axis=-1, keepdims=True), 'sp')  13.8 us
  transfers between devices with their start and end apart: 5, of which 5 were waited for; matrix products, arithmetic and copies ran while one was open for 12% of the time, Pallas kernels for 0%

commit v1 on v0

v1 whole, which is shorter than its diff:
```python
import functools
import jax
import jax.numpy as jnp
from jax import lax
from jax.experimental import pallas as pl
from jax.experimental.pallas import tpu as pltpu
from jax.sharding import PartitionSpec as P

NORM_EPS = 1e-6
MESH = pl.DeviceIdType.MESH
F32, BF16 = jnp.float32, jnp.bfloat16
IN_SPECS = (P('dp', 'sp', None), P(), P(), P(), P(None, 'tp', None), P('tp', None), P(None, 'tp', None), P(None, 'tp', None), P('tp', None), P('tp', None, None), P(), P(), P(), P(None, 'tp'), P('tp'), P('tp', None), P(), P('dp', None))
OUT_SPECS = (P('dp', None), P('dp', 'sp', None), P('dp'), P('dp', 'tp', None), P('dp', 'tp', None), P('dp', 'tp', None), P(('dp', 'tp'), None, None), P('dp', 'tp'), P(('dp', 'tp'), None))
LANES = 128
SUB = 8
GELU_C = 0.7978845608028654
GELU_A = 0.044715


def nn(a, b):
    return lax.dot_general(a, b, (((1,), (0,)), ((), ())), preferred_element_type=F32)


def nt(a, b):
    return lax.dot_general(a, b, (((1,), (1,)), ((), ())), preferred_element_type=F32)


def tn(a, b):
    return lax.dot_general(a, b, (((0,), (0,)), ((), ())), preferred_element_type=F32)


def hi_lo(a):
    hi = a.astype(BF16)
    return hi, (a - hi.astype(F32)).astype(BF16)


def iota(shape, dim):
    return lax.broadcasted_iota(jnp.int32, shape, dim)


def by_head(parts, width):
    rows, cols = parts[0].shape[0], len(parts) * width
    block = iota((rows, cols), 1) // width
    out = jnp.zeros((rows, cols), F32)
    for h, part in enumerate(parts):
        out = jnp.where(block == h, part, out)
    return out


def gelu_parts(pre):
    t = jnp.tanh(GELU_C * (pre + GELU_A * pre * pre * pre))
    value = 0.5 * pre * (1.0 + t)
    slope = 0.5 * (1.0 + t) + 0.5 * pre * (1.0 - t * t) * (GELU_C * (1.0 + 3.0 * GELU_A * pre * pre))
    return value, slope


def centre(rows):
    mean = jnp.mean(rows, axis=-1, keepdims=True)
    centred = rows - mean
    inv = lax.rsqrt(jnp.mean(centred * centred, axis=-1, keepdims=True) + NORM_EPS)
    return centred * inv, inv


def norm_back(hat, inv, cot):
    return inv * (cot - jnp.mean(cot, axis=-1, keepdims=True) - hat * jnp.mean(cot * hat, axis=-1, keepdims=True))


def barrier_all(peers):
    sem = pltpu.get_barrier_semaphore()
    for axis, dev in peers:
        pl.semaphore_signal(sem, inc=1, device_id={axis: dev}, device_id_type=MESH)
    pl.semaphore_wait(sem, len(peers))


def peers_of(axis, n):
    me = lax.axis_index(axis)
    return me, [lax.rem(me + k, n) for k in range(1, n)]


def remote(src, dst, send_sem, recv_sem, axis, dev):
    return pltpu.make_async_remote_copy(src_ref=src, dst_ref=dst, send_sem=send_sem, recv_sem=recv_sem, device_id={axis: dev}, device_id_type=MESH)


def gather_start(buf, me, peers, send_sems, recv_sems, axis):
    for k, dev in enumerate(peers):
        remote(buf.at[me], buf.at[me], send_sems.at[k], recv_sems.at[me], axis, dev).start()


def gather_wait(buf, me, peers, send_sems, recv_sems, axis):
    for k, dev in enumerate(peers):
        remote(buf.at[dev], buf.at[dev], send_sems.at[k], recv_sems.at[dev], axis, dev).wait_recv()
    for k, dev in enumerate(peers):
        remote(buf.at[me], buf.at[me], send_sems.at[k], recv_sems.at[me], axis, dev).wait_send()


def scan_kernel(heads, scale, x_ref, gain_ref, bias_ref, probe_ref, wq_ref, bq_ref, wk_ref, wv_ref, bv_ref, pk_ref, hb_ref, qk_ref, q_ref, qkr):
    rows = heads * SUB
    width = wq_ref.shape[0] // heads

    @pl.when(pl.program_id(0) == 0)
    def _():
        probe8 = jnp.broadcast_to(probe_ref[...].astype(BF16), (SUB, probe_ref.shape[1]))
        q8 = (nt(probe8, wq_ref[...]) + bq_ref[...]).astype(BF16)
        q_ref[...] = q8.astype(F32)
        qs = jnp.concatenate([q8.astype(F32)] * heads, axis=0)
        qs = jnp.where(iota(qs.shape, 0) // SUB == iota(qs.shape, 1) // width, qs, 0.0).astype(BF16)
        qk = nn(qs, wk_ref[...])
        hi, lo = hi_lo(qk)
        qkr[...] = jnp.zeros(qkr.shape, BF16)
        qkr[0:rows, :] = hi
        qkr[LANES // 2:LANES // 2 + rows, :] = lo
        for h in range(heads):
            qk_ref[h:h + 1, :] = qk[SUB * h:SUB * h + 1, :]

    images, tokens = SUB, x_ref.shape[0] // SUB
    hat, _ = centre(x_ref[...].astype(F32))
    hid = (hat * gain_ref[...] + bias_ref[...]).astype(BF16)
    r = nt(hid, qkr[...])
    s = ((r + pltpu.roll(r, LANES // 2, 1)) * scale).reshape(images, tokens, LANES)
    m = jnp.max(s, axis=1)
    e = jnp.exp(s - m[:, None, :])
    l = jnp.sum(e, axis=1)
    lane, img = iota(e.shape, 2), iota(e.shape, 0)
    ebd = jnp.where((lane % SUB == img) & (lane < rows), e, 0.0).astype(BF16).reshape(images * tokens, LANES)
    hb = tn(ebd, hid)[0:rows, :]
    hb_ref[0, :, :] = hb
    hi, lo = hi_lo(hb)
    v = nt(jnp.concatenate([hi, lo], axis=0), wv_ref[...])
    v = v[0:rows] + v[rows:2 * rows]
    cols = wq_ref.shape[0]
    vs = by_head([v[SUB * h:SUB * h + SUB] for h in range(heads)], width)
    vs = vs + by_head([l[:, SUB * h:SUB * h + 1] for h in range(heads)], width) * bv_ref[...]
    pk_ref[:, 0:cols] = vs
    pk_ref[:, cols:cols + LANES] = m
    pk_ref[:, cols + LANES:cols + 2 * LANES] = l


def scan_tokens(heads, images, scale, x, gain, bias, probe, wq, bq, wk, wv, bv):
    tokens_all, width = x.shape
    hd = wq.shape[0]
    groups = images // SUB
    block = tokens_all // groups
    full = lambda a: pl.BlockSpec(a.shape, lambda g: (0,) * a.ndim)
    return pl.pallas_call(
        functools.partial(scan_kernel, heads, scale),
        grid=(groups,),
        in_specs=[pl.BlockSpec((block, width), lambda g: (g, 0))] + [full(a) for a in (gain, bias, probe, wq, bq, wk, wv, bv)],
        out_specs=[pl.BlockSpec((SUB, hd + 2 * LANES), lambda g: (g, 0)), pl.BlockSpec((1, heads * SUB, width), lambda g: (g, 0, 0)), pl.BlockSpec((heads, width), lambda g: (0, 0)), pl.BlockSpec((SUB, hd), lambda g: (0, 0))],
        out_shape=[jax.ShapeDtypeStruct((images, hd + 2 * LANES), F32), jax.ShapeDtypeStruct((groups, heads * SUB, width), F32), jax.ShapeDtypeStruct((heads, width), F32), jax.ShapeDtypeStruct((SUB, hd), F32)],
        scratch_shapes=[pltpu.VMEM((LANES, width), BF16)],
        cost_estimate=pl.CostEstimate(flops=2 * tokens_all * width * 3 * LANES, bytes_accessed=tokens_all * width * 2, transcendentals=0),
        name='scan_tokens',
    )(x, gain, bias, probe, wq, bq, wk, wv, bv)


def head_kernel(heads, nsp, ntp, pk_ref, wo_hbm, wu_hbm, wd_hbm, og_ref, bo_ref, hg_ref, hb_ref, bu_ref, bd_ref, bv_ref,
                y_out, ga_out, pool_out, pb_out, st_out,
                wo, wu, wd, rbuf, ta, tg, td, ag, wsem, rs_send, rs_recv, ta_s, ta_r, tg_s, tg_r, td_s, td_r, ag_s, ag_r):
    sp, sp_peers = peers_of('sp', nsp)
    tp, tp_peers = peers_of('tp', ntp)
    loads = [pltpu.make_async_copy(a, b, wsem.at[i]) for i, (a, b) in enumerate(((wd_hbm, wd), (wo_hbm, wo), (wu_hbm, wu)))]
    for load in loads:
        load.start()
    barrier_all([('sp', d) for d in sp_peers] + [('tp', d) for d in tp_peers])
    sends = []
    for k, dev in enumerate(sp_peers):
        sends.append(remote(pk_ref.at[dev], rbuf.at[sp], rs_send.at[k], rs_recv.at[sp], 'sp', dev))
        sends[-1].start()
    rbuf[sp] = pk_ref[sp]
    hd = wo.shape[0]
    width = hd // heads
    model = wu.shape[0]
    og = og_ref[sp]
    loads[0].wait()
    gh = nt(og, wd[...])
    for k, dev in enumerate(sp_peers):
        remote(rbuf.at[dev], rbuf.at[dev], rs_send.at[k], rs_recv.at[dev], 'sp', dev).wait_recv()
    for send in sends:
        send.wait_send()
    m = rbuf[0, :, hd:hd + LANES]
    for j in range(1, nsp):
        m = jnp.maximum(m, rbuf[j, :, hd:hd + LANES])
    l = jnp.zeros_like(m)
    v = jnp.zeros((SUB, hd), F32)
    for j in range(nsp):
        w = jnp.exp(rbuf[j, :, hd:hd + LANES] - m)
        l = l + w * rbuf[j, :, hd + LANES:hd + 2 * LANES]
        v = v + by_head([w[:, SUB * h:SUB * h + 1] for h in range(heads)], width) * rbuf[j, :, 0:hd]
    o = v / by_head([l[:, SUB * h:SUB * h + 1] for h in range(heads)], width)
    pooled_bf = o.astype(BF16)
    lse = m + jnp.log(l)
    loads[1].wait()
    ta[tp] = nn(pooled_bf, wo[...])
    gather_start(ta, tp, tp_peers, ta_s, ta_r, 'tp')
    loads[2].wait()
    gather_wait(ta, tp, tp_peers, ta_s, ta_r, 'tp')
    attn = bo_ref[...] + ((ta[0] + ta[1]) + (ta[2] + ta[3])) if ntp == 4 else bo_ref[...] + sum(ta[t] for t in range(ntp))
    hat, inv = centre(attn)
    y = (hat * hg_ref[...] + hb_ref[...]).astype(BF16)
    value, slope = gelu_parts(nn(y, wu[...]) + bu_ref[...])
    hidden = value.astype(BF16)
    tg[tp] = nt((gh * slope).astype(BF16), wu[...])
    gather_start(tg, tp, tp_peers, tg_s, tg_r, 'tp')
    td[tp] = nn(hidden, wd[...])
    gather_start(td, tp, tp_peers, td_s, td_r, 'tp')
    gather_wait(tg, tp, tp_peers, tg_s, tg_r, 'tp')
    gno = tg[0]
    for t in range(1, ntp):
        gno = gno + tg[t]
    ga = (og.astype(F32) + norm_back(hat, inv, gno * hg_ref[...])).astype(BF16)
    gp = nt(ga, wo[...]).astype(BF16).astype(F32)
    prod = gp * (o - bv_ref[...])
    head_of = iota(prod.shape, 1) // width
    delta = by_head([jnp.sum(jnp.where(head_of == h, prod, 0.0), axis=1, keepdims=True) for h in range(heads)], SUB)
    gather_wait(td, tp, tp_peers, td_s, td_r, 'tp')
    down = td[0]
    for t in range(1, ntp):
        down = down + td[t]
    ag[sp, :, 0:model] = y.astype(F32)
    ag[sp, :, model:2 * model] = ga.astype(F32)
    ag[sp, :, 2 * model:3 * model] = (attn + down + bd_ref[...]).astype(BF16).astype(F32)
    base = 3 * model
    ag[sp, :, base:base + hd] = pooled_bf.astype(F32)
    ag[sp, :, base + hd:base + hd + LANES] = lse
    ag[sp, :, base + hd + LANES:base + hd + 2 * LANES] = jnp.concatenate([delta, jnp.zeros((SUB, LANES - heads * SUB), F32)], axis=1)
    gather_start(ag, sp, sp_peers, ag_s, ag_r, 'sp')
    gather_wait(ag, sp, sp_peers, ag_s, ag_r, 'sp')
    y_out[...] = ag[:, :, 0:model].astype(BF16)
    ga_out[...] = ag[:, :, model:2 * model].astype(BF16)
    pool_out[...] = ag[:, :, 2 * model:3 * model].astype(BF16)
    pb_out[...] = ag[:, :, base:base + hd].astype(BF16)
    st_out[...] = ag[:, :, base + hd:base + hd + 2 * LANES]


def head(heads, nsp, ntp, pk, wo, wu, wd, og, bo, hg, hb, bu, bd, bv):
    images, model = og.shape
    hd = wo.shape[0]
    own = images // nsp
    pk3 = pk.reshape(nsp, own, pk.shape[1])
    og3 = og.reshape(nsp, own, model)
    vm, hbm = pl.BlockSpec(memory_space=pltpu.VMEM), pl.BlockSpec(memory_space=pl.ANY)
    dma = pltpu.SemaphoreType.DMA
    cols = 3 * model + hd + 2 * LANES
    part = pltpu.VMEM((ntp, own, model), F32)
    shapes = [(model, BF16), (model, BF16), (model, BF16), (hd, BF16), (2 * LANES, F32)]
    return pl.pallas_call(
        functools.partial(head_kernel, heads, nsp, ntp),
        in_specs=[vm, hbm, hbm, hbm] + [vm] * 7,
        out_specs=[vm] * 5,
        out_shape=[jax.ShapeDtypeStruct((nsp, own, c), d) for c, d in shapes],
        scratch_shapes=[pltpu.VMEM(wo.shape, BF16), pltpu.VMEM(wu.shape, BF16), pltpu.VMEM(wd.shape, BF16), pltpu.VMEM(pk3.shape, F32), part, part, part, pltpu.VMEM((nsp, own, cols), F32),
                        dma((3,)), dma((nsp - 1,)), dma((nsp,)), dma((ntp - 1,)), dma((ntp,)), dma((ntp - 1,)), dma((ntp,)), dma((ntp - 1,)), dma((ntp,)), dma((nsp - 1,)), dma((nsp,))],
        compiler_params=pltpu.CompilerParams(collective_id=0, has_side_effects=True),
        name='head',
    )(pk3, wo, wu, wd, og3, bo, hg, hb, bu, bd, bv)


def spread_kernel(heads, nsp, ntp, ga_ref, wo_ref, wv_ref, hb_ref, pk_ref, st_ref, qk_ref,
                  gv_out, hbar_out, st_out, qk_out,
                  hs, hr, ha, gv_s, gv_r, fw_s, fw_r, hs_s, hs_r, ha_s, ha_r, st_s, st_r, qk_s, qk_r):
    sp, sp_peers = peers_of('sp', nsp)
    tp, tp_peers = peers_of('tp', ntp)
    core = lax.rem(sp, 2)
    mate = sp + 1 - 2 * core
    half = nsp // 2
    hd = wo_ref.shape[0]
    width = hd // heads
    model = wo_ref.shape[1]
    rows = heads * SUB

    def make_gv(i, _):
        g = lax.rem(core * half + i, nsp)
        gp = nt(ga_ref[g], wo_ref[...]).astype(BF16).astype(F32)
        gp = jnp.concatenate([gp] * heads, axis=0)
        gp = jnp.where(iota(gp.shape, 0) // SUB == iota(gp.shape, 1) // width, gp, 0.0).astype(BF16)
        gv_out[tp, g] = nn(gp, wv_ref[...])
        return 0

    lax.fori_loop(0, half, make_gv, 0)

    def make_hs(g, _):
        w = jnp.exp(pk_ref[g, :, hd:hd + LANES] - st_ref[g, :, 0:LANES])
        col = jnp.concatenate([w[:, SUB * h:SUB * h + 1] for h in range(heads)], axis=0)
        hs[g] = hb_ref[g] * col
        return 0

    lax.fori_loop(0, nsp, make_hs, 0)
    st_out[tp] = st_ref[...]
    qk_out[tp] = qk_ref[...]
    barrier_all([('sp', d) for d in sp_peers] + [('tp', d) for d in tp_peers])
    for i in range(half):
        g = core * half + i
        for k, dev in enumerate(tp_peers):
            remote(gv_out.at[tp, g], gv_out.at[tp, g], gv_s.at[k, i], gv_r.at[tp, i], 'tp', dev).start()
    for k, dev in enumerate(sp_peers):
        remote(hs.at[dev], hr.at[sp], hs_s.at[k], hs_r.at[sp], 'sp', dev).start()
    gather_start(st_out, tp, tp_peers, st_s, st_r, 'tp')
    gather_start(qk_out, tp, tp_peers, qk_s, qk_r, 'tp')
    lax.fori_loop(half, nsp, make_gv, 0)
    for k, dev in enumerate(sp_peers):
        remote(hr.at[dev], hr.at[dev], hs_s.at[k], hs_r.at[dev], 'sp', dev).wait_recv()
    for k, dev in enumerate(sp_peers):
        remote(hs.at[dev], hr.at[sp], hs_s.at[k], hs_r.at[sp], 'sp', dev).wait_send()
    hr[sp] = hs[sp]
    total = hr[0]
    for j in range(1, nsp):
        total = total + hr[j]
    ha[sp] = total
    gather_start(ha, sp, sp_peers, ha_s, ha_r, 'sp')
    for i in range(half):
        g = core * half + i
        for k, dev in enumerate(tp_peers):
            remote(gv_out.at[dev, g], gv_out.at[dev, g], gv_s.at[k, i], gv_r.at[dev, i], 'tp', dev).wait_recv()
            remote(gv_out.at[dev, g], gv_out.at[dev, g], fw_s.at[k, i], fw_r.at[dev, i], 'sp', mate).start()
    for i in range(half):
        g = core * half + i
        other = (1 - core) * half + i
        for k, dev in enumerate(tp_peers):
            remote(gv_out.at[tp, g], gv_out.at[tp, g], gv_s.at[k, i], gv_r.at[tp, i], 'tp', dev).wait_send()
            remote(gv_out.at[dev, g], gv_out.at[dev, g], fw_s.at[k, i], fw_r.at[dev, i], 'sp', mate).wait_send()
            remote(gv_out.at[dev, other], gv_out.at[dev, other], fw_s.at[k, i], fw_r.at[dev, i], 'sp', mate).wait_recv()
    gather_wait(st_out, tp, tp_peers, st_s, st_r, 'tp')
    gather_wait(qk_out, tp, tp_peers, qk_s, qk_r, 'tp')
    gather_wait(ha, sp, sp_peers, ha_s, ha_r, 'sp')
    hbar_out[...] = ha[...].astype(BF16)


def spread(heads, nsp, ntp, ga3, wo, wv, hb, pk, st, qk):
    groups, rows, model = hb.shape
    vm = pl.BlockSpec(memory_space=pltpu.VMEM)
    dma = pltpu.SemaphoreType.DMA
    half = nsp // 2
    pk3 = pk.reshape(nsp, -1, pk.shape[1])
    slots = pltpu.VMEM((nsp, rows, model), F32)
    return pl.pallas_call(
        functools.partial(spread_kernel, heads, nsp, ntp),
        in_specs=[vm] * 7,
        out_specs=[vm] * 4,
        out_shape=[jax.ShapeDtypeStruct((ntp, nsp, rows, model), F32), jax.ShapeDtypeStruct((nsp, rows, model), BF16), jax.ShapeDtypeStruct((ntp,) + st.shape, F32), jax.ShapeDtypeStruct((ntp,) + qk.shape, F32)],
        scratch_shapes=[slots, slots, slots, dma((ntp - 1, half)), dma((ntp, half)), dma((ntp - 1, half)), dma((ntp, half)), dma((nsp - 1,)), dma((nsp,)), dma((nsp - 1,)), dma((nsp,)), dma((ntp - 1,)), dma((ntp,)), dma((ntp - 1,)), dma((ntp,))],
        compiler_params=pltpu.CompilerParams(collective_id=1, has_side_effects=True),
        name='spread',
    )(ga3, wo, wv, hb, pk3, st, qk)


def back_kernel(heads, ntp, scale, x_ref, gain_ref, bias_ref, gv_ref, qk_ref, st_ref, gx_ref, u_ref, qkr, uacc):
    step = pl.program_id(0)
    rows = heads * SUB
    model = x_ref.shape[1]

    @pl.when(step == 0)
    def _():
        for t in range(ntp):
            for h in range(heads):
                hi, lo = hi_lo(jnp.broadcast_to(qk_ref[t, h:h + 1, :], (SUB, model)))
                at = (t * heads + h) * SUB
                qkr[at:at + SUB, :] = hi.astype(F32)
                qkr[LANES + at:LANES + at + SUB, :] = lo.astype(F32)
        uacc[...] = jnp.zeros(uacc.shape, F32)

    images, tokens = SUB, x_ref.shape[0] // SUB
    hat, inv = centre(x_ref[...].astype(F32))
    gain = gain_ref[...]
    hid = (hat * gain + bias_ref[...]).astype(BF16)
    qkb = qkr[...].astype(BF16)
    gv_hi, gv_lo = hi_lo(gv_ref[...].reshape(ntp * rows, model))
    r = nt(hid, qkb)
    s = (r[:, 0:LANES] + r[:, LANES:2 * LANES]) * scale
    d = nt(hid, jnp.concatenate([gv_hi, gv_lo], axis=0))
    d = d[:, 0:LANES] + d[:, LANES:2 * LANES]
    lse = jnp.concatenate([st_ref[t, 0, :, 0:rows] for t in range(ntp)], axis=1)
    delta = jnp.concatenate([st_ref[t, 0, :, LANES:LANES + rows] for t in range(ntp)], axis=1)
    shape = (images, tokens, LANES)
    keep = iota(shape, 2) % SUB == iota(shape, 0)
    p = jnp.where(keep, jnp.exp(s.reshape(shape) - lse[:, None, :]), 0.0)
    ds = p * (d.reshape(shape) - delta[:, None, :]) * scale
    pb = p.astype(BF16).reshape(images * tokens, LANES)
    db = ds.astype(BF16).reshape(images * tokens, LANES)
    gh = nn(jnp.concatenate([pb, db], axis=1), jnp.concatenate([gv_hi, qkb[0:LANES]], axis=0))
    uacc[...] += tn(db, hid)
    gx_ref[...] = norm_back(hat, inv, gh * gain).astype(BF16)

    @pl.when(step == pl.num_programs(0) - 1)
    def _():
        tp = lax.axis_index('tp')
        for h in range(heads):
            mine = uacc[pl.ds(pl.multiple_of(tp * rows + h * SUB, SUB), SUB), :]
            u_ref[h:h + 1, :] = jnp.sum(mine, axis=0, keepdims=True)


def back_tokens(heads, ntp, scale, x, gain, bias, gv, qk, st):
    tokens_all, model = x.shape
    groups, rows = gv.shape[1], gv.shape[2]
    block = tokens_all // groups
    full = lambda a: pl.BlockSpec(a.shape, lambda g: (0,) * a.ndim)
    return pl.pallas_call(
        functools.partial(back_kernel, heads, ntp, scale),
        grid=(groups,),
        in_specs=[pl.BlockSpec((block, model), lambda g: (g, 0)), full(gain), full(bias), pl.BlockSpec((ntp, 1, rows, model), lambda g: (0, g, 0, 0)), full(qk), pl.BlockSpec((ntp, 1) + st.shape[2:], lambda g: (0, g, 0, 0))],
        out_specs=[pl.BlockSpec((block, model), lambda g: (g, 0)), pl.BlockSpec((heads, model), lambda g: (0, 0))],
        out_shape=[jax.ShapeDtypeStruct((tokens_all, model), BF16), jax.ShapeDtypeStruct((heads, model), F32)],
        scratch_shapes=[pltpu.VMEM((2 * LANES, model), F32), pltpu.VMEM((LANES, model), F32)],
        name='back_tokens',
    )(x, gain, bias, gv, qk, st)


def query_kernel(heads, nsp, ntp, u_ref, q_ref, probe_ref, wq_ref, wk_ref, gwq_out, gwk_out, gpr_out, ub, pb, u_s, u_r, p_s, p_r):
    sp, sp_peers = peers_of('sp', nsp)
    tp, tp_peers = peers_of('tp', ntp)
    ub[sp] = u_ref[...]
    barrier_all([('sp', d) for d in sp_peers] + [('tp', d) for d in tp_peers])
    gather_start(ub, sp, sp_peers, u_s, u_r, 'sp')
    gather_wait(ub, sp, sp_peers, u_s, u_r, 'sp')
    u = ub[0]
    for j in range(1, nsp):
        u = u + ub[j]
    hd = wk_ref.shape[0]
    width = hd // heads
    hi, lo = hi_lo(u)
    g = nt(jnp.concatenate([hi, lo], axis=0), wk_ref[...])
    g = g[0:heads] + g[heads:2 * heads]
    gq = jnp.sum(jnp.where(iota(g.shape, 0) == iota(g.shape, 1) // width, g, 0.0), axis=0, keepdims=True)
    hi, lo = hi_lo(gq)
    gpr = nn(jnp.concatenate([hi, lo], axis=0), wq_ref[...])
    pb[tp] = gpr[0:1] + gpr[1:2]
    gather_start(pb, tp, tp_peers, p_s, p_r, 'tp')
    qcol = jnp.transpose(q_ref[...])[:, 0:1]
    gcol = jnp.transpose(jnp.broadcast_to(gq, (SUB, hd)))[:, 0:1]
    for h in range(heads):
        at = slice(width * h, width * h + width)
        gwk_out[at, :] = qcol[at, :] * u[h:h + 1, :]
        gwq_out[at, :] = gcol[at, :] * probe_ref[...]
    gather_wait(pb, tp, tp_peers, p_s, p_r, 'tp')
    total = pb[0]
    for t in range(1, ntp):
        total = total + pb[t]
    gpr_out[...] = total


def query_grads(heads, nsp, ntp, u, q, probe, wq, wk):
    hd, model = wq.shape
    vm = pl.BlockSpec(memory_space=pltpu.VMEM)
    dma = pltpu.SemaphoreType.DMA
    return pl.pallas_call(
        functools.partial(query_kernel, heads, nsp, ntp),
        in_specs=[vm] * 5,
        out_specs=[vm] * 3,
        out_shape=[jax.ShapeDtypeStruct((hd, model), F32), jax.ShapeDtypeStruct((hd, model), F32), jax.ShapeDtypeStruct((1, model), F32)],
        scratch_shapes=[pltpu.VMEM((nsp, heads, model), F32), pltpu.VMEM((ntp, 1, model), F32), dma((nsp - 1,)), dma((nsp,)), dma((ntp - 1,)), dma((ntp,))],
        compiler_params=pltpu.CompilerParams(collective_id=2, has_side_effects=True),
        name='query_grads',
    )(u, q, probe, wq, wk)


def local_head(nsp, ntp, encoded, enc_gain, enc_bias, probe, w_query, b_query, w_key, w_value, b_value, w_out, b_out, head_gain, head_bias, w_up, b_up, w_down, b_down, out_grad):
    images, tokens, model = encoded.shape
    heads, head_dim = b_query.shape
    hd = heads * head_dim
    scale = head_dim ** -0.5
    x = encoded.reshape(images * tokens, model)
    wq, wk, wv = (jnp.transpose(w, (1, 2, 0)).reshape(hd, model) for w in (w_query, w_key, w_value))
    wo = w_out.reshape(hd, model)
    row = lambda a: a.reshape(1, -1)
    bv = row(b_value)
    pk, hb, qk, q8 = scan_tokens(heads, images, scale, x, row(enc_gain), row(enc_bias), row(probe), wq, row(b_query), wk, wv, bv)
    y3, ga3, pool3, pb3, st = head(heads, nsp, ntp, pk, wo, w_up, w_down, out_grad, row(b_out), row(head_gain), row(head_bias), row(b_up), row(b_down), bv)
    gv, hbar, st_all, qk_all = spread(heads, nsp, ntp, ga3, wo, wv, hb, pk, st, qk)
    gx, u = back_tokens(heads, ntp, scale, x, row(enc_gain), row(enc_bias), gv, qk_all, st_all)
    gwq, gwk, gpr = query_grads(heads, nsp, ntp, u, q8, row(probe), wq, wk)

    y, ga, pooled_bf = (a.reshape(images, -1) for a in (y3, ga3, pb3))
    pre = jnp.dot(y, w_up, preferred_element_type=F32) + b_up
    value, slope = gelu_parts(pre)
    grad_w_down = jnp.einsum('bf,bw->fw', value.astype(BF16), out_grad, preferred_element_type=F32)
    grad_hidden = jnp.einsum('bw,fw->bf', out_grad, w_down, preferred_element_type=F32)
    grad_w_up = jnp.einsum('bw,bf->wf', y, (grad_hidden * slope).astype(BF16), preferred_element_type=F32)
    grad_w_out = jnp.einsum('bk,bw->kw', pooled_bf, ga, preferred_element_type=F32).reshape(heads, head_dim, model)
    grad_pooled = jnp.einsum('bw,kw->bk', ga, wo, preferred_element_type=F32).astype(BF16)
    gp5 = grad_pooled.reshape(nsp, images // nsp, heads, head_dim)
    hbar4 = hbar.reshape(nsp, heads, images // nsp, model)
    grad_wv = jnp.einsum('gihd,ghiw->hdw', gp5, hbar4, preferred_element_type=F32)
    back = lambda a: jnp.transpose(a.reshape(heads, head_dim, model), (2, 0, 1))
    return (pool3.reshape(images, model), gx.reshape(encoded.shape), gpr.reshape(model), back(gwq), back(gwk), back(grad_wv), grad_w_out, grad_w_up, grad_w_down)


def solution(mesh):
    body = functools.partial(local_head, mesh.shape['sp'], mesh.shape['tp'])
    return jax.shard_map(body, mesh=mesh, in_specs=IN_SPECS, out_specs=OUT_SPECS, check_vma=False)
```

time: 547 us -> 187 us (0.34); the launches traced: 539 us -> 186 us
  waiting for transfers between devices: 323 us -> 0 us
  Pallas kernels: 0 us -> 144 us
  blocking collectives: 65.3 us -> 0 us
  matrix products: 77.2 us -> 22.7 us
  other arithmetic: 47.1 us -> 1.31 us
  between operations: 14.9 us -> 0.78 us
  local copies, waits for them, and re-layouts: 10.5 us -> 17.5 us
    psum x5 -> x0, waiting for transfers between devices: 323 us -> none  [the longest x1 173 us: local_head(): lax.psum(jnp.dot(hidden, w_down, preferred_element_type=jnp.float32), 'tp')]
    pallas_call x0 -> x5, Pallas kernels: none -> 144 us  [the longest x1 52.8 us: spread(): pl.pallas_call(functools.partial(spread_kernel, heads, nsp, ntp), in_spec...]
    dot_general x21 -> x6, matrix products: 77.2 us -> 22.7 us  [the longest x1 8.86 us: local_head(): jnp.einsum('bw,bf->wf', y, (grad_hidden * slope).astype(BF16), preferred_...]
    psum x4 -> x0, blocking collectives: 51.4 us -> none  [the longest x1 14.6 us: local_head(): lax.psum(jnp.sum(weights * grad_weights, axis=-1, keepdims=True), 'sp')]
    reduce_sum x10 -> x0, other arithmetic: 29.2 us -> none  [the longest x2 10.1 us: layer_norm(): centred = rows_in - row_mean]
    pmax x1 -> x0, blocking collectives: 13.8 us -> none  [local_head(): score_max = lax.pmax(jnp.max(scores, axis=-1, keepdims=True), 'sp')]
    convert_element_type x7 -> x0, other arithmetic: 13.4 us -> none  [the longest x1 9.25 us: local_head(): norm_vjp(enc_f32, enc_gain, enc_bias, grad_normed).astype(jnp.bfloat16)]
    reshape x0 -> x11, local copies, waits for them, and re-layouts: none -> 13.1 us  [the longest x10 13 us: local_head(): row = lambda a: a.reshape(1, -1)]
  transfers between devices with their start and end apart: 5 -> 0, of which waited for: 5 -> 0; matrix products, arithmetic and copies ran while one was open for 12% -> 0% of each run, Pallas kernels for 0% -> 0%
where the time goes in v1:
time: 187 us; the launch traced here: 186 us
  Pallas kernels  144 us (77%)
  matrix products  22.7 us (12%)
  local copies, waits for them, and re-layouts  17.5 us (9%)
    pallas_call x1, Pallas kernels, spread(): pl.pallas_call(functools.partial(spread_kernel, heads, nsp, ntp), in_spec...  52.8 us
    pallas_call x1, Pallas kernels, head(): pl.pallas_call(functools.partial(head_kernel, heads, nsp, ntp), in_specs=...  43.4 us
    pallas_call x1, Pallas kernels, scan_tokens(): pl.pallas_call(functools.partial(scan_kernel, heads, scale), grid=(groups...  18.1 us
    pallas_call x1, Pallas kernels, back_tokens(): pl.pallas_call(functools.partial(back_kernel, heads, ntp, scale), grid=(g...  15.8 us
    pallas_call x1, Pallas kernels, query_grads(): pl.pallas_call(functools.partial(query_kernel, heads, nsp, ntp), in_specs...  13.8 us
    reshape x10, local copies, waits for them, and re-layouts, local_head(): row = lambda a: a.reshape(1, -1)  13 us
    dot_general x1, matrix products, local_head(): jnp.einsum('bw,bf->wf', y, (grad_hidden * slope).astype(BF16), preferred_...  8.86 us
    dot_general x1, matrix products, local_head(): jnp.einsum('bf,bw->fw', value.astype(BF16), out_grad, preferred_element_t...  5.17 us

profile of v1, /device:TPU:97, one launch (start us, length us, event | category | flops | bytes accessed | tf_op | source)
XLA Modules:
  0.0 186.3 jit_solution(10971870945274942230)
XLA Ops:
  0.6 1.3 reshape.114.bv_ref
  2.0 1.3 reshape.111.bq_ref
  3.3 1.3 reshape.107.gain_ref
  4.6 1.3 reshape.108.bias_ref
  5.9 1.3 reshape.109.probe_ref
  7.2 1.3 reshape.118.bo_ref
  8.5 1.3 reshape.119.hg_ref
  9.8 1.3 reshape.120.hb_ref
  11.1 1.3 reshape.122.bd_ref
  12.4 1.3 reshape.121.bu_ref
  13.7 18.1 %scan_tokens.1 = (f32[64,640]{1,0:T(8,128)}, f32[8,32,1536]{2,1,0:T(8,128)}, f32[4,1536]{1,0:T(4,128)}, f32[8,384]{1,0:T(8,128)}) custom-call(bf16[2048,1536]{1,0:T(8,128)(2,1)} %bitcast.52, f32[1,1536]{1,0:T(1,128)} %reshape.107.gain_ref, f32[1,1536]{1,0:T(1,128)} %reshape.108.bias_ref, f32[1,1536]{1,0:T(1,128)} %reshape.109.probe_ref, ...), custom_call_target="tpu_custom_call" | custom-call | flops 2415919104 | bytes 6291456 | tf_op jit(solution)/shard_map/scan_tokens/pallas_call | solution.py:144
  31.8 0.0 copy-start
  31.8 0.0 copy-start.8
  31.8 43.4 %head.1 = (bf16[8,8,1536]{2,1,0:T(8,128)(2,1)}, bf16[8,8,1536]{2,1,0:T(8,128)(2,1)}, bf16[8,8,1536]{2,1,0:T(8,128)(2,1)}, bf16[8,8,384]{2,1,0:T(8,128)(2,1)}, f32[8,8,256]{2,1,0:T(8,128)}) custom-call(f32[8,8,640]{2,1,0:T(8,128)} %bitcast.66, bf16[384,1536]{1,0:T(8,128)(2,1)} %bitcast.54, bf16[1536,1536]{1,0:T(8,128)(2,1)} %wu_hbm.1, ...), custom_call_target="tpu_custom_call" | custom-call | tf_op jit(solution)/shard_map/head/pallas_call | solution.py:246
  75.2 0.0 copy-start.4
  75.2 0.0 copy-done
  75.2 1.5 convolution_convert_fusion
  76.7 0.1 reshape.129
  76.8 0.9 dot_general.28
  77.7 0.0 copy-done.8
  77.8 3.4 %convolution_add_fusion = f32[64,1536]{1,0:T(8,128)S(1)} fusion(bf16[1536,1536]{1,0:T(8,128)(2,1)} %wu_hbm.1, bf16[8,8,1536]{2,1,0:T(8,128)(2,1)} %get-tuple-element.44, f32[1536]{0:T(1024)S(1)} %copy-done.8), kind=kOutput, calls=%fused_computation.1 | convolution fusion | flops 302088192 | bytes 5314560 | tf_op jit(solution)/shard_map/dot_general | solution.py:472
  81.1 0.0 copy-done.4
  81.2 1.9 %fusion.18 = f32[4,96,1536]{2,1,0:T(8,128)} fusion(bf16[8,8,1536]{2,1,0:T(8,128)(2,1)S(1)} %copy-done.4, bf16[4,96,64]{1,0,2:T(4,128)(2,1)S(1)} %dot_general.28), kind=kOutput, calls=%fused_computation.23 | convolution fusion | flops 75497472 | bytes 2605056 | tf_op jit(solution)/shard_map/bk,bw->kw/dot_general | solution.py:477
  83.1 52.8 %spread.1 = (f32[4,8,32,1536]{3,2,1,0:T(8,128)}, bf16[8,32,1536]{2,1,0:T(8,128)(2,1)}, f32[4,8,8,256]{3,2,1,0:T(8,128)}, f32[4,4,1536]{2,1,0:T(4,128)}) custom-call(bf16[8,8,1536]{2,1,0:T(8,128)(2,1)} %get-tuple-element.29.ga_ref, bf16[384,1536]{1,0:T(8,128)(2,1)} %bitcast.55, bf16[384,1536]{1,0:T(8,128)(2,1)} %bitcast.62, ...), custom_call_target="tpu_custom_call" | custom-call | tf_op jit(solution)/shard_map/spread/pallas_call | solution.py:335
  135.8 0.0 copy-start.6
  135.8 15.8 %back_tokens.1 = (bf16[2048,1536]{1,0:T(8,128)(2,1)}, f32[4,1536]{1,0:T(4,128)}) custom-call(bf16[2048,1536]{1,0:T(8,128)(2,1)} %bitcast.53, f32[1,1536]{1,0:T(1,128)} %reshape.107.gain_ref, f32[1,1536]{1,0:T(1,128)} %reshape.108.bias_ref, f32[4,8,32,1536]{3,2,1,0:T(8,128)} %get-tuple-element.33.gv_ref, f32[4,4,1536]{2,1,0:T(4,128)} %get-tuple-element.34.qk_ref, ...), custom_call_target="tpu_custom_call" | custom-call | tf_op jit(solution)/shard_map/back_tokens/pallas_call | solution.py:396
  151.7 0.0 copy-start.3
  151.7 0.0 copy-start.5
  151.7 0.0 copy-done.6
  151.7 1.9 %convolution_bitcast_fusion = f32[1536,4,96]{0,2,1:T(8,128)} fusion(bf16[8,8,4,96]{3,2,1,0:T(4,128)(2,1)S(1)} %reshape.129, bf16[8,32,1536]{2,1,0:T(8,128)(2,1)S(1)} %copy-done.6), kind=kOutput, calls=%fused_computation | convolution fusion | flops 75497472 | bytes 3194880 | tf_op jit(solution)/shard_map/gihd,ghiw->hdw/dot_general | solution.py:481
  153.6 13.8 %query_grads.1 = (f32[384,1536]{1,0:T(8,128)}, f32[384,1536]{1,0:T(8,128)}, f32[1,1536]{1,0:T(1,128)}) custom-call(f32[4,1536]{1,0:T(4,128)} %get-tuple-element.37.u_ref, f32[8,384]{1,0:T(8,128)} %get-tuple-element.38.q_ref, f32[1,1536]{1,0:T(1,128)} %reshape.109.probe_ref, bf16[384,1536]{1,0:T(8,128)(2,1)} %bitcast.58, bf16[384,1536]{1,0:T(8,128)(2,1)} %bitcast.60), custom_call_target="tpu_custom_call" | custom-call | tf_op jit(solution)/shard_map/query_grads/pallas_call | solution.py:444
  167.4 1.3 reduce
  168.7 0.0 copy-done.3
  168.7 0.0 copy-done.5
  168.7 8.9 %fusion.1 = f32[1536,1536]{1,0:T(8,128)} fusion(bf16[64,1536]{1,0:T(8,128)(2,1)S(1)} %copy-done.3, bf16[1536,1536]{1,0:T(8,128)(2,1)} %wd_hbm.1, f32[64,1536]{1,0:T(8,128)S(1)} %convolution_add_fusion, bf16[8,8,1536]{2,1,0:T(8,128)(2,1)S(1)} %copy-done.5), kind=kOutput, calls=%fused_computation.4 | convolution fusion | flops 605847552 | bytes 14942208 | tf_op jit(solution)/shard_map/bw,bf->wf/dot_general | solution.py:476
  177.6 0.0 copy-start.7
  177.6 0.0 copy-start.2
  177.6 5.2 %fusion.17 = f32[1536,1536]{1,0:T(8,128)} fusion(bf16[64,1536]{1,0:T(8,128)(2,1)S(1)} %copy-done.3, f32[64,1536]{1,0:T(8,128)S(1)} %convolution_add_fusion), kind=kOutput, calls=%fused_computation.22 | convolution fusion | flops 302874624 | bytes 10027008 | tf_op jit(solution)/shard_map/bf,bw->fw/dot_general | solution.py:474
  182.8 0.0 copy-done.7
  182.8 0.0 copy-start.1
  182.8 0.7 copy.42
  183.5 0.0 copy-done.2
  183.5 1.4 copy.43
  184.9 0.0 copy-done.1
  184.9 1.4 copy.44
Async XLA Ops:
  31.8 43.5 %copy-start = (bf16[4,96,1536]{2,1,0:T(8,128)(2,1)S(1)}, bf16[4,96,1536]{2,1,0:T(8,128)(2,1)}, u32[]{:S(2)}) copy-start(bf16[4,96,1536]{2,1,0:T(8,128)(2,1)} %param.27) | copy-start | bytes 3538948
  31.8 46.0 %copy-start.8 = (f32[1536]{0:T(1024)S(1)}, f32[1536]{0:T(1024)}, u32[]{:S(2)}) copy-start(f32[1536]{0:T(1024)} %param.32) | copy-start | bytes 18436
  75.2 5.9 %copy-start.4 = (bf16[8,8,1536]{2,1,0:T(8,128)(2,1)S(1)}, bf16[8,8,1536]{2,1,0:T(8,128)(2,1)}, u32[]{:S(2)}) copy-start(bf16[8,8,1536]{2,1,0:T(8,128)(2,1)} %get-tuple-element.29.ga_ref) | copy-start | bytes 589828
  135.8 15.9 %copy-start.6 = (bf16[8,32,1536]{2,1,0:T(8,128)(2,1)S(1)}, bf16[8,32,1536]{2,1,0:T(8,128)(2,1)}, u32[]{:S(2)}) copy-start(bf16[8,32,1536]{2,1,0:T(8,128)(2,1)} %get-tuple-element.42) | copy-start | bytes 2359300
  151.7 17.1 %copy-start.3 = (bf16[64,1536]{1,0:T(8,128)(2,1)S(1)}, bf16[64,1536]{1,0:T(8,128)(2,1)}, u32[]{:S(2)}) copy-start(bf16[64,1536]{1,0:T(8,128)(2,1)} %param.35) | copy-start | bytes 589828
  151.7 17.1 %copy-start.5 = (bf16[8,8,1536]{2,1,0:T(8,128)(2,1)S(1)}, bf16[8,8,1536]{2,1,0:T(8,128)(2,1)}, u32[]{:S(2)}) copy-start(bf16[8,8,1536]{2,1,0:T(8,128)(2,1)} %get-tuple-element.44) | copy-start | bytes 589828
  177.6 5.2 %copy-start.7 = (bf16[8,8,1536]{2,1,0:T(8,128)(2,1)S(1)}, bf16[8,8,1536]{2,1,0:T(8,128)(2,1)}, u32[]{:S(2)}) copy-start(bf16[8,8,1536]{2,1,0:T(8,128)(2,1)} %get-tuple-element.28) | copy-start | bytes 589828
  177.6 5.9 %copy-start.2 = (f32[384,1536]{1,0:T(8,128)S(1)}, f32[384,1536]{1,0:T(8,128)}, u32[]{:S(2)}) copy-start(f32[384,1536]{1,0:T(8,128)} %get-tuple-element.40) | copy-start | bytes 7077892
  182.8 2.1 %copy-start.1 = (f32[384,1536]{1,0:T(8,128)S(1)}, f32[384,1536]{1,0:T(8,128)}, u32[]{:S(2)}) copy-start(f32[384,1536]{1,0:T(8,128)} %get-tuple-element.41) | copy-start | bytes 7077892

commit v2 on v1

--- a/solution.py
+++ b/solution.py
@@ -47,6 +47,17 @@
     return out
 
 
+def row(ref):
+    return ref[...].reshape(1, -1)
+
+
+def flat(ref):
+    heads, width = ref.shape
+    wide = jnp.concatenate([ref[...]] * heads, axis=1)
+    keep = iota(wide.shape, 0) == iota(wide.shape, 1) // width
+    return jnp.sum(jnp.where(keep, wide, 0.0), axis=0, keepdims=True)
+
+
 def gelu_parts(pre):
     t = jnp.tanh(GELU_C * (pre + GELU_A * pre * pre * pre))
     value = 0.5 * pre * (1.0 + t)
@@ -99,8 +110,8 @@
 
     @pl.when(pl.program_id(0) == 0)
     def _():
-        probe8 = jnp.broadcast_to(probe_ref[...].astype(BF16), (SUB, probe_ref.shape[1]))
-        q8 = (nt(probe8, wq_ref[...]) + bq_ref[...]).astype(BF16)
+        probe8 = jnp.broadcast_to(row(probe_ref), (SUB, probe_ref.shape[0])).astype(BF16)
+        q8 = (nt(probe8, wq_ref[...]) + flat(bq_ref)).astype(BF16)
         q_ref[...] = q8.astype(F32)
         qs = jnp.concatenate([q8.astype(F32)] * heads, axis=0)
         qs = jnp.where(iota(qs.shape, 0) // SUB == iota(qs.shape, 1) // width, qs, 0.0).astype(BF16)
@@ -114,7 +125,7 @@
 
     images, tokens = SUB, x_ref.shape[0] // SUB
     hat, _ = centre(x_ref[...].astype(F32))
-    hid = (hat * gain_ref[...] + bias_ref[...]).astype(BF16)
+    hid = (hat * row(gain_ref) + row(bias_ref)).astype(BF16)
     r = nt(hid, qkr[...])
     s = ((r + pltpu.roll(r, LANES // 2, 1)) * scale).reshape(images, tokens, LANES)
     m = jnp.max(s, axis=1)
@@ -129,7 +140,7 @@
     v = v[0:rows] + v[rows:2 * rows]
     cols = wq_ref.shape[0]
     vs = by_head([v[SUB * h:SUB * h + SUB] for h in range(heads)], width)
-    vs = vs + by_head([l[:, SUB * h:SUB * h + 1] for h in range(heads)], width) * bv_ref[...]
+    vs = vs + by_head([l[:, SUB * h:SUB * h + 1] for h in range(heads)], width) * flat(bv_ref)
     pk_ref[:, 0:cols] = vs
     pk_ref[:, cols:cols + LANES] = m
     pk_ref[:, cols + LANES:cols + 2 * LANES] = l
@@ -153,12 +164,12 @@
     )(x, gain, bias, probe, wq, bq, wk, wv, bv)
 
 
-def head_kernel(heads, nsp, ntp, pk_ref, wo_hbm, wu_hbm, wd_hbm, og_ref, bo_ref, hg_ref, hb_ref, bu_ref, bd_ref, bv_ref,
-                y_out, ga_out, pool_out, pb_out, st_out,
-                wo, wu, wd, rbuf, ta, tg, td, ag, wsem, rs_send, rs_recv, ta_s, ta_r, tg_s, tg_r, td_s, td_r, ag_s, ag_r):
+def head_kernel(heads, nsp, ntp, pk_ref, hb_hbm, wo_hbm, wu_hbm, wd_hbm, og_ref, bo_ref, hg_ref, hb_ref, bu_ref, bd_ref, bv_ref,
+                ga_out, st_out, own_out, hbar_out,
+                wo, wu, wd, rbuf, ta, tg, td, ag, hr, wsem, rs_send, rs_recv, ta_s, ta_r, tg_s, tg_r, td_s, td_r, ag_s, ag_r, hr_s, hr_r):
     sp, sp_peers = peers_of('sp', nsp)
     tp, tp_peers = peers_of('tp', ntp)
-    loads = [pltpu.make_async_copy(a, b, wsem.at[i]) for i, (a, b) in enumerate(((wd_hbm, wd), (wo_hbm, wo), (wu_hbm, wu)))]
+    loads = [pltpu.make_async_copy(a, b, wsem.at[i]) for i, (a, b) in enumerate(((wd_hbm, wd), (wo_hbm, wo), (wu_hbm, wu), (hb_hbm.at[sp], hr.at[sp])))]
     for load in loads:
         load.start()
     barrier_all([('sp', d) for d in sp_peers] + [('tp', d) for d in tp_peers])
@@ -166,6 +177,10 @@
     for k, dev in enumerate(sp_peers):
         sends.append(remote(pk_ref.at[dev], rbuf.at[sp], rs_send.at[k], rs_recv.at[sp], 'sp', dev))
         sends[-1].start()
+    late = []
+    for k, dev in enumerate(sp_peers):
+        late.append(remote(hb_hbm.at[dev], hr.at[sp], hr_s.at[k], hr_r.at[sp], 'sp', dev))
+        late[-1].start()
     rbuf[sp] = pk_ref[sp]
     hd = wo.shape[0]
     width = hd // heads
@@ -194,124 +209,162 @@
     gather_start(ta, tp, tp_peers, ta_s, ta_r, 'tp')
     loads[2].wait()
     gather_wait(ta, tp, tp_peers, ta_s, ta_r, 'tp')
-    attn = bo_ref[...] + ((ta[0] + ta[1]) + (ta[2] + ta[3])) if ntp == 4 else bo_ref[...] + sum(ta[t] for t in range(ntp))
+    attn = ta[0]
+    for t in range(1, ntp):
+        attn = attn + ta[t]
+    attn = attn + row(bo_ref)
     hat, inv = centre(attn)
-    y = (hat * hg_ref[...] + hb_ref[...]).astype(BF16)
-    value, slope = gelu_parts(nn(y, wu[...]) + bu_ref[...])
-    hidden = value.astype(BF16)
+    gain = row(hg_ref)
+    y = (hat * gain + row(hb_ref)).astype(BF16)
+    value, slope = gelu_parts(nn(y, wu[...]) + row(bu_ref))
     tg[tp] = nt((gh * slope).astype(BF16), wu[...])
     gather_start(tg, tp, tp_peers, tg_s, tg_r, 'tp')
-    td[tp] = nn(hidden, wd[...])
+    td[tp] = nn(value.astype(BF16), wd[...])
     gather_start(td, tp, tp_peers, td_s, td_r, 'tp')
     gather_wait(tg, tp, tp_peers, tg_s, tg_r, 'tp')
     gno = tg[0]
     for t in range(1, ntp):
         gno = gno + tg[t]
-    ga = (og.astype(F32) + norm_back(hat, inv, gno * hg_ref[...])).astype(BF16)
+    ga = (og.astype(F32) + norm_back(hat, inv, gno * gain)).astype(BF16)
     gp = nt(ga, wo[...]).astype(BF16).astype(F32)
-    prod = gp * (o - bv_ref[...])
+    prod = gp * (o - flat(bv_ref))
     head_of = iota(prod.shape, 1) // width
     delta = by_head([jnp.sum(jnp.where(head_of == h, prod, 0.0), axis=1, keepdims=True) for h in range(heads)], SUB)
+    ag[sp, :, 0:model] = ga.astype(F32)
+    ag[sp, :, model:model + LANES] = lse
+    ag[sp, :, model + LANES:model + 2 * LANES] = jnp.concatenate([delta, jnp.zeros((SUB, LANES - heads * SUB), F32)], axis=1)
+    gather_start(ag, sp, sp_peers, ag_s, ag_r, 'sp')
     gather_wait(td, tp, tp_peers, td_s, td_r, 'tp')
     down = td[0]
     for t in range(1, ntp):
         down = down + td[t]
-    ag[sp, :, 0:model] = y.astype(F32)
-    ag[sp, :, model:2 * model] = ga.astype(F32)
-    ag[sp, :, 2 * model:3 * model] = (attn + down + bd_ref[...]).astype(BF16).astype(F32)
-    base = 3 * model
-    ag[sp, :, base:base + hd] = pooled_bf.astype(F32)
-    ag[sp, :, base + hd:base + hd + LANES] = lse
-    ag[sp, :, base + hd + LANES:base + hd + 2 * LANES] = jnp.concatenate([delta, jnp.zeros((SUB, LANES - heads * SUB), F32)], axis=1)
-    gather_start(ag, sp, sp_peers, ag_s, ag_r, 'sp')
+    own_out[:, 0:model] = y.astype(F32)
+    own_out[:, model:2 * model] = (attn + down + row(bd_ref)).astype(BF16).astype(F32)
+    own_out[:, 2 * model:2 * model + hd] = pooled_bf.astype(F32)
+    loads[3].wait()
+    for k, dev in enumerate(sp_peers):
+        remote(hr.at[dev], hr.at[dev], hr_s.at[k], hr_r.at[dev], 'sp', dev).wait_recv()
+    for send in late:
+        send.wait_send()
+    hbar = jnp.zeros(hbar_out.shape, F32)
+    for j in range(nsp):
+        w = jnp.exp(rbuf[j, :, hd:hd + LANES] - lse)
+        hbar = hbar + hr[j] * jnp.concatenate([w[:, SUB * h:SUB * h + 1] for h in range(heads)], axis=0)
+    hbar_out[...] = hbar
     gather_wait(ag, sp, sp_peers, ag_s, ag_r, 'sp')
-    y_out[...] = ag[:, :, 0:model].astype(BF16)
-    ga_out[...] = ag[:, :, model:2 * model].astype(BF16)
-    pool_out[...] = ag[:, :, 2 * model:3 * model].astype(BF16)
-    pb_out[...] = ag[:, :, base:base + hd].astype(BF16)
-    st_out[...] = ag[:, :, base + hd:base + hd + 2 * LANES]
-
-
-def head(heads, nsp, ntp, pk, wo, wu, wd, og, bo, hg, hb, bu, bd, bv):
-    images, model = og.shape
+    ga_out[...] = ag[:, :, 0:model].astype(BF16)
+    st_out[...] = ag[:, :, model:model + 2 * LANES]
+
+
+def head(heads, nsp, ntp, pk, hb, wo, wu, wd, og3, vectors):
+    own, model = og3.shape[1:]
     hd = wo.shape[0]
-    own = images // nsp
     pk3 = pk.reshape(nsp, own, pk.shape[1])
-    og3 = og.reshape(nsp, own, model)
     vm, hbm = pl.BlockSpec(memory_space=pltpu.VMEM), pl.BlockSpec(memory_space=pl.ANY)
     dma = pltpu.SemaphoreType.DMA
-    cols = 3 * model + hd + 2 * LANES
     part = pltpu.VMEM((ntp, own, model), F32)
-    shapes = [(model, BF16), (model, BF16), (model, BF16), (hd, BF16), (2 * LANES, F32)]
     return pl.pallas_call(
         functools.partial(head_kernel, heads, nsp, ntp),
-        in_specs=[vm, hbm, hbm, hbm] + [vm] * 7,
-        out_specs=[vm] * 5,
-        out_shape=[jax.ShapeDtypeStruct((nsp, own, c), d) for c, d in shapes],
-        scratch_shapes=[pltpu.VMEM(wo.shape, BF16), pltpu.VMEM(wu.shape, BF16), pltpu.VMEM(wd.shape, BF16), pltpu.VMEM(pk3.shape, F32), part, part, part, pltpu.VMEM((nsp, own, cols), F32),
-                        dma((3,)), dma((nsp - 1,)), dma((nsp,)), dma((ntp - 1,)), dma((ntp,)), dma((ntp - 1,)), dma((ntp,)), dma((ntp - 1,)), dma((ntp,)), dma((nsp - 1,)), dma((nsp,))],
+        in_specs=[vm, hbm, hbm, hbm, hbm] + [vm] * 7,
+        out_specs=[vm] * 4,
+        out_shape=[jax.ShapeDtypeStruct((nsp, own, model), BF16), jax.ShapeDtypeStruct((nsp, own, 2 * LANES), F32), jax.ShapeDtypeStruct((own, 2 * model + hd), F32), jax.ShapeDtypeStruct(hb.shape[1:], F32)],
+        scratch_shapes=[pltpu.VMEM(wo.shape, BF16), pltpu.VMEM(wu.shape, BF16), pltpu.VMEM(wd.shape, BF16), pltpu.VMEM(pk3.shape, F32), part, part, part, pltpu.VMEM((nsp, own, model + 2 * LANES), F32), pltpu.VMEM(hb.shape, F32),
+                        dma((4,)), dma((nsp - 1,)), dma((nsp,)), dma((ntp - 1,)), dma((ntp,)), dma((ntp - 1,)), dma((ntp,)), dma((ntp - 1,)), dma((ntp,)), dma((nsp - 1,)), dma((nsp,)), dma((nsp - 1,)), dma((nsp,))],
         compiler_params=pltpu.CompilerParams(collective_id=0, has_side_effects=True),
         name='head',
-    )(pk3, wo, wu, wd, og3, bo, hg, hb, bu, bd, bv)
-
-
-def spread_kernel(heads, nsp, ntp, ga_ref, wo_ref, wv_ref, hb_ref, pk_ref, st_ref, qk_ref,
-                  gv_out, hbar_out, st_out, qk_out,
-                  hs, hr, ha, gv_s, gv_r, fw_s, fw_r, hs_s, hs_r, ha_s, ha_r, st_s, st_r, qk_s, qk_r):
+    )(pk3, hb, wo, wu, wd, og3, *vectors)
+
+
+def chip_start(buf, sp, mate, sames, send_sems, recv_sems):
+    for k, dev in enumerate([mate] + sames):
+        remote(buf.at[sp], buf.at[sp], send_sems.at[k], recv_sems.at[sp], 'sp', dev).start()
+
+
+def chip_forward(buf, sp, mate, sames, send_sems, recv_sems):
+    for k, dev in enumerate(sames):
+        remote(buf.at[dev], buf.at[dev], send_sems.at[k + 1], recv_sems.at[dev], 'sp', dev).wait_recv()
+        remote(buf.at[dev], buf.at[dev], send_sems.at[len(sames) + 1 + k], recv_sems.at[dev], 'sp', mate).start()
+
+
+def chip_finish(buf, sp, mate, sames, others, send_sems, recv_sems):
+    for dev in [mate] + others:
+        remote(buf.at[dev], buf.at[dev], send_sems.at[0], recv_sems.at[dev], 'sp', mate).wait_recv()
+    for k, dev in enumerate([mate] + sames):
+        remote(buf.at[sp], buf.at[sp], send_sems.at[k], recv_sems.at[sp], 'sp', dev).wait_send()
+    for k, dev in enumerate(sames):
+        remote(buf.at[dev], buf.at[dev], send_sems.at[len(sames) + 1 + k], recv_sems.at[dev], 'sp', mate).wait_send()
+
+
+def spread_kernel(heads, nsp, ntp, ga_ref, wo_ref, wv_ref, own_ref, hbar_ref, st_ref, qk_ref, og_ref, bu_ref, wu_hbm, wd_hbm,
+                  gv_out, hbar_out, st_out, qk_out, gp_out, y_out, pool_out, pb_out, hid_out, gpre_out,
+                  wu, wd, pa, ha, wsem, gv_s, gv_r, fw_s, fw_r, pa_s, pa_r, ha_s, ha_r, st_s, st_r, qk_s, qk_r):
     sp, sp_peers = peers_of('sp', nsp)
     tp, tp_peers = peers_of('tp', ntp)
     core = lax.rem(sp, 2)
     mate = sp + 1 - 2 * core
+    sames = [lax.rem(sp + 2 * k, nsp) for k in range(1, nsp // 2)]
+    others = [lax.rem(mate + 2 * k, nsp) for k in range(1, nsp // 2)]
     half = nsp // 2
     hd = wo_ref.shape[0]
     width = hd // heads
     model = wo_ref.shape[1]
-    rows = heads * SUB
+    images = nsp * SUB
+    loads = [pltpu.make_async_copy(a, b, wsem.at[i]) for i, (a, b) in enumerate(((wd_hbm, wd), (wu_hbm, wu)))]
+    for load in loads:
+        load.start()
+    sem = pltpu.get_barrier_semaphore()
+    for axis, devs in (('sp', sp_peers), ('tp', tp_peers)):
+        for dev in devs:
+            pl.semaphore_signal(sem, inc=1, device_id={axis: dev}, device_id_type=MESH)
+    pa[sp] = own_ref[...]
+    ha[sp] = hbar_ref[...]
+    st_out[tp] = st_ref[...]
+    qk_out[tp] = qk_ref[...]
+    gp_all = nt(ga_ref[...].reshape(images, model), wo_ref[...]).astype(BF16)
+    gp_out[...] = gp_all.reshape(nsp, SUB, hd)
 
     def make_gv(i, _):
         g = lax.rem(core * half + i, nsp)
-        gp = nt(ga_ref[g], wo_ref[...]).astype(BF16).astype(F32)
+        gp = gp_out[g].astype(F32)
         gp = jnp.concatenate([gp] * heads, axis=0)
         gp = jnp.where(iota(gp.shape, 0) // SUB == iota(gp.shape, 1) // width, gp, 0.0).astype(BF16)
         gv_out[tp, g] = nn(gp, wv_ref[...])
         return 0
 
     lax.fori_loop(0, half, make_gv, 0)
-
-    def make_hs(g, _):
-        w = jnp.exp(pk_ref[g, :, hd:hd + LANES] - st_ref[g, :, 0:LANES])
-        col = jnp.concatenate([w[:, SUB * h:SUB * h + 1] for h in range(heads)], axis=0)
-        hs[g] = hb_ref[g] * col
-        return 0
-
-    lax.fori_loop(0, nsp, make_hs, 0)
-    st_out[tp] = st_ref[...]
-    qk_out[tp] = qk_ref[...]
-    barrier_all([('sp', d) for d in sp_peers] + [('tp', d) for d in tp_peers])
+    pl.semaphore_wait(sem, len(sp_peers) + len(tp_peers))
     for i in range(half):
         g = core * half + i
         for k, dev in enumerate(tp_peers):
             remote(gv_out.at[tp, g], gv_out.at[tp, g], gv_s.at[k, i], gv_r.at[tp, i], 'tp', dev).start()
-    for k, dev in enumerate(sp_peers):
-        remote(hs.at[dev], hr.at[sp], hs_s.at[k], hs_r.at[sp], 'sp', dev).start()
-    gather_start(st_out, tp, tp_peers, st_s, st_r, 'tp')
-    gather_start(qk_out, tp, tp_peers, qk_s, qk_r, 'tp')
+        if i == 0:
+            gather_start(st_out, tp, tp_peers, st_s, st_r, 'tp')
+            gather_start(qk_out, tp, tp_peers, qk_s, qk_r, 'tp')
+    chip_start(pa, sp, mate, sames, pa_s, pa_r)
+    chip_start(ha, sp, mate, sames, ha_s, ha_r)
     lax.fori_loop(half, nsp, make_gv, 0)
-    for k, dev in enumerate(sp_peers):
-        remote(hr.at[dev], hr.at[dev], hs_s.at[k], hs_r.at[dev], 'sp', dev).wait_recv()
-    for k, dev in enumerate(sp_peers):
-        remote(hs.at[dev], hr.at[sp], hs_s.at[k], hs_r.at[sp], 'sp', dev).wait_send()
-    hr[sp] = hs[sp]
-    total = hr[0]
-    for j in range(1, nsp):
-        total = total + hr[j]
-    ha[sp] = total
-    gather_start(ha, sp, sp_peers, ha_s, ha_r, 'sp')
+    loads[0].wait()
+    og = og_ref[...].reshape(images, model)
+    gh = nt(og, wd[...])
+    chip_forward(pa, sp, mate, sames, pa_s, pa_r)
+    chip_finish(pa, sp, mate, sames, others, pa_s, pa_r)
+    y = pa[:, :, 0:model].astype(BF16)
+    y_out[...] = y
+    pool_out[...] = pa[:, :, model:2 * model].astype(BF16)
+    pb_out[...] = pa[:, :, 2 * model:2 * model + hd].astype(BF16)
+    loads[1].wait()
+    value, slope = gelu_parts(nn(y.reshape(images, model), wu[...]) + row(bu_ref))
+    hid_out[...] = value.astype(BF16)
+    gpre_out[...] = (gh * slope).astype(BF16)
     for i in range(half):
         g = core * half + i
         for k, dev in enumerate(tp_peers):
             remote(gv_out.at[dev, g], gv_out.at[dev, g], gv_s.at[k, i], gv_r.at[dev, i], 'tp', dev).wait_recv()
             remote(gv_out.at[dev, g], gv_out.at[dev, g], fw_s.at[k, i], fw_r.at[dev, i], 'sp', mate).start()
+        if i == 1:
+            chip_forward(ha, sp, mate, sames, ha_s, ha_r)
+    chip_finish(ha, sp, mate, sames, others, ha_s, ha_r)
+    hbar_out[...] = ha[...].astype(BF16)
     for i in range(half):
         g = core * half + i
         other = (1 - core) * half + i
@@ -321,26 +374,50 @@
             remote(gv_out.at[dev, other], gv_out.at[dev, other], fw_s.at[k, i], fw_r.at[dev, i], 'sp', mate).wait_recv()
     gather_wait(st_out, tp, tp_peers, st_s, st_r, 'tp')
     gather_wait(qk_out, tp, tp_peers, qk_s, qk_r, 'tp')
-    gather_wait(ha, sp, sp_peers, ha_s, ha_r, 'sp')
-    hbar_out[...] = ha[...].astype(BF16)
-
-
-def spread(heads, nsp, ntp, ga3, wo, wv, hb, pk, st, qk):
-    groups, rows, model = hb.shape
-    vm = pl.BlockSpec(memory_space=pltpu.VMEM)
+
+
+def spread(heads, nsp, ntp, ga3, wo, wv, own, hbar, st, qk, og3, bu, wu, wd):
+    rows, model = hbar.shape
+    hd = wo.shape[0]
+    images = nsp * SUB
+    vm, hbm = pl.BlockSpec(memory_space=pltpu.VMEM), pl.BlockSpec(memory_space=pl.ANY)
     dma = pltpu.SemaphoreType.DMA
     half = nsp // 2
-    pk3 = pk.reshape(nsp, -1, pk.shape[1])
-    slots = pltpu.VMEM((nsp, rows, model), F32)
+    sds = jax.ShapeDtypeStruct
+    chip = 2 * half
     return pl.pallas_call(
         functools.partial(spread_kernel, heads, nsp, ntp),
-        in_specs=[vm] * 7,
-        out_specs=[vm] * 4,
-        out_shape=[jax.ShapeDtypeStruct((ntp, nsp, rows, model), F32), jax.ShapeDtypeStruct((nsp, rows, model), BF16), jax.ShapeDtypeStruct((ntp,) + st.shape, F32), jax.ShapeDtypeStruct((ntp,) + qk.shape, F32)],
-        scratch_shapes=[slots, slots, slots, dma((ntp - 1, half)), dma((ntp, half)), dma((ntp - 1, half)), dma((ntp, half)), dma((nsp - 1,)), dma((nsp,)), dma((nsp - 1,)), dma((nsp,)), dma((ntp - 1,)), dma((ntp,)), dma((ntp - 1,)), dma((ntp,))],
+        in_specs=[vm] * 9 + [hbm] * 2,
+        out_specs=[vm] * 10,
+        out_shape=[sds((ntp, nsp, rows, model), F32), sds((nsp, rows, model), BF16), sds((ntp,) + st.shape, F32), sds((ntp,) + qk.shape, F32), sds((nsp, SUB, hd), BF16),
+                   sds((nsp, SUB, model), BF16), sds((nsp, SUB, model), BF16), sds((nsp, SUB, hd), BF16), sds((images, model), BF16), sds((images, model), BF16)],
+        scratch_shapes=[pltpu.VMEM(wu.shape, BF16), pltpu.VMEM(wd.shape, BF16), pltpu.VMEM((nsp,) + own.shape, F32), pltpu.VMEM((nsp, rows, model), F32), dma((2,)),
+                        dma((ntp - 1, half)), dma((ntp, half)), dma((ntp - 1, half)), dma((ntp, half)), dma((chip,)), dma((nsp,)), dma((chip,)), dma((nsp,)), dma((ntp - 1,)), dma((ntp,)), dma((ntp - 1,)), dma((ntp,))],
         compiler_params=pltpu.CompilerParams(collective_id=1, has_side_effects=True),
         name='spread',
-    )(ga3, wo, wv, hb, pk3, st, qk)
+    )(ga3, wo, wv, own, hbar, st, qk, og3, bu, wu, wd)
+
+
+def products_kernel(y_ref, gpre_ref, hid_ref, og_ref, gup_ref, gdown_ref):
+    gup_ref[...] = tn(y_ref[...], gpre_ref[...])
+    gdown_ref[...] = tn(hid_ref[...], og_ref[...])
+
+
+def products(y, gpre, hid, og):
+    images, model = y.shape
+    cols = gpre.shape[1]
+    tile = 2 * LANES
+    part = pl.BlockSpec((images, tile), lambda i: (0, i))
+    whole = pl.BlockSpec((images, cols), lambda i: (0, 0))
+    out = pl.BlockSpec((tile, cols), lambda i: (i, 0))
+    return pl.pallas_call(
+        products_kernel,
+        grid=(model // tile,),
+        in_specs=[part, whole, part, whole],
+        out_specs=[out, out],
+        out_shape=[jax.ShapeDtypeStruct((model, cols), F32), jax.ShapeDtypeStruct((cols, model), F32)],
+        name='products',
+    )(y, gpre, hid, og)
 
 
 def back_kernel(heads, ntp, scale, x_ref, gain_ref, bias_ref, gv_ref, qk_ref, st_ref, gx_ref, u_ref, qkr, uacc):
@@ -360,8 +437,8 @@
 
     images, tokens = SUB, x_ref.shape[0] // SUB
     hat, inv = centre(x_ref[...].astype(F32))
-    gain = gain_ref[...]
-    hid = (hat * gain + bias_ref[...]).astype(BF16)
+    gain = row(gain_ref)
+    hid = (hat * gain + row(bias_ref)).astype(BF16)
     qkb = qkr[...].astype(BF16)
     gv_hi, gv_lo = hi_lo(gv_ref[...].reshape(ntp * rows, model))
     r = nt(hid, qkb)
@@ -404,52 +481,63 @@
     )(x, gain, bias, gv, qk, st)
 
 
-def query_kernel(heads, nsp, ntp, u_ref, q_ref, probe_ref, wq_ref, wk_ref, gwq_out, gwk_out, gpr_out, ub, pb, u_s, u_r, p_s, p_r):
+def query_kernel(heads, nsp, ntp, u_ref, wq_ref, wk_ref, u_out, gq_out, gpr_out, ub, pb, u_s, u_r, p_s, p_r):
     sp, sp_peers = peers_of('sp', nsp)
-    tp, tp_peers = peers_of('tp', ntp)
+    tp = lax.axis_index('tp')
+    hd = wk_ref.shape[0]
+    width = hd // heads
+    everyone = [(lax.rem(tp + a, ntp), lax.rem(sp + b, nsp)) for a in range(ntp) for b in range(nsp) if a or b]
+    sem = pltpu.get_barrier_semaphore()
+    for t, j in everyone:
+        pl.semaphore_signal(sem, inc=1, device_id={'tp': t, 'sp': j}, device_id_type=MESH)
     ub[sp] = u_ref[...]
-    barrier_all([('sp', d) for d in sp_peers] + [('tp', d) for d in tp_peers])
+
+    def query_grad(u):
+        hi, lo = hi_lo(u)
+        g = nt(jnp.concatenate([hi, lo], axis=0), wk_ref[...])
+        g = g[0:heads] + g[heads:2 * heads]
+        return jnp.sum(jnp.where(iota(g.shape, 0) == iota(g.shape, 1) // width, g, 0.0), axis=0, keepdims=True)
+
+    hi, lo = hi_lo(query_grad(u_ref[...]))
+    gpr = nn(jnp.concatenate([hi, lo], axis=0), wq_ref[...])
+    mine = tp * nsp + sp
+    pb[mine] = gpr[0:1] + gpr[1:2]
+    pl.semaphore_wait(sem, len(everyone))
     gather_start(ub, sp, sp_peers, u_s, u_r, 'sp')
+    sends = []
+    for k, (t, j) in enumerate(everyone):
+        sends.append(pltpu.make_async_remote_copy(src_ref=pb.at[mine], dst_ref=pb.at[mine], send_sem=p_s.at[k], recv_sem=p_r.at[mine], device_id={'tp': t, 'sp': j}, device_id_type=MESH))
+        sends[-1].start()
     gather_wait(ub, sp, sp_peers, u_s, u_r, 'sp')
     u = ub[0]
     for j in range(1, nsp):
         u = u + ub[j]
-    hd = wk_ref.shape[0]
-    width = hd // heads
-    hi, lo = hi_lo(u)
-    g = nt(jnp.concatenate([hi, lo], axis=0), wk_ref[...])
-    g = g[0:heads] + g[heads:2 * heads]
-    gq = jnp.sum(jnp.where(iota(g.shape, 0) == iota(g.shape, 1) // width, g, 0.0), axis=0, keepdims=True)
-    hi, lo = hi_lo(gq)
-    gpr = nn(jnp.concatenate([hi, lo], axis=0), wq_ref[...])
-    pb[tp] = gpr[0:1] + gpr[1:2]
-    gather_start(pb, tp, tp_peers, p_s, p_r, 'tp')
-    qcol = jnp.transpose(q_ref[...])[:, 0:1]
-    gcol = jnp.transpose(jnp.broadcast_to(gq, (SUB, hd)))[:, 0:1]
-    for h in range(heads):
-        at = slice(width * h, width * h + width)
-        gwk_out[at, :] = qcol[at, :] * u[h:h + 1, :]
-        gwq_out[at, :] = gcol[at, :] * probe_ref[...]
-    gather_wait(pb, tp, tp_peers, p_s, p_r, 'tp')
+    u_out[...] = u
+    gq_out[...] = query_grad(u)
+    for k, (t, j) in enumerate(everyone):
+        slot = t * nsp + j
+        pltpu.make_async_remote_copy(src_ref=pb.at[slot], dst_ref=pb.at[slot], send_sem=p_s.at[k], recv_sem=p_r.at[slot], device_id={'tp': t, 'sp': j}, device_id_type=MESH).wait_recv()
+    for send in sends:
+        send.wait_send()
     total = pb[0]
-    for t in range(1, ntp):
-        total = total + pb[t]
+    for j in range(1, ntp * nsp):
+        total = total + pb[j]
     gpr_out[...] = total
 
 
-def query_grads(heads, nsp, ntp, u, q, probe, wq, wk):
+def query_grads(heads, nsp, ntp, u, wq, wk):
     hd, model = wq.shape
     vm = pl.BlockSpec(memory_space=pltpu.VMEM)
     dma = pltpu.SemaphoreType.DMA
     return pl.pallas_call(
         functools.partial(query_kernel, heads, nsp, ntp),
-        in_specs=[vm] * 5,
+        in_specs=[vm] * 3,
         out_specs=[vm] * 3,
-        out_shape=[jax.ShapeDtypeStruct((hd, model), F32), jax.ShapeDtypeStruct((hd, model), F32), jax.ShapeDtypeStruct((1, model), F32)],
-        scratch_shapes=[pltpu.VMEM((nsp, heads, model), F32), pltpu.VMEM((ntp, 1, model), F32), dma((nsp - 1,)), dma((nsp,)), dma((ntp - 1,)), dma((ntp,))],
+        out_shape=[jax.ShapeDtypeStruct((heads, model), F32), jax.ShapeDtypeStruct((1, hd), F32), jax.ShapeDtypeStruct((1, model), F32)],
+        scratch_shapes=[pltpu.VMEM((nsp, heads, model), F32), pltpu.VMEM((ntp * nsp, 1, model), F32), dma((nsp - 1,)), dma((nsp,)), dma((ntp * nsp - 1,)), dma((ntp * nsp,))],
         compiler_params=pltpu.CompilerParams(collective_id=2, has_side_effects=True),
         name='query_grads',
-    )(u, q, probe, wq, wk)
+    )(u, wq, wk)
 
 
 def local_head(nsp, ntp, encoded, enc_gain, enc_bias, probe, w_query, b_query, w_key, w_value, b_value, w_out, b_out, head_gain, head_bias, w_up, b_up, w_down, b_down, out_grad):
@@ -460,27 +548,22 @@
     x = encoded.reshape(images * tokens, model)
     wq, wk, wv = (jnp.transpose(w, (1, 2, 0)).reshape(hd, model) for w in (w_query, w_key, w_value))
     wo = w_out.reshape(hd, model)
-    row = lambda a: a.reshape(1, -1)
-    bv = row(b_value)
-    pk, hb, qk, q8 = scan_tokens(heads, images, scale, x, row(enc_gain), row(enc_bias), row(probe), wq, row(b_query), wk, wv, bv)
-    y3, ga3, pool3, pb3, st = head(heads, nsp, ntp, pk, wo, w_up, w_down, out_grad, row(b_out), row(head_gain), row(head_bias), row(b_up), row(b_down), bv)
-    gv, hbar, st_all, qk_all = spread(heads, nsp, ntp, ga3, wo, wv, hb, pk, st, qk)
-    gx, u = back_tokens(heads, ntp, scale, x, row(enc_gain), row(enc_bias), gv, qk_all, st_all)
-    gwq, gwk, gpr = query_grads(heads, nsp, ntp, u, q8, row(probe), wq, wk)
-
+    og3 = out_grad.reshape(nsp, images // nsp, model)
+    pk, hb, qk, q8 = scan_tokens(heads, images, scale, x, enc_gain, enc_bias, probe, wq, b_query, wk, wv, b_value)
+    ga3, st, own, hbar_own = head(heads, nsp, ntp, pk, hb, wo, w_up, w_down, og3, (b_out, head_gain, head_bias, b_up, b_down, b_value))
+    gv, hbar, st_all, qk_all, gp3, y3, pool3, pb3, hidden, grad_pre = spread(heads, nsp, ntp, ga3, wo, wv, own, hbar_own, st, qk, og3, b_up, w_up, w_down)
+    gx, u = back_tokens(heads, ntp, scale, x, enc_gain, enc_bias, gv, qk_all, st_all)
+    u, gq, gpr = query_grads(heads, nsp, ntp, u, wq, wk)
     y, ga, pooled_bf = (a.reshape(images, -1) for a in (y3, ga3, pb3))
-    pre = jnp.dot(y, w_up, preferred_element_type=F32) + b_up
-    value, slope = gelu_parts(pre)
-    grad_w_down = jnp.einsum('bf,bw->fw', value.astype(BF16), out_grad, preferred_element_type=F32)
-    grad_hidden = jnp.einsum('bw,fw->bf', out_grad, w_down, preferred_element_type=F32)
-    grad_w_up = jnp.einsum('bw,bf->wf', y, (grad_hidden * slope).astype(BF16), preferred_element_type=F32)
+    grad_w_up, grad_w_down = products(y, grad_pre, hidden, out_grad)
     grad_w_out = jnp.einsum('bk,bw->kw', pooled_bf, ga, preferred_element_type=F32).reshape(heads, head_dim, model)
-    grad_pooled = jnp.einsum('bw,kw->bk', ga, wo, preferred_element_type=F32).astype(BF16)
-    gp5 = grad_pooled.reshape(nsp, images // nsp, heads, head_dim)
+    gp4 = gp3.reshape(nsp, images // nsp, heads, head_dim)
     hbar4 = hbar.reshape(nsp, heads, images // nsp, model)
-    grad_wv = jnp.einsum('gihd,ghiw->hdw', gp5, hbar4, preferred_element_type=F32)
-    back = lambda a: jnp.transpose(a.reshape(heads, head_dim, model), (2, 0, 1))
-    return (pool3.reshape(images, model), gx.reshape(encoded.shape), gpr.reshape(model), back(gwq), back(gwk), back(grad_wv), grad_w_out, grad_w_up, grad_w_down)
+    grad_wv = jnp.einsum('gihd,ghiw->hdw', gp4, hbar4, preferred_element_type=F32)
+    grad_wk = q8[0].reshape(heads, head_dim, 1) * u[:, None, :]
+    grad_wq = gq.reshape(heads, head_dim, 1) * probe[None, None, :]
+    back = lambda a: jnp.transpose(a, (2, 0, 1))
+    return (pool3.reshape(images, model), gx.reshape(encoded.shape), gpr.reshape(model), back(grad_wq), back(grad_wk), back(grad_wv), grad_w_out, grad_w_up, grad_w_down)
 
 
 def solution(mesh):

time: 187 us -> 155 us (0.83)
  matrix products: 22.7 us -> 4.94 us
  local copies, waits for them, and re-layouts: 17.5 us -> 2.57 us
  other arithmetic: 1.31 us -> 4.67 us
  Pallas kernels: 144 us -> 141 us
    dot_general x5 -> x1, matrix products: 20.8 us -> 3.04 us  [local_head(): jnp.einsum('gihd,ghiw->hdw', gp4, hbar4, preferred_element_type=F32)]
    reshape x11 -> x1, local copies, waits for them, and re-layouts: 13.1 us -> 0.89 us  [local_head(): gp4 = gp3.reshape(nsp, images // nsp, heads, head_dim)]
    pallas_call x0 -> x1, Pallas kernels: none -> 8.17 us  [products(): pl.pallas_call(products_kernel, grid=(model // tile,), in_specs=[part, wh...]
    pallas_call x1, Pallas kernels: 43.4 us -> 35.4 us  [head(): pl.pallas_call(functools.partial(head_kernel, heads, nsp, ntp), in_specs=...]
    mul x0 -> x1, other arithmetic: none -> 3.36 us  [local_head(): grad_wk = q8[0].reshape(heads, head_dim, 1) * u[:, None, :]]
    unnamed x21 -> x11, local copies, waits for them, and re-layouts: 3.52 us -> 0.7 us
    pallas_call x1, Pallas kernels: 52.8 us -> 50 us  [spread(): pl.pallas_call(functools.partial(spread_kernel, heads, nsp, ntp), in_spec...]
where the time goes in v2:
time: 155 us; the launch traced here: 154 us
  Pallas kernels  141 us (91%)
  matrix products  4.94 us (3%)
  other arithmetic  4.67 us (3%)
  local copies, waits for them, and re-layouts  2.57 us (2%)
    pallas_call x1, Pallas kernels, spread(): pl.pallas_call(functools.partial(spread_kernel, heads, nsp, ntp), in_spec...  50 us
    pallas_call x1, Pallas kernels, head(): pl.pallas_call(functools.partial(head_kernel, heads, nsp, ntp), in_specs=...  35.4 us
    pallas_call x1, Pallas kernels, scan_tokens(): pl.pallas_call(functools.partial(scan_kernel, heads, scale), grid=(groups...  18.2 us
    pallas_call x1, Pallas kernels, back_tokens(): pl.pallas_call(functools.partial(back_kernel, heads, ntp, scale), grid=(g...  15.8 us
    pallas_call x1, Pallas kernels, query_grads(): pl.pallas_call(functools.partial(query_kernel, heads, nsp, ntp), in_specs...  13.6 us
    pallas_call x1, Pallas kernels, products(): pl.pallas_call(products_kernel, grid=(model // tile,), in_specs=[part, wh...  8.17 us
    mul x1, other arithmetic, local_head(): grad_wk = q8[0].reshape(heads, head_dim, 1) * u[:, None, :]  3.36 us

profile of v2, /device:TPU:97, one launch (start us, length us, event | category | flops | bytes accessed | tf_op | source)
XLA Modules:
  0.0 154.0 jit_solution(17569781588140321350)
XLA Ops:
  0.6 18.2 %scan_tokens.1 = (f32[64,640]{1,0:T(8,128)}, f32[8,32,1536]{2,1,0:T(8,128)}, f32[4,1536]{1,0:T(4,128)}, f32[8,384]{1,0:T(8,128)}) custom-call(bf16[2048,1536]{1,0:T(8,128)(2,1)} %bitcast.36, f32[1536]{0:T(1024)} %gain_ref.3, f32[1536]{0:T(1024)} %bias_ref.3, f32[1536]{0:T(1024)} %probe_ref.1, bf16[384,1536]{1,0:T(8,128)(2,1)} %bitcast.42, f32[4,96]{1,0:T(4,128)} %bq_ref.1, ...), custom_call_target="tpu_custom_call" | custom-call | flops 2415919104 | bytes 6291456 | tf_op jit(solution)/shard_map/scan_tokens/pallas_call | solution.py:155
  18.8 35.4 %head.1 = (bf16[8,8,1536]{2,1,0:T(8,128)(2,1)}, f32[8,8,256]{2,1,0:T(8,128)}, f32[8,3456]{1,0:T(8,128)}, f32[32,1536]{1,0:T(8,128)}) custom-call(f32[8,8,640]{2,1,0:T(8,128)} %bitcast.50, f32[8,32,1536]{2,1,0:T(8,128)} %get-tuple-element.35.hb_hbm, bf16[384,1536]{1,0:T(8,128)(2,1)} %bitcast.38, bf16[1536,1536]{1,0:T(8,128)(2,1)} %wu_hbm.3, ...), custom_call_target="tpu_custom_call" | custom-call | tf_op jit(solution)/shard_map/head/pallas_call | solution.py:266
  54.2 50.0 %spread.1 = (f32[4,8,32,1536]{3,2,1,0:T(8,128)}, bf16[8,32,1536]{2,1,0:T(8,128)(2,1)}, f32[4,8,8,256]{3,2,1,0:T(8,128)}, f32[4,4,1536]{2,1,0:T(4,128)}, bf16[8,8...) custom-call(bf16[8,8,1536]{2,1,0:T(8,128)(2,1)} %get-tuple-element.3, ...), custom_call_target="tpu_custom_call" | custom-call | tf_op jit(solution)/shard_map/spread/pallas_call | solution.py:388
  104.2 8.2 %products.1 = (f32[1536,1536]{1,0:T(8,128)}, f32[1536,1536]{1,0:T(8,128)}) custom-call(bf16[64,1536]{1,0:T(8,128)(2,1)} %bitcast.49, bf16[64,1536]{1,0:T(8,128)(2,1)} %get-tuple-element.55.gpre_ref, bf16[64,1536]{1,0:T(8,128)(2,1)} %get-tuple-element.56.hid_ref, bf16[64,1536]{1,0:T(8,128)(2,1)} %og_ref.1), custom_call_target="tpu_custom_call" | custom-call | tf_op jit(solution)/shard_map/products/pallas_call | solution.py:413
  112.4 0.9 reshape.80
  113.3 3.0 %convolution_bitcast_fusion = f32[1536,4,96]{0,2,1:T(8,128)} fusion(bf16[8,8,4,96]{3,2,1,0:T(4,128)(2,1)S(1)} %reshape.80, bf16[8,32,1536]{2,1,0:T(8,128)(2,1)} %get-tuple-element.52), kind=kOutput, calls=%fused_computation | convolution fusion | flops 75497472 | bytes 3194880 | tf_op jit(solution)/shard_map/gihd,ghiw->hdw/dot_general | solution.py:562
  116.3 15.8 %back_tokens.1 = (bf16[2048,1536]{1,0:T(8,128)(2,1)}, f32[4,1536]{1,0:T(4,128)}) custom-call(bf16[2048,1536]{1,0:T(8,128)(2,1)} %bitcast.37, f32[1536]{0:T(1024)} %gain_ref.3, f32[1536]{0:T(1024)} %bias_ref.3, f32[4,8,32,1536]{3,2,1,0:T(8,128)} %get-tuple-element.42.gv_ref, f32[4,4,1536]{2,1,0:T(4,128)} %get-tuple-element.43.qk_ref, ...), custom_call_target="tpu_custom_call" | custom-call | tf_op jit(solution)/shard_map/back_tokens/pallas_call | solution.py:473
  132.1 0.0 copy-start.3
  132.1 13.6 %query_grads.1 = (f32[4,1536]{1,0:T(4,128)}, f32[1,384]{1,0:T(1,128)}, f32[1,1536]{1,0:T(1,128)}) custom-call(f32[4,1536]{1,0:T(4,128)} %get-tuple-element.46.u_ref, bf16[384,1536]{1,0:T(8,128)(2,1)} %bitcast.43, bf16[384,1536]{1,0:T(8,128)(2,1)} %bitcast.45), custom_call_target="tpu_custom_call" | custom-call | tf_op jit(solution)/shard_map/query_grads/pallas_call | solution.py:532
  145.7 0.7 reduce.1
  146.4 0.1 mul.34
  146.5 0.7 slice_reduce_fusion
  147.2 0.1 mul.38
  147.3 0.0 copy-done.3
  147.3 0.0 copy-start.4
  147.3 0.0 copy-start.2
  147.3 0.0 copy-start
  147.3 3.4 %broadcast_multiply_fusion = (f32[1536,4,96]{0,2,1:T(8,128)}, f32[1536,4,96]{0,2,1:T(8,128)}) fusion(f32[1536,4]{0,1:T(4,128)} %bitcast.52, f32[4,96]{1,0:T(4,128)S(1)} %mul.38, f32[1536]{0:T(1024)S(1)} %copy-done.3, f32[4,96]{1,0:T(4,128)S(1)} %mul.34), kind=kLoop, calls=%fused_computation.1 | loop fusion | flops 1179648 | bytes 4752384 | tf_op jit(solution)/shard_map/mul | solution.py:563
  150.7 0.0 copy-start.1
  150.7 0.0 copy-done.4
  150.7 0.6 reduce
  151.3 0.0 copy-done.2
  151.3 0.1 dot_general.12
  151.4 0.0 copy-done
  151.4 1.9 %fusion.1 = f32[4,96,1536]{2,1,0:T(8,128)} fusion(bf16[8,8,1536]{2,1,0:T(8,128)(2,1)S(1)} %copy-done, bf16[4,96,64]{1,0,2:T(4,128)(2,1)S(1)} %dot_general.12), kind=kOutput, calls=%fused_computation.4 | convolution fusion | flops 75497472 | bytes 2605056 | tf_op jit(solution)/shard_map/bk,bw->kw/dot_general | solution.py:559
  153.3 0.0 copy-done.1
  153.3 0.7 copy.40
Async XLA Ops:
  132.1 15.2 %copy-start.3 = (f32[1536]{0:T(1024)S(1)}, f32[1536]{0:T(1024)}, u32[]{:S(2)}) copy-start(f32[1536]{0:T(1024)} %probe_ref.1) | copy-start | bytes 18436
  147.3 3.4 %copy-start.4 = (f32[1,1536]{1,0:T(1,128)S(1)}, f32[1,1536]{1,0:T(1,128)}, u32[]{:S(2)}) copy-start(f32[1,1536]{1,0:T(1,128)} %get-tuple-element.47) | copy-start | bytes 18436
  147.3 4.0 %copy-start.2 = (bf16[8,8,384]{2,1,0:T(8,128)(2,1)S(1)}, bf16[8,8,384]{2,1,0:T(8,128)(2,1)}, u32[]{:S(2)}) copy-start(bf16[8,8,384]{2,1,0:T(8,128)(2,1)} %get-tuple-element.53) | copy-start | bytes 147460
  147.3 4.1 %copy-start = (bf16[8,8,1536]{2,1,0:T(8,128)(2,1)S(1)}, bf16[8,8,1536]{2,1,0:T(8,128)(2,1)}, u32[]{:S(2)}) copy-start(bf16[8,8,1536]{2,1,0:T(8,128)(2,1)} %get-tuple-element.36.ga_ref) | copy-start | bytes 589828
  150.7 2.6 %copy-start.1 = (bf16[8,8,1536]{2,1,0:T(8,128)(2,1)S(1)}, bf16[8,8,1536]{2,1,0:T(8,128)(2,1)}, u32[]{:S(2)}) copy-start(bf16[8,8,1536]{2,1,0:T(8,128)(2,1)} %get-tuple-element.41) | copy-start | bytes 589828

commit v3 on v2

v3 whole, which is shorter than its diff:
```python
import functools
import jax
import jax.numpy as jnp
from jax import lax
from jax.experimental import pallas as pl
from jax.experimental.pallas import tpu as pltpu
from jax.sharding import PartitionSpec as P

NORM_EPS = 1e-6
MESH = pl.DeviceIdType.MESH
F32, BF16 = jnp.float32, jnp.bfloat16
IN_SPECS = (P('dp', 'sp', None), P(), P(), P(), P(None, 'tp', None), P('tp', None), P(None, 'tp', None), P(None, 'tp', None), P('tp', None), P('tp', None, None), P(), P(), P(), P(None, 'tp'), P('tp'), P('tp', None), P(), P('dp', None))
OUT_SPECS = (P('dp', None), P('dp', 'sp', None), P('dp'), P('dp', 'tp', None), P('dp', 'tp', None), P('dp', 'tp', None), P(('dp', 'tp'), None, None), P('dp', 'tp'), P(('dp', 'tp'), None))
LANES = 128
SUB = 8
GELU_C = 0.7978845608028654
GELU_A = 0.044715


def nn(a, b):
    return lax.dot_general(a, b, (((1,), (0,)), ((), ())), preferred_element_type=F32)


def nt(a, b):
    return lax.dot_general(a, b, (((1,), (1,)), ((), ())), preferred_element_type=F32)


def tn(a, b):
    return lax.dot_general(a, b, (((0,), (0,)), ((), ())), preferred_element_type=F32)


def hi_lo(a):
    hi = a.astype(BF16)
    return hi, (a - hi.astype(F32)).astype(BF16)


def iota(shape, dim):
    return lax.broadcasted_iota(jnp.int32, shape, dim)


def by_head(parts, width):
    rows, cols = parts[0].shape[0], len(parts) * width
    block = iota((rows, cols), 1) // width
    out = jnp.zeros((rows, cols), F32)
    for h, part in enumerate(parts):
        out = jnp.where(block == h, part, out)
    return out


def row(ref):
    return ref[...].reshape(1, -1)


def flat(ref):
    heads, width = ref.shape
    wide = jnp.concatenate([ref[...]] * heads, axis=1)
    keep = iota(wide.shape, 0) == iota(wide.shape, 1) // width
    return jnp.sum(jnp.where(keep, wide, 0.0), axis=0, keepdims=True)


def gelu_parts(pre):
    t = jnp.tanh(GELU_C * (pre + GELU_A * pre * pre * pre))
    value = 0.5 * pre * (1.0 + t)
    slope = 0.5 * (1.0 + t) + 0.5 * pre * (1.0 - t * t) * (GELU_C * (1.0 + 3.0 * GELU_A * pre * pre))
    return value, slope


def centre(rows):
    mean = jnp.mean(rows, axis=-1, keepdims=True)
    centred = rows - mean
    inv = lax.rsqrt(jnp.mean(centred * centred, axis=-1, keepdims=True) + NORM_EPS)
    return centred * inv, inv


def norm_back(hat, inv, cot):
    return inv * (cot - jnp.mean(cot, axis=-1, keepdims=True) - hat * jnp.mean(cot * hat, axis=-1, keepdims=True))


def barrier_all(peers):
    sem = pltpu.get_barrier_semaphore()
    for axis, dev in peers:
        pl.semaphore_signal(sem, inc=1, device_id={axis: dev}, device_id_type=MESH)
    pl.semaphore_wait(sem, len(peers))


def peers_of(axis, n):
    me = lax.axis_index(axis)
    return me, [lax.rem(me + k, n) for k in range(1, n)]


def remote(src, dst, send_sem, recv_sem, axis, dev):
    return pltpu.make_async_remote_copy(src_ref=src, dst_ref=dst, send_sem=send_sem, recv_sem=recv_sem, device_id={axis: dev}, device_id_type=MESH)


def gather_start(buf, me, peers, send_sems, recv_sems, axis):
    for k, dev in enumerate(peers):
        remote(buf.at[me], buf.at[me], send_sems.at[k], recv_sems.at[me], axis, dev).start()


def gather_wait(buf, me, peers, send_sems, recv_sems, axis):
    for k, dev in enumerate(peers):
        remote(buf.at[dev], buf.at[dev], send_sems.at[k], recv_sems.at[dev], axis, dev).wait_recv()
    for k, dev in enumerate(peers):
        remote(buf.at[me], buf.at[me], send_sems.at[k], recv_sems.at[me], axis, dev).wait_send()


class ChipRing:
    def __init__(self, nsp):
        me = lax.axis_index('sp')
        self.me, self.core = me, lax.rem(me, 2)
        self.mate = me + 1 - 2 * self.core
        self.up, self.down, self.far = (lax.rem(me + k, nsp) for k in (2, nsp - 2, 4))
        self.mates = [lax.rem(self.mate + k, nsp) for k in (2, nsp - 2, 4)]
        self.around = [self.mate, self.up, self.down, self.far] + self.mates

    def start(self, buf, send, recv):
        for k, dev in enumerate((self.mate, self.up, self.down)):
            remote(buf.at[self.me], buf.at[self.me], send.at[k], recv.at[self.me], 'sp', dev).start()

    def relay(self, buf, send, recv, upward):
        for k, dev in ((3, self.down), (4, self.up)):
            remote(buf.at[dev], buf.at[dev], send.at[k], recv.at[dev], 'sp', dev).wait_recv()
            if upward == (k == 3):
                remote(buf.at[dev], buf.at[dev], send.at[5], recv.at[dev], 'sp', self.up if upward else self.down).start()
            remote(buf.at[dev], buf.at[dev], send.at[k], recv.at[dev], 'sp', self.mate).start()

    def finish(self, buf, send, recv, upward):
        far = self.far
        remote(buf.at[far], buf.at[far], send.at[6], recv.at[far], 'sp', self.mate).wait_recv()
        remote(buf.at[far], buf.at[far], send.at[6], recv.at[far], 'sp', self.mate).start()
        for dev in [self.mate] + self.mates:
            remote(buf.at[dev], buf.at[dev], send.at[0], recv.at[dev], 'sp', self.mate).wait_recv()
        via = self.down if upward else self.up
        for k, slot in ((0, self.me), (1, self.me), (2, self.me), (3, self.down), (4, self.up), (5, via), (6, far)):
            remote(buf.at[slot], buf.at[slot], send.at[k], recv.at[slot], 'sp', self.mate).wait_send()


RING_SEMS = 7


def scan_kernel(heads, scale, x_ref, gain_ref, bias_ref, probe_ref, wq_ref, bq_ref, wk_ref, wv_ref, bv_ref, pk_ref, hb_ref, qk_ref, q_ref, qkr, hball):
    rows = heads * SUB
    width = wq_ref.shape[0] // heads

    @pl.when(pl.program_id(0) == 0)
    def _():
        probe8 = jnp.broadcast_to(row(probe_ref), (SUB, probe_ref.shape[0])).astype(BF16)
        q8 = (nt(probe8, wq_ref[...]) + flat(bq_ref)).astype(BF16)
        q_ref[...] = q8.astype(F32)
        qs = jnp.concatenate([q8.astype(F32)] * heads, axis=0)
        qs = jnp.where(iota(qs.shape, 0) // SUB == iota(qs.shape, 1) // width, qs, 0.0).astype(BF16)
        qk = nn(qs, wk_ref[...])
        hi, lo = hi_lo(qk)
        qkr[...] = jnp.zeros(qkr.shape, BF16)
        qkr[0:rows, :] = hi
        qkr[LANES // 2:LANES // 2 + rows, :] = lo
        for h in range(heads):
            qk_ref[h:h + 1, :] = qk[SUB * h:SUB * h + 1, :]

    step = pl.program_id(0)
    images, tokens = SUB, x_ref.shape[0] // SUB
    hat, _ = centre(x_ref[...].astype(F32))
    hid = (hat * row(gain_ref) + row(bias_ref)).astype(BF16)
    r = nt(hid, qkr[...])
    s = ((r + pltpu.roll(r, LANES // 2, 1)) * scale).reshape(images, tokens, LANES)
    m = jnp.max(s, axis=1)
    e = jnp.exp(s - m[:, None, :])
    l = jnp.sum(e, axis=1)
    lane, img = iota(e.shape, 2), iota(e.shape, 0)
    ebd = jnp.where((lane % SUB == img) & (lane < rows), e, 0.0).astype(BF16).reshape(images * tokens, LANES)
    hb = tn(ebd, hid)[0:rows, :]
    hb_ref[0, :, :] = hb
    hball[step] = hb
    cols = wq_ref.shape[0]
    mine = pl.ds(pl.multiple_of(step * SUB, SUB), SUB)
    pk_ref[mine, cols:cols + LANES] = m
    pk_ref[mine, cols + LANES:cols + 2 * LANES] = l

    @pl.when(step == pl.num_programs(0) - 1)
    def _():
        groups = hball.shape[0]
        every = groups * rows
        hi, lo = hi_lo(hball[...].reshape(every, hball.shape[2]))
        v = nt(hi, wv_ref[...]) + nt(lo, wv_ref[...])
        bias = flat(bv_ref)
        for g in range(groups):
            vs = by_head([v[g * rows + SUB * h:g * rows + SUB * h + SUB] for h in range(heads)], width)
            tot = pk_ref[g * SUB:g * SUB + SUB, cols + LANES:cols + 2 * LANES]
            pk_ref[g * SUB:g * SUB + SUB, 0:cols] = vs + by_head([tot[:, SUB * h:SUB * h + 1] for h in range(heads)], width) * bias


def scan_tokens(heads, images, scale, x, gain, bias, probe, wq, bq, wk, wv, bv):
    tokens_all, width = x.shape
    hd = wq.shape[0]
    groups = images // SUB
    block = tokens_all // groups
    full = lambda a: pl.BlockSpec(a.shape, lambda g: (0,) * a.ndim)
    return pl.pallas_call(
        functools.partial(scan_kernel, heads, scale),
        grid=(groups,),
        in_specs=[pl.BlockSpec((block, width), lambda g: (g, 0))] + [full(a) for a in (gain, bias, probe, wq, bq, wk, wv, bv)],
        out_specs=[pl.BlockSpec((images, hd + 2 * LANES), lambda g: (0, 0)), pl.BlockSpec((1, heads * SUB, width), lambda g: (g, 0, 0)), pl.BlockSpec((heads, width), lambda g: (0, 0)), pl.BlockSpec((SUB, hd), lambda g: (0, 0))],
        out_shape=[jax.ShapeDtypeStruct((images, hd + 2 * LANES), F32), jax.ShapeDtypeStruct((groups, heads * SUB, width), F32), jax.ShapeDtypeStruct((heads, width), F32), jax.ShapeDtypeStruct((SUB, hd), F32)],
        scratch_shapes=[pltpu.VMEM((LANES, width), BF16), pltpu.VMEM((groups, heads * SUB, width), F32)],
        name='scan_tokens',
    )(x, gain, bias, probe, wq, bq, wk, wv, bv)


def middle_kernel(heads, nsp, ntp, scale, pk_ref, og_ref, qk_ref, bo_ref, hg_ref, hb_ref, bu_ref, bd_ref, bv_ref, eg_ref, eb_ref, hb_hbm, x_hbm, wo_hbm, wu_hbm, wd_hbm, wv_hbm, wk_hbm, wq_hbm,
                  gv_out, hbar_out, st_out, qk_out, gp_out, y_out, ga_out, pool_out, pb_out, hid_out, gpre_out, u_out, gq_out, gpr_out,
                  wo, wu, wd, wv, wk, wq, rbuf, ta, tg, td, ag, hr, relay, pa, ha, xb, rhs, uacc, ub, prb, ghb,
                  wsem, xsem, rs_send, rs_recv, ta_s, ta_r, tg_s, tg_r, td_s, td_r, ag_s, ag_r, hr_s, hr_r, rl_r, gv_s, gv_r, fw_s, fw_r, pa_s, pa_r, ha_s, ha_r, st_s, st_r, qk_s, qk_r, ub_s, ub_r, pr_s, pr_r):
    sp, sp_peers = peers_of('sp', nsp)
    tp, tp_peers = peers_of('tp', ntp)
    ring = ChipRing(nsp)
    core, mate = ring.core, ring.mate
    loads = [pltpu.make_async_copy(a, b, wsem.at[i]) for i, (a, b) in enumerate(((wd_hbm, wd), (wo_hbm, wo), (wu_hbm, wu), (hb_hbm.at[sp], hr.at[sp]), (wv_hbm, wv), (wk_hbm, wk), (wq_hbm, wq)))]
    for load in loads:
        load.start()
    sem = pltpu.get_barrier_semaphore()
    for axis, devs in (('sp', sp_peers), ('tp', tp_peers)):
        for dev in devs:
            pl.semaphore_signal(sem, inc=1, device_id={axis: dev}, device_id_type=MESH)

    def x_load(g):
        return pltpu.make_async_copy(x_hbm.at[g], xb.at[g % 2], xsem.at[g % 2])

    x_load(0).start()
    x_load(1).start()
    hd = wo.shape[0]
    width = hd // heads
    model = wu.shape[0]
    rows = heads * SUB
    images = nsp * SUB
    qk_out[tp] = qk_ref[...]
    rbuf[sp] = pk_ref[sp]
    for h in range(heads):
        hi, lo = hi_lo(jnp.broadcast_to(qk_ref[h:h + 1, :], (SUB, model)))
        rhs[h * SUB:h * SUB + SUB, :] = hi.astype(F32)
        rhs[2 * rows + h * SUB:2 * rows + h * SUB + SUB, :] = lo.astype(F32)
    og = og_ref[sp]
    pl.semaphore_wait(sem, len(sp_peers) + len(tp_peers))

    sends = []
    for k, dev in enumerate(sp_peers):
        sends.append(remote(pk_ref.at[dev], rbuf.at[sp], rs_send.at[k], rs_recv.at[sp], 'sp', dev))
        sends[-1].start()
    far0, far1 = ring.far - core, ring.far - core + 1
    late = [remote(hb_hbm.at[far0], relay.at[0], hr_s.at[0], rl_r.at[0], 'sp', ring.up), remote(hb_hbm.at[far1], relay.at[1], hr_s.at[1], rl_r.at[1], 'sp', ring.down)]
    for k, dev in enumerate((ring.up, ring.down, ring.mates[0], ring.mates[1], mate)):
        late.append(remote(hb_hbm.at[dev], hr.at[sp], hr_s.at[2 + k], hr_r.at[sp], 'sp', dev))
    for send in late:
        send.start()
    gather_start(qk_out, tp, tp_peers, qk_s, qk_r, 'tp')
    loads[0].wait()
    gh = nt(og, wd[...])
    for k, dev in enumerate(sp_peers):
        remote(rbuf.at[dev], rbuf.at[dev], rs_send.at[k], rs_recv.at[dev], 'sp', dev).wait_recv()
    for send in sends:
        send.wait_send()
    m = rbuf[0, :, hd:hd + LANES]
    for j in range(1, nsp):
        m = jnp.maximum(m, rbuf[j, :, hd:hd + LANES])
    l = jnp.zeros_like(m)
    v = jnp.zeros((SUB, hd), F32)
    for j in range(nsp):
        w = jnp.exp(rbuf[j, :, hd:hd + LANES] - m)
        l = l + w * rbuf[j, :, hd + LANES:hd + 2 * LANES]
        v = v + by_head([w[:, SUB * h:SUB * h + 1] for h in range(heads)], width) * rbuf[j, :, 0:hd]
    o = v / by_head([l[:, SUB * h:SUB * h + 1] for h in range(heads)], width)
    pooled_bf = o.astype(BF16)
    lse = m + jnp.log(l)

    loads[1].wait()
    ta[tp] = nn(pooled_bf, wo[...])
    gather_start(ta, tp, tp_peers, ta_s, ta_r, 'tp')
    for k, (src, dst) in enumerate(((ring.down, ring.up - core), (ring.up, ring.down - core + 1))):
        remote(relay.at[k], relay.at[k], hr_s.at[k], rl_r.at[k], 'sp', src).wait_recv()
        late.append(remote(relay.at[k], hr.at[src], hr_s.at[7 + k], hr_r.at[src], 'sp', dst))
        late[-1].start()
    loads[2].wait()
    gather_wait(ta, tp, tp_peers, ta_s, ta_r, 'tp')
    attn = ta[0]
    for t in range(1, ntp):
        attn = attn + ta[t]
    attn = attn + row(bo_ref)
    hat, inv = centre(attn)
    gain = row(hg_ref)
    y = (hat * gain + row(hb_ref)).astype(BF16)
    value, slope = gelu_parts(nn(y, wu[...]) + row(bu_ref))
    tg[tp] = nt((gh * slope).astype(BF16), wu[...])
    gather_start(tg, tp, tp_peers, tg_s, tg_r, 'tp')
    td[tp] = nn(value.astype(BF16), wd[...])
    gather_start(td, tp, tp_peers, td_s, td_r, 'tp')
    gather_wait(tg, tp, tp_peers, tg_s, tg_r, 'tp')
    gno = tg[0]
    for t in range(1, ntp):
        gno = gno + tg[t]
    ga = (og.astype(F32) + norm_back(hat, inv, gno * gain)).astype(BF16)
    gp = nt(ga, wo[...]).astype(BF16).astype(F32)
    prod = gp * (o - flat(bv_ref))
    head_of = iota(prod.shape, 1) // width
    delta = by_head([jnp.sum(jnp.where(head_of == h, prod, 0.0), axis=1, keepdims=True) for h in range(heads)], SUB)
    ag[sp, :, 0:model] = ga.astype(F32)
    ag[sp, :, model:model + LANES] = jnp.concatenate([lse[:, 0:rows], delta, jnp.zeros((SUB, LANES - 2 * rows), F32)], axis=1)
    ring.start(ag, ag_s, ag_r)

    gather_wait(td, tp, tp_peers, td_s, td_r, 'tp')
    down = td[0]
    for t in range(1, ntp):
        down = down + td[t]
    pa[sp, :, 0:model] = y.astype(F32)
    pa[sp, :, model:2 * model] = (attn + down + row(bd_ref)).astype(BF16).astype(F32)
    pa[sp, :, 2 * model:2 * model + hd] = pooled_bf.astype(F32)
    ring.start(pa, pa_s, pa_r)
    ring.relay(ag, ag_s, ag_r, True)
    loads[3].wait()
    for k, dev in enumerate(sp_peers):
        remote(hr.at[dev], hr.at[dev], hr_s.at[k], hr_r.at[dev], 'sp', dev).wait_recv()
    for send in late:
        send.wait_send()
    hbar = jnp.zeros(hr.shape[1:], F32)
    for j in range(nsp):
        w = jnp.exp(rbuf[j, :, hd:hd + LANES] - lse)
        hbar = hbar + hr[j] * jnp.concatenate([w[:, SUB * h:SUB * h + 1] for h in range(heads)], axis=0)
    ha[sp] = hbar
    ring.start(ha, ha_s, ha_r)
    loads[4].wait()
    ring.finish(ag, ag_s, ag_r, True)

    ga_out[...] = ag[:, :, 0:model].astype(BF16)
    st_out[tp] = ag[:, :, model:model + LANES]
    near_up, near_down, far_tp = lax.rem(tp + 1, ntp), lax.rem(tp + ntp - 1, ntp), lax.rem(tp + 2, ntp)
    half = nsp // 2
    gp_all = nt(ga_out[...].reshape(images, model), wo[...]).astype(BF16)
    gp_out[...] = gp_all.reshape(nsp, SUB, hd)

    def make_gv(i):
        g = lax.rem(core * half + i, nsp)
        part = gp_out[g].astype(F32)
        part = jnp.concatenate([part] * heads, axis=0)
        part = jnp.where(iota(part.shape, 0) // SUB == iota(part.shape, 1) // width, part, 0.0).astype(BF16)
        gv_out[tp, g] = nn(part, wv[...])

    def piece(i, owner):
        return gv_out.at[owner, core * half + i]

    def send_gv(i, k, owner, dev):
        return remote(piece(i, owner), piece(i, owner), gv_s.at[k, i], gv_r.at[owner, i], 'tp', dev)

    def forward(i, k, owner):
        return remote(piece(i, owner), piece(i, owner), fw_s.at[k, i], fw_r.at[owner, i], 'sp', mate)

    def near(i):
        for k, owner in ((0, near_down), (1, near_up)):
            send_gv(i, k, owner, owner).wait_recv()
            if k == i % 2:
                send_gv(i, 2, owner, near_down if k else near_up).start()
            forward(i, k, owner).start()

    def beyond(i):
        send_gv(i, 2, far_tp, far_tp).wait_recv()
        forward(i, 2, far_tp).start()

    for i in range(half):
        make_gv(i)
        send_gv(i, 0, tp, near_up).start()
        send_gv(i, 1, tp, near_down).start()
        if i == 0:
            gather_start(st_out, tp, tp_peers, st_s, st_r, 'tp')

    def rest_gv(i, _):
        make_gv(i)
        return 0

    lax.fori_loop(half, nsp, rest_gv, 0)

    uacc[...] = jnp.zeros(uacc.shape, F32)

    def u_step(g):
        x_load(g).wait()
        tokens = xb.shape[1] // SUB
        xhat, _ = centre(xb[g % 2].astype(F32))
        if g + 2 < nsp:
            x_load(g + 2).start()
        hidden = (xhat * row(eg_ref) + row(eb_ref)).astype(BF16)
        hi, lo = hi_lo(gv_out[tp, g])
        rhs[rows:2 * rows, :] = hi.astype(F32)
        rhs[3 * rows:4 * rows, :] = lo.astype(F32)
        r = nt(hidden, rhs[...].astype(BF16))
        r = (r + pltpu.roll(r, LANES // 2, 1)).reshape(SUB, tokens, LANES)
        lane, img = iota(r.shape, 2), iota(r.shape, 0)
        r = r * jnp.where(lane < rows, scale, 1.0) - ag[g, :, model:model + LANES][:, None, :]
        r = r.reshape(SUB * tokens, LANES)
        grad = (jnp.exp(r) * pltpu.roll(r, LANES - rows, 1) * scale).reshape(SUB, tokens, LANES)
        ds = jnp.where((lane % SUB == img) & (lane < rows), grad, 0.0).astype(BF16).reshape(SUB * tokens, LANES)
        uacc[...] += tn(ds, hidden)[0:rows, :]

    u_step(0)
    u_step(1)
    ring.relay(pa, pa_s, pa_r, True)
    near(0)
    u_step(2)
    ring.finish(pa, pa_s, pa_r, True)
    ring.relay(ha, ha_s, ha_r, False)
    u_step(3)
    near(1)
    beyond(0)
    u_step(4)
    u_step(5)
    near(2)
    beyond(1)
    ring.finish(ha, ha_s, ha_r, False)
    u_step(6)
    u_step(7)
    for h in range(heads):
        ub[sp, h:h + 1, :] = jnp.sum(uacc[SUB * h:SUB * h + SUB, :], axis=0, keepdims=True)
    gather_start(ub, sp, sp_peers, ub_s, ub_r, 'sp')

    y_all = pa[:, :, 0:model].astype(BF16)
    y_out[...] = y_all
    pool_out[...] = pa[:, :, model:2 * model].astype(BF16)
    pb_out[...] = pa[:, :, 2 * model:2 * model + hd].astype(BF16)
    hbar_out[...] = ha[...].astype(BF16)
    near(3)
    beyond(2)
    ghb[...] = nt(og_ref[...].reshape(images, model), wd[...])
    value, slope = gelu_parts(nn(y_all.reshape(images, model), wu[...]) + row(bu_ref))
    gpre_out[...] = (ghb[...] * slope).astype(BF16)
    hid_out[...] = value.astype(BF16)

    gather_wait(ub, sp, sp_peers, ub_s, ub_r, 'sp')
    u = ub[0]
    for j in range(1, nsp):
        u = u + ub[j]
    u_out[...] = u
    loads[5].wait()
    loads[6].wait()
    hi, lo = hi_lo(u)
    gq = nt(jnp.concatenate([hi, lo], axis=0), wk[...])
    gq = gq[0:heads] + gq[heads:2 * heads]
    gq = jnp.sum(jnp.where(iota(gq.shape, 0) == iota(gq.shape, 1) // width, gq, 0.0), axis=0, keepdims=True)
    gq_out[...] = gq
    hi, lo = hi_lo(gq)
    gpr = nn(jnp.concatenate([hi, lo], axis=0), wq[...])
    prb[tp] = gpr[0:1] + gpr[1:2]
    gather_start(prb, tp, tp_peers, pr_s, pr_r, 'tp')
    beyond(3)
    for i in range(half):
        other = (1 - core) * half + i
        for k, (owner, dev) in enumerate(((tp, near_up), (tp, near_down), (near_up if i % 2 else near_down, near_down if i % 2 else near_up))):
            send_gv(i, k, owner, dev).wait_send()
        for k, owner in enumerate((near_down, near_up, far_tp)):
            forward(i, k, owner).wait_send()
            remote(gv_out.at[owner, other], gv_out.at[owner, other], fw_s.at[k, i], fw_r.at[owner, i], 'sp', mate).wait_recv()
    gather_wait(st_out, tp, tp_peers, st_s, st_r, 'tp')
    gather_wait(qk_out, tp, tp_peers, qk_s, qk_r, 'tp')
    gather_wait(prb, tp, tp_peers, pr_s, pr_r, 'tp')
    total = prb[0]
    for t in range(1, ntp):
        total = total + prb[t]
    gpr_out[...] = total


def middle(heads, nsp, ntp, scale, pk, og3, qk, vectors, hb, x3, wo, wu, wd, wv, wk, wq):
    own, model = og3.shape[1:]
    hd = wo.shape[0]
    rows = hb.shape[1]
    images = nsp * own
    half = nsp // 2
    pk3 = pk.reshape(nsp, own, pk.shape[1])
    vm, hbm = pl.BlockSpec(memory_space=pltpu.VMEM), pl.BlockSpec(memory_space=pl.ANY)
    dma = pltpu.SemaphoreType.DMA
    sds = jax.ShapeDtypeStruct
    part = pltpu.VMEM((ntp, own, model), F32)
    wide = [pltpu.VMEM(w.shape, BF16) for w in (wo, wu, wd, wv, wk, wq)]
    ring, tps, tpr = [dma((RING_SEMS,)), dma((nsp,))], dma((ntp - 1,)), dma((ntp,))
    return pl.pallas_call(
        functools.partial(middle_kernel, heads, nsp, ntp, scale),
        in_specs=[vm] * 11 + [hbm] * 8,
        out_specs=[vm] * 14,
        out_shape=[sds((ntp, nsp, rows, model), F32), sds((nsp, rows, model), BF16), sds((ntp, nsp, own, LANES), F32), sds((ntp,) + qk.shape, F32), sds((nsp, own, hd), BF16),
                   sds((nsp, own, model), BF16), sds((nsp, own, model), BF16), sds((nsp, own, model), BF16), sds((nsp, own, hd), BF16), sds((images, model), BF16), sds((images, model), BF16), sds(qk.shape, F32), sds((1, hd), F32), sds((1, model), F32)],
        scratch_shapes=wide + [pltpu.VMEM(pk3.shape, F32), part, part, part, pltpu.VMEM((nsp, own, model + LANES), F32), pltpu.VMEM(hb.shape, F32), pltpu.VMEM((2,) + hb.shape[1:], F32), pltpu.VMEM((nsp, own, 2 * model + hd), F32), pltpu.VMEM(hb.shape, F32),
                               pltpu.VMEM((2,) + x3.shape[1:], BF16), pltpu.VMEM((LANES, model), F32), pltpu.VMEM((rows, model), F32), pltpu.VMEM((nsp,) + qk.shape, F32), pltpu.VMEM((ntp, 1, model), F32), pltpu.VMEM((images, model), F32),
                               dma((7,)), dma((2,)), dma((nsp - 1,)), dma((nsp,)), tps, tpr, tps, tpr, tps, tpr] + ring + [dma((9,)), dma((nsp,)), dma((2,)), dma((3, half)), dma((ntp, half)), dma((3, half)), dma((ntp, half))] + ring + ring + [tps, tpr, tps, tpr, dma((nsp - 1,)), dma((nsp,)), tps, tpr],
        compiler_params=pltpu.CompilerParams(collective_id=0, has_side_effects=True),
        name='middle',
    )(pk3, og3, qk, *vectors, hb, x3, wo, wu, wd, wv, wk, wq)


def products_kernel(heads, parts, y_ref, gpre_ref, hid_ref, og_ref, pb_ref, ga_ref, gp_ref, hbar_ref, q_ref, u_ref, gq_ref, probe_ref, pool_ref, gpr_ref, gup_ref, gdown_ref, gwo_ref, gwv_ref, gwk_ref, gwq_ref, pool_out, gpr_out):
    step = pl.program_id(0)
    gup_ref[...] = tn(y_ref[...], gpre_ref[...])
    gdown_ref[...] = tn(hid_ref[...], og_ref[...])
    tile, model = gwo_ref.shape
    width = parts * tile // heads
    part = lax.rem(step, parts)
    groups = gp_ref.shape[0]

    @pl.when(step == 0)
    def _():
        pool_out[...] = pool_ref[...]
        gpr_out[...] = gpr_ref[...].reshape(gpr_out.shape)

    @pl.when(step < parts)
    def _():
        gwo_ref[...] = tn(pb_ref[...], ga_ref[...])
        gp = jnp.concatenate([gp_ref[g].astype(F32) for g in range(groups) for _ in range(heads)], axis=0)
        keep = (iota(gp.shape, 0) // SUB) % heads == (part * tile + iota(gp.shape, 1)) // width
        gwv_ref[...] = tn(jnp.where(keep, gp, 0.0).astype(BF16), hbar_ref[...].reshape(gp.shape[0], model))

    @pl.when(step >= parts)
    def _():
        q = jnp.transpose(q_ref[...])[:, 0:1]
        head_of = (part * tile + iota((tile, model), 0)) // width
        u = jnp.zeros((tile, model), F32)
        for h in range(heads):
            u = jnp.where(head_of == h, u_ref[h:h + 1, :], u)
        gwk_ref[...] = q * u
        gq = jnp.transpose(jnp.broadcast_to(gq_ref[...], (SUB, tile)))[:, 0:1]
        gwq_ref[...] = gq * row(probe_ref)


def products(heads, y, gpre, hid, og, pb, ga, gp3, hbar, q8, u, gq, probe, pool, gpr):
    images, model = y.shape
    cols, hd = gpre.shape[1], pb.shape[1]
    parts = hd // LANES
    steps = 2 * parts
    tile = model // steps
    at = lambda a: lambda i: jnp.clip(i - parts * a, 0, parts - 1)
    lane = lambda i: lax.rem(i, parts)
    part = pl.BlockSpec((images, tile), lambda i: (0, i))
    full = lambda a: pl.BlockSpec(a.shape, lambda i: (0,) * a.ndim)
    out = pl.BlockSpec((tile, cols), lambda i: (i, 0))
    small = [pl.BlockSpec((LANES, model), lambda i, f=at(a): (f(i), 0)) for a in (0, 0, 1, 1)]
    sds = jax.ShapeDtypeStruct
    return pl.pallas_call(
        functools.partial(products_kernel, heads, parts),
        grid=(steps,),
        in_specs=[part, full(gpre), part, full(og), pl.BlockSpec((images, LANES), lambda i: (0, lane(i))), full(ga), pl.BlockSpec(gp3.shape[:2] + (LANES,), lambda i: (0, 0, lane(i))), full(hbar), pl.BlockSpec((SUB, LANES), lambda i: (0, lane(i))), full(u), pl.BlockSpec((1, LANES), lambda i: (0, lane(i))), full(probe), full(pool), full(gpr)],
        out_specs=[out, out] + small + [full(pool), full(probe)],
        out_shape=[sds((model, cols), F32), sds((cols, model), F32)] + [sds((hd, model), F32)] * 4 + [sds(pool.shape, pool.dtype), sds(probe.shape, F32)],
        name='products',
    )(y, gpre, hid, og, pb, ga, gp3, hbar, q8, u, gq, probe, pool, gpr)


def back_kernel(heads, ntp, scale, x_ref, gain_ref, bias_ref, gv_ref, qk_ref, st_ref, gx_ref, qkr):
    step = pl.program_id(0)
    rows = heads * SUB
    model = x_ref.shape[1]

    @pl.when(step == 0)
    def _():
        for t in range(ntp):
            for h in range(heads):
                hi, lo = hi_lo(jnp.broadcast_to(qk_ref[t, h:h + 1, :], (SUB, model)))
                at = (t * heads + h) * SUB
                qkr[at:at + SUB, :] = hi.astype(F32)
                qkr[LANES + at:LANES + at + SUB, :] = lo.astype(F32)

    images, tokens = SUB, x_ref.shape[0] // SUB
    hat, inv = centre(x_ref[...].astype(F32))
    gain = row(gain_ref)
    hid = (hat * gain + row(bias_ref)).astype(BF16)
    qkb = qkr[...].astype(BF16)
    gv_hi, gv_lo = hi_lo(gv_ref[...].reshape(ntp * rows, model))
    r = nt(hid, qkb)
    s = (r[:, 0:LANES] + r[:, LANES:2 * LANES]) * scale
    d = nt(hid, jnp.concatenate([gv_hi, gv_lo], axis=0))
    d = d[:, 0:LANES] + d[:, LANES:2 * LANES]
    lse = jnp.concatenate([st_ref[t, 0, :, 0:rows] for t in range(ntp)], axis=1)
    delta = jnp.concatenate([st_ref[t, 0, :, rows:2 * rows] for t in range(ntp)], axis=1)
    shape = (images, tokens, LANES)
    keep = iota(shape, 2) % SUB == iota(shape, 0)
    p = jnp.where(keep, jnp.exp(s.reshape(shape) - lse[:, None, :]), 0.0)
    ds = p * (d.reshape(shape) - delta[:, None, :]) * scale
    pb = p.astype(BF16).reshape(images * tokens, LANES)
    db = ds.astype(BF16).reshape(images * tokens, LANES)
    gh = nn(jnp.concatenate([pb, db], axis=1), jnp.concatenate([gv_hi, qkb[0:LANES]], axis=0))
    gx_ref[...] = norm_back(hat, inv, gh * gain).astype(BF16)


def back_tokens(heads, ntp, scale, x, gain, bias, gv, qk, st):
    tokens_all, model = x.shape
    groups, rows = gv.shape[1], gv.shape[2]
    block = tokens_all // groups
    full = lambda a: pl.BlockSpec(a.shape, lambda g: (0,) * a.ndim)
    return pl.pallas_call(
        functools.partial(back_kernel, heads, ntp, scale),
        grid=(groups,),
        in_specs=[pl.BlockSpec((block, model), lambda g: (g, 0)), full(gain), full(bias), pl.BlockSpec((ntp, 1, rows, model), lambda g: (0, g, 0, 0)), full(qk), pl.BlockSpec((ntp, 1) + st.shape[2:], lambda g: (0, g, 0, 0))],
        out_specs=pl.BlockSpec((block, model), lambda g: (g, 0)),
        out_shape=jax.ShapeDtypeStruct((tokens_all, model), BF16),
        scratch_shapes=[pltpu.VMEM((2 * LANES, model), F32)],
        name='back_tokens',
    )(x, gain, bias, gv, qk, st)


def local_head(nsp, ntp, encoded, enc_gain, enc_bias, probe, w_query, b_query, w_key, w_value, b_value, w_out, b_out, head_gain, head_bias, w_up, b_up, w_down, b_down, out_grad):
    images, tokens, model = encoded.shape
    heads, head_dim = b_query.shape
    hd = heads * head_dim
    scale = head_dim ** -0.5
    x = encoded.reshape(images * tokens, model)
    wq, wk, wv = (jnp.transpose(w, (1, 2, 0)).reshape(hd, model) for w in (w_query, w_key, w_value))
    wo = w_out.reshape(hd, model)
    og3 = out_grad.reshape(nsp, images // nsp, model)
    pk, hb, qk, q8 = scan_tokens(heads, images, scale, x, enc_gain, enc_bias, probe, wq, b_query, wk, wv, b_value)
    gv, hbar, st, qk_all, gp3, y3, ga3, pool3, pb3, hidden, grad_pre, u, gq, gpr = middle(heads, nsp, ntp, scale, pk, og3, qk, (b_out, head_gain, head_bias, b_up, b_down, b_value, enc_gain, enc_bias), hb, x.reshape(nsp, -1, model), wo, w_up, w_down, wv, wk, wq)
    gx = back_tokens(heads, ntp, scale, x, enc_gain, enc_bias, gv, qk_all, st)
    y, ga, pool, pooled_bf = (a.reshape(images, -1) for a in (y3, ga3, pool3, pb3))
    grad_w_up, grad_w_down, *small, pooled, grad_probe = products(heads, y, grad_pre, hidden, out_grad, pooled_bf, ga, gp3, hbar, q8, u, gq, probe, pool, gpr)
    grad_w_out, grad_wv, grad_wk, grad_wq = (a.reshape(heads, head_dim, model) for a in small)
    back = lambda a: jnp.transpose(a, (2, 0, 1))
    return (pooled, gx.reshape(encoded.shape), grad_probe, back(grad_wq), back(grad_wk), back(grad_wv), grad_w_out, grad_w_up, grad_w_down)


def solution(mesh):
    body = functools.partial(local_head, mesh.shape['sp'], mesh.shape['tp'])
    return jax.shard_map(body, mesh=mesh, in_specs=IN_SPECS, out_specs=OUT_SPECS, check_vma=False)
```

time: 155 us -> 127 us (0.82)
  Pallas kernels: 141 us -> 126 us
  matrix products: 4.94 us -> 0 us
  other arithmetic: 4.67 us -> 0 us
  local copies, waits for them, and re-layouts: 2.57 us -> 0 us
    pallas_call x4 -> x2, Pallas kernels: 107 us -> 94.5 us  [the longest x1 81.8 us: middle(): pl.pallas_call(functools.partial(middle_kernel, heads, nsp, ntp, scale),...]
    dot_general x2 -> x0, matrix products: 4.94 us -> none  [the longest x1 3.04 us: local_head(): jnp.einsum('gihd,ghiw->hdw', gp4, hbar4, preferred_element_type=F32)]
    mul x1 -> x0, other arithmetic: 3.36 us -> none  [local_head(): grad_wk = q8[0].reshape(heads, head_dim, 1) * u[:, None, :]]
    pallas_call x1, Pallas kernels: 18.2 us -> 15.6 us  [scan_tokens(): pl.pallas_call(functools.partial(scan_kernel, heads, scale), grid=(groups...]
where the time goes in v3:
time: 127 us; the launch traced here: 126 us
  Pallas kernels  126 us (99%)
    pallas_call x1, Pallas kernels, middle(): pl.pallas_call(functools.partial(middle_kernel, heads, nsp, ntp, scale),...  81.8 us
    pallas_call x1, Pallas kernels, scan_tokens(): pl.pallas_call(functools.partial(scan_kernel, heads, scale), grid=(groups...  15.6 us
    pallas_call x1, Pallas kernels, back_tokens(): pl.pallas_call(functools.partial(back_kernel, heads, ntp, scale), grid=(g...  15.5 us
    pallas_call x1, Pallas kernels, products(): pl.pallas_call(functools.partial(products_kernel, heads, parts), grid=(st...  12.7 us

profile of v3, /device:TPU:97, one launch (start us, length us, event | category | flops | bytes accessed | tf_op | source)
XLA Modules:
  0.0 126.4 jit_solution(14643703709764693804)
XLA Ops:
  0.6 15.6 %scan_tokens.1 = (f32[64,640]{1,0:T(8,128)}, f32[8,32,1536]{2,1,0:T(8,128)}, f32[4,1536]{1,0:T(4,128)}, f32[8,384]{1,0:T(8,128)}) custom-call(bf16[2048,1536]{1,0:T(8,128)(2,1)} %bitcast.29, f32[1536]{0:T(1024)} %gain_ref.3, f32[1536]{0:T(1024)} %bias_ref.3, f32[1536]{0:T(1024)} %probe_ref.3, bf16[384,1536]{1,0:T(8,128)(2,1)} %bitcast.33, f32[4,96]{1,0:T(4,128)} %bq_ref.1, ...), custom_call_target="tpu_custom_call" | custom-call | tf_op jit(solution)/shard_map/scan_tokens/pallas_call | solution.py:198
  16.2 81.8 %middle.1 = (f32[4,8,32,1536]{3,2,1,0:T(8,128)}, bf16[8,32,1536]{2,1,0:T(8,128)(2,1)}, f32[4,8,8,128]{3,2,1,0:T(8,128)}, f32[4,4,1536]{2,1,0:T(4,128)}, bf16[8,8...) custom-call(f32[8,8,640]{2,1,0:T(8,128)} %bitcast.44, ...), custom_call_target="tpu_custom_call" | custom-call | tf_op jit(solution)/shard_map/middle/pallas_call | solution.py:478
  98.1 15.5 %back_tokens.1 = bf16[2048,1536]{1,0:T(8,128)(2,1)} custom-call(bf16[2048,1536]{1,0:T(8,128)(2,1)} %bitcast.31, f32[1536]{0:T(1024)} %gain_ref.3, f32[1536]{0:T(1024)} %bias_ref.3, f32[4,8,32,1536]{3,2,1,0:T(8,128)} %get-tuple-element.51.gv_ref, f32[4,4,1536]{2,1,0:T(4,128)} %get-tuple-element.52.qk_ref, f32[4,8,8,128]{3,2,1,0:T(8,128)} %get-tuple-element.53.st_ref), custom_call_target="tpu_custom_call" | custom-call | tf_op jit(solution)/shard_map/back_tokens/pallas_call | solution.py:589
  113.6 12.7 %products.1 = (f32[1536,1536]{1,0:T(8,128)}, f32[1536,1536]{1,0:T(8,128)}, f32[384,1536]{1,0:T(8,128)}, f32[384,1536]{1,0:T(8,128)}, f32[384,1536]{1,0:T(8,128)}...) custom-call(bf16[64,1536]{1,0:T(8,128)(2,1)} %bitcast.41, ...), custom_call_target="tpu_custom_call" | custom-call | tf_op jit(solution)/shard_map/products/pallas_call | solution.py:538

commit v4 on v3

--- a/solution.py
+++ b/solution.py
@@ -69,7 +69,7 @@
     mean = jnp.mean(rows, axis=-1, keepdims=True)
     centred = rows - mean
     inv = lax.rsqrt(jnp.mean(centred * centred, axis=-1, keepdims=True) + NORM_EPS)
-    return centred * inv, inv
+    return centred * inv, inv, mean
 
 
 def norm_back(hat, inv, cot):
@@ -138,7 +138,7 @@
 RING_SEMS = 7
 
 
-def scan_kernel(heads, scale, x_ref, gain_ref, bias_ref, probe_ref, wq_ref, bq_ref, wk_ref, wv_ref, bv_ref, pk_ref, hb_ref, qk_ref, q_ref, qkr, hball):
+def scan_kernel(heads, scale, x_ref, gain_ref, bias_ref, probe_ref, wq_ref, bq_ref, wk_ref, wv_ref, bv_ref, pk_ref, hb_ref, qk_ref, q_ref, h_ref, ms_ref, qkr, hball):
     rows = heads * SUB
     width = wq_ref.shape[0] // heads
 
@@ -159,8 +159,11 @@
 
     step = pl.program_id(0)
     images, tokens = SUB, x_ref.shape[0] // SUB
-    hat, _ = centre(x_ref[...].astype(F32))
+    hat, inv, mean = centre(x_ref[...].astype(F32))
     hid = (hat * row(gain_ref) + row(bias_ref)).astype(BF16)
+    h_ref[...] = hid
+    which = iota((x_ref.shape[0], LANES), 1)
+    ms_ref[...] = jnp.where(which == 0, mean, inv)
     r = nt(hid, qkr[...])
     s = ((r + pltpu.roll(r, LANES // 2, 1)) * scale).reshape(images, tokens, LANES)
     m = jnp.max(s, axis=1)
@@ -199,17 +202,17 @@
         functools.partial(scan_kernel, heads, scale),
         grid=(groups,),
         in_specs=[pl.BlockSpec((block, width), lambda g: (g, 0))] + [full(a) for a in (gain, bias, probe, wq, bq, wk, wv, bv)],
-        out_specs=[pl.BlockSpec((images, hd + 2 * LANES), lambda g: (0, 0)), pl.BlockSpec((1, heads * SUB, width), lambda g: (g, 0, 0)), pl.BlockSpec((heads, width), lambda g: (0, 0)), pl.BlockSpec((SUB, hd), lambda g: (0, 0))],
-        out_shape=[jax.ShapeDtypeStruct((images, hd + 2 * LANES), F32), jax.ShapeDtypeStruct((groups, heads * SUB, width), F32), jax.ShapeDtypeStruct((heads, width), F32), jax.ShapeDtypeStruct((SUB, hd), F32)],
+        out_specs=[pl.BlockSpec((images, hd + 2 * LANES), lambda g: (0, 0)), pl.BlockSpec((1, heads * SUB, width), lambda g: (g, 0, 0)), pl.BlockSpec((heads, width), lambda g: (0, 0)), pl.BlockSpec((SUB, hd), lambda g: (0, 0)), pl.BlockSpec((block, width), lambda g: (g, 0)), pl.BlockSpec((block, LANES), lambda g: (g, 0))],
+        out_shape=[jax.ShapeDtypeStruct((images, hd + 2 * LANES), F32), jax.ShapeDtypeStruct((groups, heads * SUB, width), F32), jax.ShapeDtypeStruct((heads, width), F32), jax.ShapeDtypeStruct((SUB, hd), F32), jax.ShapeDtypeStruct(x.shape, BF16), jax.ShapeDtypeStruct((tokens_all, LANES), F32)],
         scratch_shapes=[pltpu.VMEM((LANES, width), BF16), pltpu.VMEM((groups, heads * SUB, width), F32)],
         name='scan_tokens',
     )(x, gain, bias, probe, wq, bq, wk, wv, bv)
 
 
-def middle_kernel(heads, nsp, ntp, scale, pk_ref, og_ref, qk_ref, bo_ref, hg_ref, hb_ref, bu_ref, bd_ref, bv_ref, eg_ref, eb_ref, hb_hbm, x_hbm, wo_hbm, wu_hbm, wd_hbm, wv_hbm, wk_hbm, wq_hbm,
+def middle_kernel(heads, nsp, ntp, scale, pk_ref, og_ref, qk_ref, bo_ref, hg_ref, hb_ref, bu_ref, bd_ref, bv_ref, hb_hbm, x_hbm, wo_hbm, wu_hbm, wd_hbm, wv_hbm, wk_hbm, wq_hbm,
                   gv_out, hbar_out, st_out, qk_out, gp_out, y_out, ga_out, pool_out, pb_out, hid_out, gpre_out, u_out, gq_out, gpr_out,
-                  wo, wu, wd, wv, wk, wq, rbuf, ta, tg, td, ag, hr, relay, pa, ha, xb, rhs, uacc, ub, prb, ghb,
-                  wsem, xsem, rs_send, rs_recv, ta_s, ta_r, tg_s, tg_r, td_s, td_r, ag_s, ag_r, hr_s, hr_r, rl_r, gv_s, gv_r, fw_s, fw_r, pa_s, pa_r, ha_s, ha_r, st_s, st_r, qk_s, qk_r, ub_s, ub_r, pr_s, pr_r):
+                  wo, wu, wd, wv, wk, wq, rbuf, ta, tg, td, ag, hr, relay, pa, ha, sg, xb, rhs, uacc, ub, prb, ghb,
+                  wsem, xsem, rs_send, rs_recv, ta_s, ta_r, tg_s, tg_r, td_s, td_r, ag_s, ag_r, hr_s, hr_r, rl_r, gv_s, gv_r, fw_s, fw_r, pa_s, pa_r, ha_s, ha_r, st_s, st_r, qk_s, qk_r, ub_s, ub_r, pr_s, pr_r, sy_s, sy_r, sg_s, sg_r):
     sp, sp_peers = peers_of('sp', nsp)
     tp, tp_peers = peers_of('tp', ntp)
     ring = ChipRing(nsp)
@@ -284,7 +287,7 @@
     for t in range(1, ntp):
         attn = attn + ta[t]
     attn = attn + row(bo_ref)
-    hat, inv = centre(attn)
+    hat, inv, _ = centre(attn)
     gain = row(hg_ref)
     y = (hat * gain + row(hb_ref)).astype(BF16)
     value, slope = gelu_parts(nn(y, wu[...]) + row(bu_ref))
@@ -301,9 +304,9 @@
     prod = gp * (o - flat(bv_ref))
     head_of = iota(prod.shape, 1) // width
     delta = by_head([jnp.sum(jnp.where(head_of == h, prod, 0.0), axis=1, keepdims=True) for h in range(heads)], SUB)
-    ag[sp, :, 0:model] = ga.astype(F32)
-    ag[sp, :, model:model + LANES] = jnp.concatenate([lse[:, 0:rows], delta, jnp.zeros((SUB, LANES - 2 * rows), F32)], axis=1)
-    ring.start(ag, ag_s, ag_r)
+    ag[sp, :, 0:hd] = gp
+    ag[sp, :, hd:hd + LANES] = jnp.concatenate([lse[:, 0:rows], delta, jnp.zeros((SUB, LANES - 2 * rows), F32)], axis=1)
+    gather_start(ag, sp, sp_peers, ag_s, ag_r, 'sp')
 
     gather_wait(td, tp, tp_peers, td_s, td_r, 'tp')
     down = td[0]
@@ -311,9 +314,56 @@
         down = down + td[t]
     pa[sp, :, 0:model] = y.astype(F32)
     pa[sp, :, model:2 * model] = (attn + down + row(bd_ref)).astype(BF16).astype(F32)
-    pa[sp, :, 2 * model:2 * model + hd] = pooled_bf.astype(F32)
+    pa[sp, :, 2 * model:3 * model] = ga.astype(F32)
+    pa[sp, :, 3 * model:3 * model + hd] = pooled_bf.astype(F32)
+    gather_wait(ag, sp, sp_peers, ag_s, ag_r, 'sp')
     ring.start(pa, pa_s, pa_r)
-    ring.relay(ag, ag_s, ag_r, True)
+
+    loads[4].wait()
+    st_out[tp] = ag[:, :, hd:hd + LANES]
+    near_up, near_down, far_tp = lax.rem(tp + 1, ntp), lax.rem(tp + ntp - 1, ntp), lax.rem(tp + 2, ntp)
+    half = nsp // 2
+    direct = half - sg.shape[2]
+    gp_out[...] = ag[:, :, 0:hd].astype(BF16)
+
+    def make_gv(first):
+        part = jnp.concatenate([ag[first + i, :, 0:hd] for i in range(half) for _ in range(heads)], axis=0)
+        keep = (iota(part.shape, 0) // SUB) % heads == iota(part.shape, 1) // width
+        gv_out[tp, pl.ds(first, half)] = nn(jnp.where(keep, part, 0.0).astype(BF16), wv[...]).reshape(half, rows, model)
+
+    def piece(i, owner):
+        return gv_out.at[owner, core * half + i]
+
+    def send_gv(i, k, owner, dev):
+        return remote(piece(i, owner), piece(i, owner), gv_s.at[k, i], gv_r.at[owner, i], 'tp', dev)
+
+    def forward(i, k, owner):
+        return remote(piece(i, owner), piece(i, owner), fw_s.at[k, i], fw_r.at[owner, i], 'sp', mate)
+
+    def near(i):
+        for k, owner in ((0, near_down), (1, near_up)):
+            send_gv(i, k, owner, owner).wait_recv()
+            if k == i % 2:
+                send_gv(i, 2, owner, near_down if k else near_up).start()
+            forward(i, k, owner).start()
+
+    def beyond(i):
+        send_gv(i, 2, far_tp, far_tp).wait_recv()
+        forward(i, 2, far_tp).start()
+
+    def send_shared(k):
+        block = pl.ds(pl.multiple_of((sp // 2) * SUB, SUB), SUB)
+        return remote(gv_out.at[tp, pl.ds(core * half + direct, half - direct), block], sg.at[sp, ntp - 1 - k], sy_s.at[k - 1], sy_r.at[ntp - 1 - k], 'tp', lax.rem(tp + k, ntp))
+
+    make_gv(core * half)
+    for k in range(1, ntp):
+        send_shared(k).start()
+    for i in range(direct):
+        send_gv(i, 0, tp, near_up).start()
+        send_gv(i, 1, tp, near_down).start()
+        if i == 0:
+            gather_start(st_out, tp, tp_peers, st_s, st_r, 'tp')
+    make_gv((1 - core) * half)
     loads[3].wait()
     for k, dev in enumerate(sp_peers):
         remote(hr.at[dev], hr.at[dev], hr_s.at[k], hr_r.at[dev], 'sp', dev).wait_recv()
@@ -325,109 +375,58 @@
         hbar = hbar + hr[j] * jnp.concatenate([w[:, SUB * h:SUB * h + 1] for h in range(heads)], axis=0)
     ha[sp] = hbar
     ring.start(ha, ha_s, ha_r)
-    loads[4].wait()
-    ring.finish(ag, ag_s, ag_r, True)
-
-    ga_out[...] = ag[:, :, 0:model].astype(BF16)
-    st_out[tp] = ag[:, :, model:model + LANES]
-    near_up, near_down, far_tp = lax.rem(tp + 1, ntp), lax.rem(tp + ntp - 1, ntp), lax.rem(tp + 2, ntp)
-    half = nsp // 2
-    gp_all = nt(ga_out[...].reshape(images, model), wo[...]).astype(BF16)
-    gp_out[...] = gp_all.reshape(nsp, SUB, hd)
-
-    def make_gv(i):
-        g = lax.rem(core * half + i, nsp)
-        part = gp_out[g].astype(F32)
-        part = jnp.concatenate([part] * heads, axis=0)
-        part = jnp.where(iota(part.shape, 0) // SUB == iota(part.shape, 1) // width, part, 0.0).astype(BF16)
-        gv_out[tp, g] = nn(part, wv[...])
-
-    def piece(i, owner):
-        return gv_out.at[owner, core * half + i]
-
-    def send_gv(i, k, owner, dev):
-        return remote(piece(i, owner), piece(i, owner), gv_s.at[k, i], gv_r.at[owner, i], 'tp', dev)
-
-    def forward(i, k, owner):
-        return remote(piece(i, owner), piece(i, owner), fw_s.at[k, i], fw_r.at[owner, i], 'sp', mate)
-
-    def near(i):
-        for k, owner in ((0, near_down), (1, near_up)):
-            send_gv(i, k, owner, owner).wait_recv()
-            if k == i % 2:
-                send_gv(i, 2, owner, near_down if k else near_up).start()
-            forward(i, k, owner).start()
-
-    def beyond(i):
-        send_gv(i, 2, far_tp, far_tp).wait_recv()
-        forward(i, 2, far_tp).start()
-
-    for i in range(half):
-        make_gv(i)
-        send_gv(i, 0, tp, near_up).start()
-        send_gv(i, 1, tp, near_down).start()
-        if i == 0:
-            gather_start(st_out, tp, tp_peers, st_s, st_r, 'tp')
-
-    def rest_gv(i, _):
-        make_gv(i)
-        return 0
-
-    lax.fori_loop(half, nsp, rest_gv, 0)
 
     uacc[...] = jnp.zeros(uacc.shape, F32)
 
     def u_step(g):
         x_load(g).wait()
         tokens = xb.shape[1] // SUB
-        xhat, _ = centre(xb[g % 2].astype(F32))
-        if g + 2 < nsp:
-            x_load(g + 2).start()
-        hidden = (xhat * row(eg_ref) + row(eb_ref)).astype(BF16)
+        hidden = xb[g % 2]
         hi, lo = hi_lo(gv_out[tp, g])
         rhs[rows:2 * rows, :] = hi.astype(F32)
         rhs[3 * rows:4 * rows, :] = lo.astype(F32)
         r = nt(hidden, rhs[...].astype(BF16))
         r = (r + pltpu.roll(r, LANES // 2, 1)).reshape(SUB, tokens, LANES)
         lane, img = iota(r.shape, 2), iota(r.shape, 0)
-        r = r * jnp.where(lane < rows, scale, 1.0) - ag[g, :, model:model + LANES][:, None, :]
+        r = r * jnp.where(lane < rows, scale, 1.0) - ag[g, :, hd:hd + LANES][:, None, :]
         r = r.reshape(SUB * tokens, LANES)
         grad = (jnp.exp(r) * pltpu.roll(r, LANES - rows, 1) * scale).reshape(SUB, tokens, LANES)
         ds = jnp.where((lane % SUB == img) & (lane < rows), grad, 0.0).astype(BF16).reshape(SUB * tokens, LANES)
         uacc[...] += tn(ds, hidden)[0:rows, :]
+        if g + 2 < nsp:
+            x_load(g + 2).start()
 
     u_step(0)
     u_step(1)
-    ring.relay(pa, pa_s, pa_r, True)
+    u_step(2)
+    ring.relay(pa, pa_s, pa_r, False)
+    for k in range(1, ntp):
+        remote(sg.at[sp, k - 1], sg.at[sp, k - 1], sy_s.at[0], sy_r.at[k - 1], 'tp', near_up).wait_recv()
+    ring.start(sg, sg_s, sg_r)
+    u_step(3)
+    u_step(4)
     near(0)
-    u_step(2)
-    ring.finish(pa, pa_s, pa_r, True)
-    ring.relay(ha, ha_s, ha_r, False)
-    u_step(3)
-    near(1)
-    beyond(0)
-    u_step(4)
     u_step(5)
-    near(2)
-    beyond(1)
-    ring.finish(ha, ha_s, ha_r, False)
     u_step(6)
+    ring.finish(pa, pa_s, pa_r, False)
+    ring.relay(ha, ha_s, ha_r, True)
     u_step(7)
     for h in range(heads):
         ub[sp, h:h + 1, :] = jnp.sum(uacc[SUB * h:SUB * h + SUB, :], axis=0, keepdims=True)
     gather_start(ub, sp, sp_peers, ub_s, ub_r, 'sp')
 
+    near(1)
+    ghb[...] = nt(og_ref[...].reshape(images, model), wd[...])
     y_all = pa[:, :, 0:model].astype(BF16)
     y_out[...] = y_all
     pool_out[...] = pa[:, :, model:2 * model].astype(BF16)
-    pb_out[...] = pa[:, :, 2 * model:2 * model + hd].astype(BF16)
-    hbar_out[...] = ha[...].astype(BF16)
-    near(3)
-    beyond(2)
-    ghb[...] = nt(og_ref[...].reshape(images, model), wd[...])
+    ga_out[...] = pa[:, :, 2 * model:3 * model].astype(BF16)
+    pb_out[...] = pa[:, :, 3 * model:3 * model + hd].astype(BF16)
     value, slope = gelu_parts(nn(y_all.reshape(images, model), wu[...]) + row(bu_ref))
     gpre_out[...] = (ghb[...] * slope).astype(BF16)
     hid_out[...] = value.astype(BF16)
+    ring.relay(sg, sg_s, sg_r, False)
+    near(2)
 
     gather_wait(ub, sp, sp_peers, ub_s, ub_r, 'sp')
     u = ub[0]
@@ -445,8 +444,18 @@
     gpr = nn(jnp.concatenate([hi, lo], axis=0), wq[...])
     prb[tp] = gpr[0:1] + gpr[1:2]
     gather_start(prb, tp, tp_peers, pr_s, pr_r, 'tp')
-    beyond(3)
-    for i in range(half):
+    beyond(0)
+    ring.finish(ha, ha_s, ha_r, True)
+    hbar_out[...] = ha[...].astype(BF16)
+    beyond(1)
+    ring.finish(sg, sg_s, sg_r, False)
+    for j in range(nsp):
+        for k in range(1, ntp):
+            gv_out[lax.rem(tp + k, ntp), (j % 2) * half + direct:(j % 2) * half + half, (j // 2) * SUB:(j // 2) * SUB + SUB, :] = sg[j, k - 1]
+    beyond(2)
+    for k in range(1, ntp):
+        send_shared(k).wait_send()
+    for i in range(direct):
         other = (1 - core) * half + i
         for k, (owner, dev) in enumerate(((tp, near_up), (tp, near_down), (near_up if i % 2 else near_down, near_down if i % 2 else near_up))):
             send_gv(i, k, owner, dev).wait_send()
@@ -477,13 +486,13 @@
     ring, tps, tpr = [dma((RING_SEMS,)), dma((nsp,))], dma((ntp - 1,)), dma((ntp,))
     return pl.pallas_call(
         functools.partial(middle_kernel, heads, nsp, ntp, scale),
-        in_specs=[vm] * 11 + [hbm] * 8,
+        in_specs=[vm] * 9 + [hbm] * 8,
         out_specs=[vm] * 14,
         out_shape=[sds((ntp, nsp, rows, model), F32), sds((nsp, rows, model), BF16), sds((ntp, nsp, own, LANES), F32), sds((ntp,) + qk.shape, F32), sds((nsp, own, hd), BF16),
                    sds((nsp, own, model), BF16), sds((nsp, own, model), BF16), sds((nsp, own, model), BF16), sds((nsp, own, hd), BF16), sds((images, model), BF16), sds((images, model), BF16), sds(qk.shape, F32), sds((1, hd), F32), sds((1, model), F32)],
-        scratch_shapes=wide + [pltpu.VMEM(pk3.shape, F32), part, part, part, pltpu.VMEM((nsp, own, model + LANES), F32), pltpu.VMEM(hb.shape, F32), pltpu.VMEM((2,) + hb.shape[1:], F32), pltpu.VMEM((nsp, own, 2 * model + hd), F32), pltpu.VMEM(hb.shape, F32),
+        scratch_shapes=wide + [pltpu.VMEM(pk3.shape, F32), part, part, part, pltpu.VMEM((nsp, own, hd + LANES), F32), pltpu.VMEM(hb.shape, F32), pltpu.VMEM((2,) + hb.shape[1:], F32), pltpu.VMEM((nsp, own, 3 * model + hd), F32), pltpu.VMEM(hb.shape, F32), pltpu.VMEM((nsp, ntp - 1, 1, own, model), F32),
                                pltpu.VMEM((2,) + x3.shape[1:], BF16), pltpu.VMEM((LANES, model), F32), pltpu.VMEM((rows, model), F32), pltpu.VMEM((nsp,) + qk.shape, F32), pltpu.VMEM((ntp, 1, model), F32), pltpu.VMEM((images, model), F32),
-                               dma((7,)), dma((2,)), dma((nsp - 1,)), dma((nsp,)), tps, tpr, tps, tpr, tps, tpr] + ring + [dma((9,)), dma((nsp,)), dma((2,)), dma((3, half)), dma((ntp, half)), dma((3, half)), dma((ntp, half))] + ring + ring + [tps, tpr, tps, tpr, dma((nsp - 1,)), dma((nsp,)), tps, tpr],
+                               dma((7,)), dma((2,)), dma((nsp - 1,)), dma((nsp,)), tps, tpr, tps, tpr, tps, tpr, dma((nsp - 1,)), dma((nsp,))] + [dma((9,)), dma((nsp,)), dma((2,)), dma((3, half)), dma((ntp, half)), dma((3, half)), dma((ntp, half))] + ring + ring + [tps, tpr, tps, tpr, dma((nsp - 1,)), dma((nsp,)), tps, tpr, tps, tpr] + ring,
         compiler_params=pltpu.CompilerParams(collective_id=0, has_side_effects=True),
         name='middle',
     )(pk3, og3, qk, *vectors, hb, x3, wo, wu, wd, wv, wk, wq)
@@ -545,7 +554,7 @@
     )(y, gpre, hid, og, pb, ga, gp3, hbar, q8, u, gq, probe, pool, gpr)
 
 
-def back_kernel(heads, ntp, scale, x_ref, gain_ref, bias_ref, gv_ref, qk_ref, st_ref, gx_ref, qkr):
+def back_kernel(heads, ntp, scale, x_ref, h_ref, ms_ref, gain_ref, gv_ref, qk_ref, st_ref, gx_ref, qkr):
     step = pl.program_id(0)
     rows = heads * SUB
     model = x_ref.shape[1]
@@ -560,9 +569,10 @@
                 qkr[LANES + at:LANES + at + SUB, :] = lo.astype(F32)
 
     images, tokens = SUB, x_ref.shape[0] // SUB
-    hat, inv = centre(x_ref[...].astype(F32))
+    inv = ms_ref[:, 1:2]
+    hat = (x_ref[...].astype(F32) - ms_ref[:, 0:1]) * inv
     gain = row(gain_ref)
-    hid = (hat * gain + row(bias_ref)).astype(BF16)
+    hid = h_ref[...]
     qkb = qkr[...].astype(BF16)
     gv_hi, gv_lo = hi_lo(gv_ref[...].reshape(ntp * rows, model))
     r = nt(hid, qkb)
@@ -581,7 +591,7 @@
     gx_ref[...] = norm_back(hat, inv, gh * gain).astype(BF16)
 
 
-def back_tokens(heads, ntp, scale, x, gain, bias, gv, qk, st):
+def back_tokens(heads, ntp, scale, x, h, ms, gain, gv, qk, st):
     tokens_all, model = x.shape
     groups, rows = gv.shape[1], gv.shape[2]
     block = tokens_all // groups
@@ -589,12 +599,12 @@
     return pl.pallas_call(
         functools.partial(back_kernel, heads, ntp, scale),
         grid=(groups,),
-        in_specs=[pl.BlockSpec((block, model), lambda g: (g, 0)), full(gain), full(bias), pl.BlockSpec((ntp, 1, rows, model), lambda g: (0, g, 0, 0)), full(qk), pl.BlockSpec((ntp, 1) + st.shape[2:], lambda g: (0, g, 0, 0))],
+        in_specs=[pl.BlockSpec((block, model), lambda g: (g, 0)), pl.BlockSpec((block, model), lambda g: (g, 0)), pl.BlockSpec((block, LANES), lambda g: (g, 0)), full(gain), pl.BlockSpec((ntp, 1, rows, model), lambda g: (0, g, 0, 0)), full(qk), pl.BlockSpec((ntp, 1) + st.shape[2:], lambda g: (0, g, 0, 0))],
         out_specs=pl.BlockSpec((block, model), lambda g: (g, 0)),
         out_shape=jax.ShapeDtypeStruct((tokens_all, model), BF16),
         scratch_shapes=[pltpu.VMEM((2 * LANES, model), F32)],
         name='back_tokens',
-    )(x, gain, bias, gv, qk, st)
+    )(x, h, ms, gain, gv, qk, st)
 
 
 def local_head(nsp, ntp, encoded, enc_gain, enc_bias, probe, w_query, b_query, w_key, w_value, b_value, w_out, b_out, head_gain, head_bias, w_up, b_up, w_down, b_down, out_grad):
@@ -606,9 +616,9 @@
     wq, wk, wv = (jnp.transpose(w, (1, 2, 0)).reshape(hd, model) for w in (w_query, w_key, w_value))
     wo = w_out.reshape(hd, model)
     og3 = out_grad.reshape(nsp, images // nsp, model)
-    pk, hb, qk, q8 = scan_tokens(heads, images, scale, x, enc_gain, enc_bias, probe, wq, b_query, wk, wv, b_value)
-    gv, hbar, st, qk_all, gp3, y3, ga3, pool3, pb3, hidden, grad_pre, u, gq, gpr = middle(heads, nsp, ntp, scale, pk, og3, qk, (b_out, head_gain, head_bias, b_up, b_down, b_value, enc_gain, enc_bias), hb, x.reshape(nsp, -1, model), wo, w_up, w_down, wv, wk, wq)
-    gx = back_tokens(heads, ntp, scale, x, enc_gain, enc_bias, gv, qk_all, st)
+    pk, hb, qk, q8, h, ms = scan_tokens(heads, images, scale, x, enc_gain, enc_bias, probe, wq, b_query, wk, wv, b_value)
+    gv, hbar, st, qk_all, gp3, y3, ga3, pool3, pb3, hidden, grad_pre, u, gq, gpr = middle(heads, nsp, ntp, scale, pk, og3, qk, (b_out, head_gain, head_bias, b_up, b_down, b_value), hb, h.reshape(nsp, -1, model), wo, w_up, w_down, wv, wk, wq)
+    gx = back_tokens(heads, ntp, scale, x, h, ms, enc_gain, gv, qk_all, st)
     y, ga, pool, pooled_bf = (a.reshape(images, -1) for a in (y3, ga3, pool3, pb3))
     grad_w_up, grad_w_down, *small, pooled, grad_probe = products(heads, y, grad_pre, hidden, out_grad, pooled_bf, ga, gp3, hbar, q8, u, gq, probe, pool, gpr)
     grad_w_out, grad_wv, grad_wk, grad_wq = (a.reshape(heads, head_dim, model) for a in small)

time: 127 us -> 112 us (0.88)
  Pallas kernels: 126 us -> 110 us
    pallas_call x1, Pallas kernels: 81.8 us -> 65.3 us  [middle(): pl.pallas_call(functools.partial(middle_kernel, heads, nsp, ntp, scale),...]
where the time goes in v4:
time: 112 us; the launch traced here: 111 us
  Pallas kernels  110 us (98%)
    pallas_call x1, Pallas kernels, middle(): pl.pallas_call(functools.partial(middle_kernel, heads, nsp, ntp, scale),...  65.3 us
    pallas_call x1, Pallas kernels, scan_tokens(): pl.pallas_call(functools.partial(scan_kernel, heads, scale), grid=(groups...  16.7 us
    pallas_call x1, Pallas kernels, back_tokens(): pl.pallas_call(functools.partial(back_kernel, heads, ntp, scale), grid=(g...  15.6 us
    pallas_call x1, Pallas kernels, products(): pl.pallas_call(functools.partial(products_kernel, heads, parts), grid=(st...  12.7 us

profile of v4, /device:TPU:97, one launch (start us, length us, event | category | flops | bytes accessed | tf_op | source)
XLA Modules:
  0.0 111.1 jit_solution(2426174502763481727)
XLA Ops:
  0.6 16.7 %scan_tokens.1 = (f32[64,640]{1,0:T(8,128)}, f32[8,32,1536]{2,1,0:T(8,128)}, f32[4,1536]{1,0:T(4,128)}, f32[8,384]{1,0:T(8,128)}, bf16[2048,1536]{1,0:T(8,128)(2,1)}, /*index=5*/f32[2048,128]{1,0:T(8,128)}) custom-call(bf16[2048,1536]{1,0:T(8,128)(2,1)} %bitcast.29, f32[1536]{0:T(1024)} %gain_ref.3, f32[1536]{0:T(1024)} %bias_ref.1, f32[1536]{0:T(1024)} %probe_ref.3, ...), custom_call_target="tpu_custom_call" | custom-call | tf_op jit(solution)/shard_map/scan_tokens/pallas_call | solution.py:201
  17.3 65.3 %middle.1 = (f32[4,8,32,1536]{3,2,1,0:T(8,128)}, bf16[8,32,1536]{2,1,0:T(8,128)(2,1)}, f32[4,8,8,128]{3,2,1,0:T(8,128)}, f32[4,4,1536]{2,1,0:T(4,128)}, bf16[8,8...) custom-call(f32[8,8,640]{2,1,0:T(8,128)} %bitcast.44, ...), custom_call_target="tpu_custom_call" | custom-call | tf_op jit(solution)/shard_map/middle/pallas_call | solution.py:487
  82.7 15.6 %back_tokens.1 = bf16[2048,1536]{1,0:T(8,128)(2,1)} custom-call(bf16[2048,1536]{1,0:T(8,128)(2,1)} %bitcast.30, bf16[2048,1536]{1,0:T(8,128)(2,1)} %get-tuple-element.40.h_ref, f32[2048,128]{1,0:T(8,128)} %get-tuple-element.54.ms_ref, f32[1536]{0:T(1024)} %gain_ref.3, f32[4,8,32,1536]{3,2,1,0:T(8,128)} %get-tuple-element.55.gv_ref, ...), custom_call_target="tpu_custom_call" | custom-call | tf_op jit(solution)/shard_map/back_tokens/pallas_call | solution.py:599
  98.2 12.7 %products.1 = (f32[1536,1536]{1,0:T(8,128)}, f32[1536,1536]{1,0:T(8,128)}, f32[384,1536]{1,0:T(8,128)}, f32[384,1536]{1,0:T(8,128)}, f32[384,1536]{1,0:T(8,128)}...) custom-call(bf16[64,1536]{1,0:T(8,128)(2,1)} %bitcast.41, ...), custom_call_target="tpu_custom_call" | custom-call | tf_op jit(solution)/shard_map/products/pallas_call | solution.py:547

commit v5 on v4

--- a/solution.py
+++ b/solution.py
@@ -13,6 +13,7 @@
 OUT_SPECS = (P('dp', None), P('dp', 'sp', None), P('dp'), P('dp', 'tp', None), P('dp', 'tp', None), P('dp', 'tp', None), P(('dp', 'tp'), None, None), P('dp', 'tp'), P(('dp', 'tp'), None))
 LANES = 128
 SUB = 8
+PER = 2
 GELU_C = 0.7978845608028654
 GELU_A = 0.044715
 
@@ -158,26 +159,28 @@
             qk_ref[h:h + 1, :] = qk[SUB * h:SUB * h + 1, :]
 
     step = pl.program_id(0)
-    images, tokens = SUB, x_ref.shape[0] // SUB
-    hat, inv, mean = centre(x_ref[...].astype(F32))
-    hid = (hat * row(gain_ref) + row(bias_ref)).astype(BF16)
-    h_ref[...] = hid
-    which = iota((x_ref.shape[0], LANES), 1)
-    ms_ref[...] = jnp.where(which == 0, mean, inv)
-    r = nt(hid, qkr[...])
-    s = ((r + pltpu.roll(r, LANES // 2, 1)) * scale).reshape(images, tokens, LANES)
-    m = jnp.max(s, axis=1)
-    e = jnp.exp(s - m[:, None, :])
-    l = jnp.sum(e, axis=1)
-    lane, img = iota(e.shape, 2), iota(e.shape, 0)
-    ebd = jnp.where((lane % SUB == img) & (lane < rows), e, 0.0).astype(BF16).reshape(images * tokens, LANES)
-    hb = tn(ebd, hid)[0:rows, :]
-    hb_ref[0, :, :] = hb
-    hball[step] = hb
+    block = x_ref.shape[0] // PER
+    images, tokens = SUB, block // SUB
     cols = wq_ref.shape[0]
-    mine = pl.ds(pl.multiple_of(step * SUB, SUB), SUB)
-    pk_ref[mine, cols:cols + LANES] = m
-    pk_ref[mine, cols + LANES:cols + 2 * LANES] = l
+    for j in range(PER):
+        at = slice(j * block, j * block + block)
+        hat, inv, mean = centre(x_ref[at, :].astype(F32))
+        hid = (hat * row(gain_ref) + row(bias_ref)).astype(BF16)
+        h_ref[at, :] = hid
+        ms_ref[at, :] = jnp.where(iota((block, LANES), 1) == 0, mean, inv)
+        r = nt(hid, qkr[...])
+        s = ((r + pltpu.roll(r, LANES // 2, 1)) * scale).reshape(images, tokens, LANES)
+        m = jnp.max(s, axis=1)
+        e = jnp.exp(s - m[:, None, :])
+        l = jnp.sum(e, axis=1)
+        lane, img = iota(e.shape, 2), iota(e.shape, 0)
+        ebd = jnp.where((lane % SUB == img) & (lane < rows), e, 0.0).astype(BF16).reshape(images * tokens, LANES)
+        hb = tn(ebd, hid)[0:rows, :]
+        hb_ref[j, :, :] = hb
+        hball[step * PER + j] = hb
+        mine = pl.ds(pl.multiple_of((step * PER + j) * SUB, SUB), SUB)
+        pk_ref[mine, cols:cols + LANES] = m
+        pk_ref[mine, cols + LANES:cols + 2 * LANES] = l
 
     @pl.when(step == pl.num_programs(0) - 1)
     def _():
@@ -196,13 +199,13 @@
     tokens_all, width = x.shape
     hd = wq.shape[0]
     groups = images // SUB
-    block = tokens_all // groups
+    block = tokens_all // groups * PER
     full = lambda a: pl.BlockSpec(a.shape, lambda g: (0,) * a.ndim)
     return pl.pallas_call(
         functools.partial(scan_kernel, heads, scale),
-        grid=(groups,),
+        grid=(groups // PER,),
         in_specs=[pl.BlockSpec((block, width), lambda g: (g, 0))] + [full(a) for a in (gain, bias, probe, wq, bq, wk, wv, bv)],
-        out_specs=[pl.BlockSpec((images, hd + 2 * LANES), lambda g: (0, 0)), pl.BlockSpec((1, heads * SUB, width), lambda g: (g, 0, 0)), pl.BlockSpec((heads, width), lambda g: (0, 0)), pl.BlockSpec((SUB, hd), lambda g: (0, 0)), pl.BlockSpec((block, width), lambda g: (g, 0)), pl.BlockSpec((block, LANES), lambda g: (g, 0))],
+        out_specs=[pl.BlockSpec((images, hd + 2 * LANES), lambda g: (0, 0)), pl.BlockSpec((PER, heads * SUB, width), lambda g: (g, 0, 0)), pl.BlockSpec((heads, width), lambda g: (0, 0)), pl.BlockSpec((SUB, hd), lambda g: (0, 0)), pl.BlockSpec((block, width), lambda g: (g, 0)), pl.BlockSpec((block, LANES), lambda g: (g, 0))],
         out_shape=[jax.ShapeDtypeStruct((images, hd + 2 * LANES), F32), jax.ShapeDtypeStruct((groups, heads * SUB, width), F32), jax.ShapeDtypeStruct((heads, width), F32), jax.ShapeDtypeStruct((SUB, hd), F32), jax.ShapeDtypeStruct(x.shape, BF16), jax.ShapeDtypeStruct((tokens_all, LANES), F32)],
         scratch_shapes=[pltpu.VMEM((LANES, width), BF16), pltpu.VMEM((groups, heads * SUB, width), F32)],
         name='scan_tokens',
@@ -488,12 +491,12 @@
         functools.partial(middle_kernel, heads, nsp, ntp, scale),
         in_specs=[vm] * 9 + [hbm] * 8,
         out_specs=[vm] * 14,
-        out_shape=[sds((ntp, nsp, rows, model), F32), sds((nsp, rows, model), BF16), sds((ntp, nsp, own, LANES), F32), sds((ntp,) + qk.shape, F32), sds((nsp, own, hd), BF16),
+        out_shape=[pltpu.VMEM((ntp, nsp, rows, model), F32), sds((nsp, rows, model), BF16), sds((ntp, nsp, own, LANES), F32), sds((ntp,) + qk.shape, F32), sds((nsp, own, hd), BF16),
                    sds((nsp, own, model), BF16), sds((nsp, own, model), BF16), sds((nsp, own, model), BF16), sds((nsp, own, hd), BF16), sds((images, model), BF16), sds((images, model), BF16), sds(qk.shape, F32), sds((1, hd), F32), sds((1, model), F32)],
         scratch_shapes=wide + [pltpu.VMEM(pk3.shape, F32), part, part, part, pltpu.VMEM((nsp, own, hd + LANES), F32), pltpu.VMEM(hb.shape, F32), pltpu.VMEM((2,) + hb.shape[1:], F32), pltpu.VMEM((nsp, own, 3 * model + hd), F32), pltpu.VMEM(hb.shape, F32), pltpu.VMEM((nsp, ntp - 1, 1, own, model), F32),
                                pltpu.VMEM((2,) + x3.shape[1:], BF16), pltpu.VMEM((LANES, model), F32), pltpu.VMEM((rows, model), F32), pltpu.VMEM((nsp,) + qk.shape, F32), pltpu.VMEM((ntp, 1, model), F32), pltpu.VMEM((images, model), F32),
                                dma((7,)), dma((2,)), dma((nsp - 1,)), dma((nsp,)), tps, tpr, tps, tpr, tps, tpr, dma((nsp - 1,)), dma((nsp,))] + [dma((9,)), dma((nsp,)), dma((2,)), dma((3, half)), dma((ntp, half)), dma((3, half)), dma((ntp, half))] + ring + ring + [tps, tpr, tps, tpr, dma((nsp - 1,)), dma((nsp,)), tps, tpr, tps, tpr] + ring,
-        compiler_params=pltpu.CompilerParams(collective_id=0, has_side_effects=True),
+        compiler_params=pltpu.CompilerParams(collective_id=0, has_side_effects=True, vmem_limit_bytes=57 << 20),
         name='middle',
     )(pk3, og3, qk, *vectors, hb, x3, wo, wu, wd, wv, wk, wq)
 
@@ -568,41 +571,45 @@
                 qkr[at:at + SUB, :] = hi.astype(F32)
                 qkr[LANES + at:LANES + at + SUB, :] = lo.astype(F32)
 
-    images, tokens = SUB, x_ref.shape[0] // SUB
-    inv = ms_ref[:, 1:2]
-    hat = (x_ref[...].astype(F32) - ms_ref[:, 0:1]) * inv
+    block = x_ref.shape[0] // PER
+    images, tokens = SUB, block // SUB
     gain = row(gain_ref)
-    hid = h_ref[...]
     qkb = qkr[...].astype(BF16)
-    gv_hi, gv_lo = hi_lo(gv_ref[...].reshape(ntp * rows, model))
-    r = nt(hid, qkb)
-    s = (r[:, 0:LANES] + r[:, LANES:2 * LANES]) * scale
-    d = nt(hid, jnp.concatenate([gv_hi, gv_lo], axis=0))
-    d = d[:, 0:LANES] + d[:, LANES:2 * LANES]
-    lse = jnp.concatenate([st_ref[t, 0, :, 0:rows] for t in range(ntp)], axis=1)
-    delta = jnp.concatenate([st_ref[t, 0, :, rows:2 * rows] for t in range(ntp)], axis=1)
-    shape = (images, tokens, LANES)
-    keep = iota(shape, 2) % SUB == iota(shape, 0)
-    p = jnp.where(keep, jnp.exp(s.reshape(shape) - lse[:, None, :]), 0.0)
-    ds = p * (d.reshape(shape) - delta[:, None, :]) * scale
-    pb = p.astype(BF16).reshape(images * tokens, LANES)
-    db = ds.astype(BF16).reshape(images * tokens, LANES)
-    gh = nn(jnp.concatenate([pb, db], axis=1), jnp.concatenate([gv_hi, qkb[0:LANES]], axis=0))
-    gx_ref[...] = norm_back(hat, inv, gh * gain).astype(BF16)
+    for j in range(PER):
+        at = slice(j * block, j * block + block)
+        hid = h_ref[at, :]
+        gv_hi, gv_lo = hi_lo(jnp.concatenate([gv_ref[t, step * PER + j] for t in range(ntp)], axis=0))
+        r = nt(hid, qkb)
+        s = (r[:, 0:LANES] + r[:, LANES:2 * LANES]) * scale
+        d = nt(hid, jnp.concatenate([gv_hi, gv_lo], axis=0))
+        d = d[:, 0:LANES] + d[:, LANES:2 * LANES]
+        lse = jnp.concatenate([st_ref[t, j, :, 0:rows] for t in range(ntp)], axis=1)
+        delta = jnp.concatenate([st_ref[t, j, :, rows:2 * rows] for t in range(ntp)], axis=1)
+        shape = (images, tokens, LANES)
+        keep = iota(shape, 2) % SUB == iota(shape, 0)
+        p = jnp.where(keep, jnp.exp(s.reshape(shape) - lse[:, None, :]), 0.0)
+        ds = p * (d.reshape(shape) - delta[:, None, :]) * scale
+        pb = p.astype(BF16).reshape(images * tokens, LANES)
+        db = ds.astype(BF16).reshape(images * tokens, LANES)
+        gh = nn(jnp.concatenate([pb, db], axis=1), jnp.concatenate([gv_hi, qkb[0:LANES]], axis=0))
+        inv = ms_ref[at, 1:2]
+        hat = (x_ref[at, :].astype(F32) - ms_ref[at, 0:1]) * inv
+        gx_ref[at, :] = norm_back(hat, inv, gh * gain).astype(BF16)
 
 
 def back_tokens(heads, ntp, scale, x, h, ms, gain, gv, qk, st):
     tokens_all, model = x.shape
     groups, rows = gv.shape[1], gv.shape[2]
-    block = tokens_all // groups
+    block = tokens_all // groups * PER
     full = lambda a: pl.BlockSpec(a.shape, lambda g: (0,) * a.ndim)
     return pl.pallas_call(
         functools.partial(back_kernel, heads, ntp, scale),
-        grid=(groups,),
-        in_specs=[pl.BlockSpec((block, model), lambda g: (g, 0)), pl.BlockSpec((block, model), lambda g: (g, 0)), pl.BlockSpec((block, LANES), lambda g: (g, 0)), full(gain), pl.BlockSpec((ntp, 1, rows, model), lambda g: (0, g, 0, 0)), full(qk), pl.BlockSpec((ntp, 1) + st.shape[2:], lambda g: (0, g, 0, 0))],
+        grid=(groups // PER,),
+        in_specs=[pl.BlockSpec((block, model), lambda g: (g, 0)), pl.BlockSpec((block, model), lambda g: (g, 0)), pl.BlockSpec((block, LANES), lambda g: (g, 0)), full(gain), pl.BlockSpec(memory_space=pltpu.VMEM), full(qk), pl.BlockSpec((ntp, PER) + st.shape[2:], lambda g: (0, g, 0, 0))],
         out_specs=pl.BlockSpec((block, model), lambda g: (g, 0)),
         out_shape=jax.ShapeDtypeStruct((tokens_all, model), BF16),
         scratch_shapes=[pltpu.VMEM((2 * LANES, model), F32)],
+        compiler_params=pltpu.CompilerParams(vmem_limit_bytes=57 << 20),
         name='back_tokens',
     )(x, h, ms, gain, gv, qk, st)
 
@@ -618,6 +625,7 @@
     og3 = out_grad.reshape(nsp, images // nsp, model)
     pk, hb, qk, q8, h, ms = scan_tokens(heads, images, scale, x, enc_gain, enc_bias, probe, wq, b_query, wk, wv, b_value)
     gv, hbar, st, qk_all, gp3, y3, ga3, pool3, pb3, hidden, grad_pre, u, gq, gpr = middle(heads, nsp, ntp, scale, pk, og3, qk, (b_out, head_gain, head_bias, b_up, b_down, b_value), hb, h.reshape(nsp, -1, model), wo, w_up, w_down, wv, wk, wq)
+    gv = pltpu.with_memory_space_constraint(gv, pltpu.VMEM)
     gx = back_tokens(heads, ntp, scale, x, h, ms, enc_gain, gv, qk_all, st)
     y, ga, pool, pooled_bf = (a.reshape(images, -1) for a in (y3, ga3, pool3, pb3))
     grad_w_up, grad_w_down, *small, pooled, grad_probe = products(heads, y, grad_pre, hidden, out_grad, pooled_bf, ga, gp3, hbar, q8, u, gq, probe, pool, gpr)

time: 112 us -> 106 us (0.946)
  Pallas kernels: 110 us -> 105 us
    pallas_call x1, Pallas kernels: 15.6 us -> 13.1 us  [back_tokens(): pl.pallas_call(functools.partial(back_kernel, heads, ntp, scale), grid=(g...]
    pallas_call x1, Pallas kernels: 65.3 us -> 63.4 us  [middle(): pl.pallas_call(functools.partial(middle_kernel, heads, nsp, ntp, scale),...]
where the time goes in v5:
time: 106 us
  Pallas kernels  105 us (99%)
    pallas_call x1, Pallas kernels, middle(): pl.pallas_call(functools.partial(middle_kernel, heads, nsp, ntp, scale),...  63.4 us
    pallas_call x1, Pallas kernels, scan_tokens(): pl.pallas_call(functools.partial(scan_kernel, heads, scale), grid=(groups...  15.7 us
    pallas_call x1, Pallas kernels, back_tokens(): pl.pallas_call(functools.partial(back_kernel, heads, ntp, scale), grid=(g...  13.1 us
    pallas_call x1, Pallas kernels, products(): pl.pallas_call(functools.partial(products_kernel, heads, parts), grid=(st...  12.7 us

profile of v5, /device:TPU:97, one launch (start us, length us, event | category | flops | bytes accessed | tf_op | source)
XLA Modules:
  0.0 105.7 jit_solution(15593347124488798274)
XLA Ops:
  0.6 15.7 %scan_tokens.1 = (f32[64,640]{1,0:T(8,128)}, f32[8,32,1536]{2,1,0:T(8,128)}, f32[4,1536]{1,0:T(4,128)}, f32[8,384]{1,0:T(8,128)}, bf16[2048,1536]{1,0:T(8,128)(2,1)}, /*index=5*/f32[2048,128]{1,0:T(8,128)}) custom-call(bf16[2048,1536]{1,0:T(8,128)(2,1)} %bitcast.29, f32[1536]{0:T(1024)} %gain_ref.3, f32[1536]{0:T(1024)} %bias_ref.1, f32[1536]{0:T(1024)} %probe_ref.3, ...), custom_call_target="tpu_custom_call" | custom-call | tf_op jit(solution)/shard_map/scan_tokens/pallas_call | solution.py:204
  16.3 63.4 %middle.1 = (f32[4,8,32,1536]{3,2,1,0:T(8,128)S(1)}, bf16[8,32,1536]{2,1,0:T(8,128)(2,1)}, f32[4,8,8,128]{3,2,1,0:T(8,128)}, f32[4,4,1536]{2,1,0:T(4,128)}, bf16...) custom-call(f32[8,8,640]{2,1,0:T(8,128)} %bitcast.44, ...), custom_call_target="tpu_custom_call" | custom-call | tf_op jit(solution)/shard_map/middle/pallas_call | solution.py:490
  79.7 13.1 %back_tokens.1 = bf16[2048,1536]{1,0:T(8,128)(2,1)} custom-call(bf16[2048,1536]{1,0:T(8,128)(2,1)} %bitcast.30, bf16[2048,1536]{1,0:T(8,128)(2,1)} %get-tuple-element.40.h_ref, f32[2048,128]{1,0:T(8,128)} %get-tuple-element.54.ms_ref, f32[1536]{0:T(1024)} %gain_ref.3, f32[4,8,32,1536]{3,2,1,0:T(8,128)S(1)} %get-tuple-element.55.gv_ref, ...), custom_call_target="tpu_custom_call" | custom-call | tf_op jit(solution)/shard_map/back_tokens/pallas_call | solution.py:605
  92.8 12.7 %products.1 = (f32[1536,1536]{1,0:T(8,128)}, f32[1536,1536]{1,0:T(8,128)}, f32[384,1536]{1,0:T(8,128)}, f32[384,1536]{1,0:T(8,128)}, f32[384,1536]{1,0:T(8,128)}...) custom-call(bf16[64,1536]{1,0:T(8,128)(2,1)} %bitcast.41, ...), custom_call_target="tpu_custom_call" | custom-call | tf_op jit(solution)/shard_map/products/pallas_call | solution.py:550

commit v6 on v5

--- a/solution.py
+++ b/solution.py
@@ -139,12 +139,15 @@
 RING_SEMS = 7
 
 
-def scan_kernel(heads, scale, x_ref, gain_ref, bias_ref, probe_ref, wq_ref, bq_ref, wk_ref, wv_ref, bv_ref, pk_ref, hb_ref, qk_ref, q_ref, h_ref, ms_ref, qkr, hball):
+def scan_kernel(heads, scale, x_ref, gain_ref, bias_ref, probe_ref, wq_ref, bq_ref, wk_ref, wv_hbm, bv_ref, pk_ref, hb_ref, qk_ref, q_ref, h_ref, ms_ref, qkr, hball, wv_ref, wv_sem):
     rows = heads * SUB
     width = wq_ref.shape[0] // heads
 
+    load = pltpu.make_async_copy(wv_hbm, wv_ref, wv_sem)
+
     @pl.when(pl.program_id(0) == 0)
     def _():
+        load.start()
         probe8 = jnp.broadcast_to(row(probe_ref), (SUB, probe_ref.shape[0])).astype(BF16)
         q8 = (nt(probe8, wq_ref[...]) + flat(bq_ref)).astype(BF16)
         q_ref[...] = q8.astype(F32)
@@ -186,6 +189,7 @@
     def _():
         groups = hball.shape[0]
         every = groups * rows
+        load.wait()
         hi, lo = hi_lo(hball[...].reshape(every, hball.shape[2]))
         v = nt(hi, wv_ref[...]) + nt(lo, wv_ref[...])
         bias = flat(bv_ref)
@@ -204,10 +208,10 @@
     return pl.pallas_call(
         functools.partial(scan_kernel, heads, scale),
         grid=(groups // PER,),
-        in_specs=[pl.BlockSpec((block, width), lambda g: (g, 0))] + [full(a) for a in (gain, bias, probe, wq, bq, wk, wv, bv)],
+        in_specs=[pl.BlockSpec((block, width), lambda g: (g, 0))] + [full(a) for a in (gain, bias, probe, wq, bq, wk)] + [pl.BlockSpec(memory_space=pl.ANY), full(bv)],
         out_specs=[pl.BlockSpec((images, hd + 2 * LANES), lambda g: (0, 0)), pl.BlockSpec((PER, heads * SUB, width), lambda g: (g, 0, 0)), pl.BlockSpec((heads, width), lambda g: (0, 0)), pl.BlockSpec((SUB, hd), lambda g: (0, 0)), pl.BlockSpec((block, width), lambda g: (g, 0)), pl.BlockSpec((block, LANES), lambda g: (g, 0))],
         out_shape=[jax.ShapeDtypeStruct((images, hd + 2 * LANES), F32), jax.ShapeDtypeStruct((groups, heads * SUB, width), F32), jax.ShapeDtypeStruct((heads, width), F32), jax.ShapeDtypeStruct((SUB, hd), F32), jax.ShapeDtypeStruct(x.shape, BF16), jax.ShapeDtypeStruct((tokens_all, LANES), F32)],
-        scratch_shapes=[pltpu.VMEM((LANES, width), BF16), pltpu.VMEM((groups, heads * SUB, width), F32)],
+        scratch_shapes=[pltpu.VMEM((LANES, width), BF16), pltpu.VMEM((groups, heads * SUB, width), F32), pltpu.VMEM(wv.shape, BF16), pltpu.SemaphoreType.DMA(())],
         name='scan_tokens',
     )(x, gain, bias, probe, wq, bq, wk, wv, bv)
 

time: 106 us -> 106 us (level)
  no operation moved by 1% of the time
where the time goes in v6:
time: 106 us; the launch traced here: 105 us
  Pallas kernels  105 us (99%)
    pallas_call x1, Pallas kernels, middle(): pl.pallas_call(functools.partial(middle_kernel, heads, nsp, ntp, scale),...  63.5 us
    pallas_call x1, Pallas kernels, scan_tokens(): pl.pallas_call(functools.partial(scan_kernel, heads, scale), grid=(groups...  15.3 us
    pallas_call x1, Pallas kernels, back_tokens(): pl.pallas_call(functools.partial(back_kernel, heads, ntp, scale), grid=(g...  13.1 us
    pallas_call x1, Pallas kernels, products(): pl.pallas_call(functools.partial(products_kernel, heads, parts), grid=(st...  12.7 us

profile of v6, /device:TPU:97, one launch (start us, length us, event | category | flops | bytes accessed | tf_op | source)
XLA Modules:
  0.0 105.4 jit_solution(8466250051969775020)
XLA Ops:
  0.6 15.3 %scan_tokens.1 = (f32[64,640]{1,0:T(8,128)}, f32[8,32,1536]{2,1,0:T(8,128)}, f32[4,1536]{1,0:T(4,128)}, f32[8,384]{1,0:T(8,128)}, bf16[2048,1536]{1,0:T(8,128)(2,1)}, /*index=5*/f32[2048,128]{1,0:T(8,128)}) custom-call(bf16[2048,1536]{1,0:T(8,128)(2,1)} %bitcast.29, f32[1536]{0:T(1024)} %gain_ref.3, f32[1536]{0:T(1024)} %bias_ref.1, f32[1536]{0:T(1024)} %probe_ref.3, ...), custom_call_target="tpu_custom_call" | custom-call | tf_op jit(solution)/shard_map/scan_tokens/pallas_call | solution.py:208
  15.9 63.5 %middle.1 = (f32[4,8,32,1536]{3,2,1,0:T(8,128)S(1)}, bf16[8,32,1536]{2,1,0:T(8,128)(2,1)}, f32[4,8,8,128]{3,2,1,0:T(8,128)}, f32[4,4,1536]{2,1,0:T(4,128)}, bf16...) custom-call(f32[8,8,640]{2,1,0:T(8,128)} %bitcast.44, ...), custom_call_target="tpu_custom_call" | custom-call | tf_op jit(solution)/shard_map/middle/pallas_call | solution.py:494
  79.4 13.1 %back_tokens.1 = bf16[2048,1536]{1,0:T(8,128)(2,1)} custom-call(bf16[2048,1536]{1,0:T(8,128)(2,1)} %bitcast.30, bf16[2048,1536]{1,0:T(8,128)(2,1)} %get-tuple-element.40.h_ref, f32[2048,128]{1,0:T(8,128)} %get-tuple-element.54.ms_ref, f32[1536]{0:T(1024)} %gain_ref.3, f32[4,8,32,1536]{3,2,1,0:T(8,128)S(1)} %get-tuple-element.55.gv_ref, ...), custom_call_target="tpu_custom_call" | custom-call | tf_op jit(solution)/shard_map/back_tokens/pallas_call | solution.py:609
  92.5 12.7 %products.1 = (f32[1536,1536]{1,0:T(8,128)}, f32[1536,1536]{1,0:T(8,128)}, f32[384,1536]{1,0:T(8,128)}, f32[384,1536]{1,0:T(8,128)}, f32[384,1536]{1,0:T(8,128)}...) custom-call(bf16[64,1536]{1,0:T(8,128)(2,1)} %bitcast.41, ...), custom_call_target="tpu_custom_call" | custom-call | tf_op jit(solution)/shard_map/products/pallas_call | solution.py:554
